TPU v7x, 32 devices: a whole 2x2x4 slice. The times are simulated.
32 devices in a mesh: dp: 16 (over z, x, core), tensor: 2 (over y).
Axes of the slice: x: 2, y: 2, z: 4, core: 2. Of those that a mesh axis runs over, the one named last changes fastest.
Arguments:
- inputs: bfloat16 [4096, 2048], P(('dp', 'tensor')), may hold values from -6 to 6
- input_gain: bfloat16 [2048], P(('dp', 'tensor')), may hold values from 0.5 to 1.5
- post_gain: bfloat16 [2048], P(('dp', 'tensor')), may hold values from 0.5 to 1.5
- query_gain: bfloat16 [128], P(('dp', 'tensor')), may hold values from 0.25 to 1.75
- key_gain: bfloat16 [128], P(('dp', 'tensor')), may hold values from 0.25 to 1.75
- query_weight: bfloat16 [4096, 2048], P('tensor', 'dp'), may hold values from -0.125 to 0.125
- key_projection_matrix: bfloat16 [512, 2048], P('tensor', 'dp'), may hold values from -0.125 to 0.125
- value_projection_matrix: bfloat16 [512, 2048], P('tensor', 'dp'), may hold values from -0.125 to 0.125
- output_weight: bfloat16 [2048, 4096], P('dp', 'tensor'), may hold values from -0.375 to 0.375
- router_weight: bfloat16 [2048, 32], P(('dp', 'tensor')), may hold values from -0.125 to 0.125
- gate_weight: bfloat16 [32, 2048, 768], P('dp', None, 'tensor'), may hold values from -0.125 to 0.125
- up_weight: bfloat16 [32, 2048, 768], P('dp', None, 'tensor'), may hold values from -0.125 to 0.125
- down_weight: bfloat16 [32, 768, 2048], P('dp', 'tensor'), may hold values from -0.625 to 0.625
- routes: int32 [4096, 8], P(('dp', 'tensor')), may hold values from 0 to 31, all different within a row; in each aligned block of 128 rows (0 to 127, 128 to 255, ...) at most 64 rows name the same one
- cotangent: bfloat16 [4096, 2048], P(('dp', 'tensor')), may hold values from -6 to 6
Outputs:
- output: bfloat16 [4096, 2048], P(('dp', 'tensor'))
- grad_inputs: bfloat16 [4096, 2048], P(('dp', 'tensor'))
- grad_input_gain: float32 [2048], P(('dp', 'tensor'))
- grad_post_gain: float32 [2048], P(('dp', 'tensor'))
- grad_query_gain: float32 [128], P(('dp', 'tensor'))
- grad_key_gain: float32 [128], P(('dp', 'tensor'))
- grad_query_weight: float32 [4096, 2048], P('tensor', 'dp')
- grad_key_weight: float32 [512, 2048], P('tensor', 'dp')
- grad_value_weight: float32 [512, 2048], P('tensor', 'dp')
- grad_output_weight: float32 [2048, 4096], P('dp', 'tensor')
- grad_router_weight: float32 [2048, 32], P(('dp', 'tensor'))
- grad_gate_weight: float32 [32, 2048, 768], P('dp', None, 'tensor')
- grad_up_weight: float32 [32, 2048, 768], P('dp', None, 'tensor')
- grad_down_weight: float32 [32, 768, 2048], P('dp', 'tensor')
Inputs may be any that keep to these rules, and one draw needn't show every extreme that they name: `routes`: each row names 8 different experts. In each aligned block of 128 rows (the rows of one device) no expert is named by more than 64 rows, a bound that some block reaches.
All inputs are finite; a program needn't handle non-finite values.
Results may differ from a plain program's by a relative error of at most 0.025.
Values may be sent and summed in bfloat16 or wider, within the bound.
No kernel may reach another device: no remote copies, remote signals or barrier semaphores. Data moves between devices by JAX's collectives and lax.ppermute only.
A program may use at most 384 MiB of HBM per device.

v0:
```python
import math

import jax
import jax.numpy as jnp
from jax import lax
from jax.sharding import PartitionSpec as P

MODEL_WIDTH = 2048
HEAD_SIZE = 128


EPSILON = 1e-06
ROPE_BASE = 1000000.0


def norm_rows(values, weights):
    inverse = lax.rsqrt(jnp.mean(values * values, axis=-1, keepdims=True) + EPSILON)
    normalized_rows = values * inverse
    return (normalized_rows * weights, normalized_rows, inverse)


def norm_back(upstream, weights, normalized_rows, inverse):
    scaled = upstream * weights
    inner_term = jnp.mean(scaled * normalized_rows, axis=-1, keepdims=True)
    return (inverse * (scaled - normalized_rows * inner_term), upstream * normalized_rows)


def rope_tables(length, head_width):
    half_width = head_width // 2
    frequency = jnp.exp(
        jnp.arange(half_width, dtype=jnp.float32) * (-2.0 * math.log(ROPE_BASE) / head_width)
    )
    angles = jnp.arange(length, dtype=jnp.float32)[:, None] * frequency[None, :]
    angles = jnp.concatenate([angles, angles], axis=-1)
    return (jnp.cos(angles), jnp.sin(angles))


def rotate_half(values):
    half_width = values.shape[-1] // 2
    return jnp.concatenate([-values[..., half_width:], values[..., :half_width]], axis=-1)


def rotate_back(values):
    half_width = values.shape[-1] // 2
    return jnp.concatenate([values[..., half_width:], -values[..., :half_width]], axis=-1)


def gather_tokens(rows):
    return lax.all_gather(rows, "tensor", axis=0, tiled=True)


def sum_tokens(terms):
    return lax.psum_scatter(
        terms.astype(jnp.bfloat16), "tensor", scatter_dimension=0, tiled=True
    ).astype(jnp.float32)


def move_rows(rows):
    return lax.all_to_all(rows, "dp", split_axis=0, concat_axis=0, tiled=True)


def to_slots(rows):
    routed = move_rows(rows)
    return lax.all_gather(routed[None], "tensor", axis=0, tiled=True)


def from_slots(terms, group_count, width):
    summed = lax.psum_scatter(
        terms.astype(jnp.bfloat16), "tensor", scatter_dimension=0, tiled=True
    ).astype(jnp.float32)[0]
    low_rows = summed.reshape(group_count, -1, width).astype(jnp.bfloat16)
    return move_rows(low_rows)


def on_device(
    inputs,
    input_gain,
    post_gain,
    query_gain,
    key_gain,
    query_weight,
    key_projection_matrix,
    value_projection_matrix,
    output_weight,
    router_weight,
    gate_weight,
    up_weight,
    down_weight,
    routes,
    cotangent,
):
    small_params = (
        lax.all_gather(router_weight, ("dp", "tensor"), axis=0, tiled=True),
        lax.all_gather(input_gain, ("dp", "tensor"), axis=0, tiled=True),
        lax.all_gather(post_gain, ("dp", "tensor"), axis=0, tiled=True),
        lax.all_gather(query_gain, ("dp", "tensor"), axis=0, tiled=True),
        lax.all_gather(key_gain, ("dp", "tensor"), axis=0, tiled=True),
    )
    router_full = small_params[0]
    input_scale = small_params[1].astype(jnp.float32)
    post_scale = small_params[2].astype(jnp.float32)
    query_scale = small_params[3].astype(jnp.float32)
    key_scale = small_params[4].astype(jnp.float32)
    residual_in = inputs.astype(jnp.float32)
    normed_in, input_hat, input_inv = norm_rows(residual_in, input_scale)
    sequence = gather_tokens(normed_in.astype(jnp.bfloat16))
    query_full, key_full, value_full, output_full = (
        lax.all_gather(query_weight, "dp", axis=1, tiled=True),
        lax.all_gather(key_projection_matrix, "dp", axis=1, tiled=True),
        lax.all_gather(value_projection_matrix, "dp", axis=1, tiled=True),
        lax.all_gather(output_weight, "dp", axis=0, tiled=True),
    )
    seq_len = sequence.shape[0]
    local_heads = query_full.shape[0] // HEAD_SIZE
    local_groups = key_full.shape[0] // HEAD_SIZE
    per_group = local_heads // local_groups
    query_raw = jnp.einsum(
        "sd,hd->sh", sequence, query_full, preferred_element_type=jnp.float32
    ).reshape(seq_len, local_heads, HEAD_SIZE)
    key_unrotated = jnp.einsum(
        "sd,hd->sh", sequence, key_full, preferred_element_type=jnp.float32
    ).reshape(seq_len, local_groups, HEAD_SIZE)
    value_reduced = (
        jnp.einsum("sd,hd->sh", sequence, value_full, preferred_element_type=jnp.float32)
        .astype(jnp.bfloat16)
        .reshape(seq_len, local_groups, HEAD_SIZE)
    )
    cosine_table, sine_table = rope_tables(seq_len, HEAD_SIZE)
    query_norm, query_hat, query_inv = norm_rows(query_raw, query_scale)
    query_rot = (
        query_norm * cosine_table[:, None, :] + rotate_half(query_norm) * sine_table[:, None, :]
    )
    key_norm, key_hat, key_inv = norm_rows(key_unrotated, key_scale)
    key_rot = key_norm * cosine_table[:, None, :] + rotate_half(key_norm) * sine_table[:, None, :]
    key_low = key_rot.astype(jnp.bfloat16)
    score_scale = 1.0 / math.sqrt(HEAD_SIZE)
    block_rows = min(seq_len, 512)
    block_count = seq_len // block_rows
    query_blocks = query_rot.astype(jnp.bfloat16).reshape(
        block_count, block_rows, local_groups, per_group, HEAD_SIZE
    )
    starts = jnp.arange(block_count, dtype=jnp.int32) * block_rows

    def block_scores(query_block, first_row):
        scores = (
            jnp.einsum("qhgd,khd->hgqk", query_block, key_low, preferred_element_type=jnp.float32)
            * score_scale
        )
        row_index = first_row + jnp.arange(block_rows, dtype=jnp.int32)
        key_index = jnp.arange(seq_len, dtype=jnp.int32)
        return jnp.where(key_index[None, :] <= row_index[:, None], scores, -1e30)

    def forward_block(operands):
        query_block, first_row = operands
        scores = block_scores(query_block, first_row)
        top_score = jnp.max(scores, axis=-1, keepdims=True)
        log_total = top_score + jnp.log(
            jnp.sum(jnp.exp(scores - top_score), axis=-1, keepdims=True)
        )
        attend_low = jnp.exp(scores - log_total).astype(jnp.bfloat16)
        mixed_heads = jnp.einsum(
            "hgqk,khd->qhgd", attend_low, value_reduced, preferred_element_type=jnp.float32
        )
        return (mixed_heads.astype(jnp.bfloat16), log_total)

    mixed_blocks, log_totals = lax.map(forward_block, (query_blocks, starts))
    mixed_low = mixed_blocks.reshape(seq_len, local_heads * HEAD_SIZE)
    attention_terms = jnp.einsum(
        "sh,dh->sd", mixed_low, output_full, preferred_element_type=jnp.float32
    )
    residual_mid = residual_in + sum_tokens(attention_terms)
    post_norm, post_hat, post_inv = norm_rows(residual_mid, post_scale)
    post_low = post_norm.astype(jnp.bfloat16)
    logits = jnp.dot(post_low, router_full, preferred_element_type=jnp.float32)
    experts = logits.shape[1]
    row_count = routes.shape[0]
    top_count = routes.shape[1]
    expert_ids = jnp.arange(experts, dtype=jnp.int32)
    chosen_mask = routes[:, :, None] == expert_ids[None, None, :]
    picked = jnp.sum(jnp.where(chosen_mask, logits[:, None, :], 0.0), axis=-1)
    route_gate = jax.nn.softmax(picked, axis=-1)
    route_total = row_count * top_count
    flat_routes = routes.reshape(-1)
    route_hits = (flat_routes[:, None] == expert_ids[None, :]).astype(jnp.int32)
    earlier = jnp.cumsum(route_hits, axis=0) - route_hits
    position = jnp.sum(earlier * route_hits, axis=1)
    capacity = 2 * row_count * top_count // experts
    slot_index = flat_routes * capacity + position
    filler = (
        jnp.full((experts * capacity,), route_total, dtype=jnp.int32)
        .at[slot_index]
        .set(jnp.arange(route_total, dtype=jnp.int32))
    )
    dp_count = lax.axis_size("dp")
    local_experts = gate_weight.shape[0]
    gate_use, up_use, down_use = (gate_weight, up_weight, down_weight)
    post_padded = jnp.concatenate(
        [post_low, jnp.zeros((1, MODEL_WIDTH), dtype=jnp.bfloat16)], axis=0
    )
    outgoing = post_padded[filler // top_count].reshape(
        dp_count, local_experts * capacity, MODEL_WIDTH
    )
    slot_input = to_slots(outgoing).reshape(-1, dp_count, local_experts, capacity, MODEL_WIDTH)
    gate_pre = jnp.einsum(
        "tnecd,edf->tnecf", slot_input, gate_use, preferred_element_type=jnp.float32
    )
    up_pre = jnp.einsum("tnecd,edf->tnecf", slot_input, up_use, preferred_element_type=jnp.float32)
    hidden_low = (jax.nn.silu(gate_pre) * up_pre).astype(jnp.bfloat16)
    expert_terms = jnp.einsum(
        "tnecf,efd->tnecd", hidden_low, down_use, preferred_element_type=jnp.float32
    )
    returned = from_slots(expert_terms, dp_count, MODEL_WIDTH).reshape(
        experts * capacity, MODEL_WIDTH
    )
    gathered = returned[slot_index].reshape(row_count, top_count, MODEL_WIDTH).astype(jnp.float32)
    result = (residual_mid + jnp.sum(route_gate[:, :, None] * gathered, axis=1)).astype(
        jnp.bfloat16
    )
    grad_out = cotangent.astype(jnp.float32)
    grad_gate = jnp.sum(gathered * grad_out[:, None, :], axis=-1)
    grad_routed = (
        (route_gate[:, :, None] * grad_out[:, None, :])
        .astype(jnp.bfloat16)
        .reshape(route_total, MODEL_WIDTH)
    )
    grad_padded = jnp.concatenate(
        [grad_routed, jnp.zeros((1, MODEL_WIDTH), dtype=jnp.bfloat16)], axis=0
    )
    grad_send = grad_padded[filler].reshape(dp_count, local_experts * capacity, MODEL_WIDTH)
    grad_slots = to_slots(grad_send).reshape(-1, dp_count, local_experts, capacity, MODEL_WIDTH)
    grad_hidden = jnp.einsum(
        "tnecd,efd->tnecf", grad_slots, down_use, preferred_element_type=jnp.float32
    )
    grad_down = jnp.einsum(
        "tnecf,tnecd->efd", hidden_low, grad_slots, preferred_element_type=jnp.float32
    )
    gate_sigmoid = jax.nn.sigmoid(gate_pre)
    grad_gate_pre = (
        grad_hidden * up_pre * gate_sigmoid * (1.0 + gate_pre * (1.0 - gate_sigmoid))
    ).astype(jnp.bfloat16)
    grad_up_pre = (grad_hidden * gate_pre * gate_sigmoid).astype(jnp.bfloat16)
    grad_gate_w = jnp.einsum(
        "tnecd,tnecf->edf", slot_input, grad_gate_pre, preferred_element_type=jnp.float32
    )
    grad_up_w = jnp.einsum(
        "tnecd,tnecf->edf", slot_input, grad_up_pre, preferred_element_type=jnp.float32
    )
    grad_slot_terms = jnp.einsum(
        "tnecf,edf->tnecd", grad_gate_pre, gate_use, preferred_element_type=jnp.float32
    )
    grad_slot_terms = grad_slot_terms + jnp.einsum(
        "tnecf,edf->tnecd", grad_up_pre, up_use, preferred_element_type=jnp.float32
    )
    grad_back = from_slots(grad_slot_terms, dp_count, MODEL_WIDTH).reshape(
        experts * capacity, MODEL_WIDTH
    )
    grad_post = jnp.sum(
        grad_back[slot_index].reshape(row_count, top_count, MODEL_WIDTH).astype(jnp.float32), axis=1
    )
    grad_picked = route_gate * (grad_gate - jnp.sum(route_gate * grad_gate, axis=-1, keepdims=True))
    grad_logits = jnp.sum(jnp.where(chosen_mask, grad_picked[:, :, None], 0.0), axis=1).astype(
        jnp.bfloat16
    )
    grad_post = grad_post + jnp.einsum(
        "te,de->td", grad_logits, router_full, preferred_element_type=jnp.float32
    )
    grad_router = jnp.einsum("td,te->de", post_low, grad_logits, preferred_element_type=jnp.float32)
    grad_mid_norm, post_terms = norm_back(grad_post, post_scale, post_hat, post_inv)
    grad_post_gain = jnp.sum(post_terms, axis=0)
    grad_mid = grad_out + grad_mid_norm
    grad_attention = gather_tokens(grad_mid.astype(jnp.bfloat16))
    held_weights = lax.optimization_barrier(
        (
            query_weight,
            key_projection_matrix,
            value_projection_matrix,
            output_weight,
            grad_attention,
        )
    )
    query_use, key_use, value_use, output_use = (
        lax.all_gather(held_weights[0], "dp", axis=1, tiled=True),
        lax.all_gather(held_weights[1], "dp", axis=1, tiled=True),
        lax.all_gather(held_weights[2], "dp", axis=1, tiled=True),
        lax.all_gather(held_weights[3], "dp", axis=0, tiled=True),
    )
    grad_mixed = jnp.einsum(
        "sd,dh->sh", grad_attention, output_use, preferred_element_type=jnp.float32
    ).astype(jnp.bfloat16)
    grad_output_w = jnp.einsum(
        "sd,sh->dh", grad_attention, mixed_low, preferred_element_type=jnp.float32
    )
    grad_mixed_blocks = grad_mixed.reshape(
        block_count, block_rows, local_groups, per_group, HEAD_SIZE
    )

    def backward_block(running, operands):
        grad_key_acc, grad_value_acc = running
        query_block, grad_block, log_block, first_row = operands
        attend = jnp.exp(block_scores(query_block, first_row) - log_block)
        attend_low = attend.astype(jnp.bfloat16)
        grad_attend = jnp.einsum(
            "qhgd,khd->hgqk", grad_block, value_reduced, preferred_element_type=jnp.float32
        )
        grad_value_acc = grad_value_acc + jnp.einsum(
            "hgqk,qhgd->khd", attend_low, grad_block, preferred_element_type=jnp.float32
        )
        row_inner = jnp.sum(attend * grad_attend, axis=-1, keepdims=True)
        grad_scores = (attend * (grad_attend - row_inner)).astype(jnp.bfloat16)
        grad_query_block = (
            jnp.einsum("hgqk,khd->qhgd", grad_scores, key_low, preferred_element_type=jnp.float32)
            * score_scale
        )
        grad_key_acc = (
            grad_key_acc
            + jnp.einsum(
                "hgqk,qhgd->khd", grad_scores, query_block, preferred_element_type=jnp.float32
            )
            * score_scale
        )
        return ((grad_key_acc, grad_value_acc), grad_query_block)

    zero_state = jnp.zeros((seq_len, local_groups, HEAD_SIZE), dtype=jnp.float32)
    (grad_key_rot, grad_value), grad_query_blocks = lax.scan(
        backward_block,
        (zero_state, zero_state),
        (query_blocks, grad_mixed_blocks, log_totals, starts),
    )
    grad_query_rot = grad_query_blocks.reshape(seq_len, local_heads, HEAD_SIZE)
    grad_query_norm = grad_query_rot * cosine_table[:, None, :] + rotate_back(
        grad_query_rot * sine_table[:, None, :]
    )
    grad_query_raw, query_terms = norm_back(grad_query_norm, query_scale, query_hat, query_inv)
    grad_query_gain = jnp.sum(query_terms, axis=(0, 1))
    grad_key_norm = grad_key_rot * cosine_table[:, None, :] + rotate_back(
        grad_key_rot * sine_table[:, None, :]
    )
    grad_key_raw, key_terms = norm_back(grad_key_norm, key_scale, key_hat, key_inv)
    grad_key_gain = jnp.sum(key_terms, axis=(0, 1))
    grad_query_low = grad_query_raw.reshape(seq_len, local_heads * HEAD_SIZE).astype(jnp.bfloat16)
    grad_key_low = grad_key_raw.reshape(seq_len, local_groups * HEAD_SIZE).astype(jnp.bfloat16)
    grad_value_low = grad_value.reshape(seq_len, local_groups * HEAD_SIZE).astype(jnp.bfloat16)
    grad_norm_terms = jnp.einsum(
        "sh,hd->sd", grad_query_low, query_use, preferred_element_type=jnp.float32
    )
    grad_norm_terms = grad_norm_terms + jnp.einsum(
        "sh,hd->sd", grad_key_low, key_use, preferred_element_type=jnp.float32
    )
    grad_norm_terms = grad_norm_terms + jnp.einsum(
        "sh,hd->sd", grad_value_low, value_use, preferred_element_type=jnp.float32
    )
    grad_normed = sum_tokens(grad_norm_terms)
    grad_query_w = jnp.einsum(
        "sh,sd->hd", grad_query_low, sequence, preferred_element_type=jnp.float32
    )
    grad_key_w = jnp.einsum("sh,sd->hd", grad_key_low, sequence, preferred_element_type=jnp.float32)
    grad_value_w = jnp.einsum(
        "sh,sd->hd", grad_value_low, sequence, preferred_element_type=jnp.float32
    )
    grad_in_norm, input_terms = norm_back(grad_normed, input_scale, input_hat, input_inv)
    grad_input_gain = jnp.sum(input_terms, axis=0)
    grad_inputs = (grad_mid + grad_in_norm).astype(jnp.bfloat16)
    grad_query_w, grad_key_w, grad_value_w, grad_output_w = (
        lax.psum_scatter(grad_query_w, "dp", scatter_dimension=1, tiled=True),
        lax.psum_scatter(grad_key_w, "dp", scatter_dimension=1, tiled=True),
        lax.psum_scatter(grad_value_w, "dp", scatter_dimension=1, tiled=True),
        lax.psum_scatter(grad_output_w, "dp", scatter_dimension=0, tiled=True),
    )
    grad_router, grad_input_gain, grad_post_gain, grad_query_gain, grad_key_gain = (
        lax.psum_scatter(grad_router, ("dp", "tensor"), scatter_dimension=0, tiled=True),
        lax.psum_scatter(grad_input_gain, ("dp", "tensor"), scatter_dimension=0, tiled=True),
        lax.psum_scatter(grad_post_gain, ("dp", "tensor"), scatter_dimension=0, tiled=True),
        lax.psum_scatter(grad_query_gain, ("dp", "tensor"), scatter_dimension=0, tiled=True),
        lax.psum_scatter(grad_key_gain, ("dp", "tensor"), scatter_dimension=0, tiled=True),
    )
    return (
        result,
        grad_inputs,
        grad_input_gain,
        grad_post_gain,
        grad_query_gain,
        grad_key_gain,
        grad_query_w,
        grad_key_w,
        grad_value_w,
        grad_output_w,
        grad_router,
        grad_gate_w,
        grad_up_w,
        grad_down,
    )


def solution(mesh):
    return jax.shard_map(
        on_device,
        mesh=mesh,
        in_specs=(
            P(("dp", "tensor"), None),
            P(("dp", "tensor")),
            P(("dp", "tensor")),
            P(("dp", "tensor")),
            P(("dp", "tensor")),
            P("tensor", "dp"),
            P("tensor", "dp"),
            P("tensor", "dp"),
            P("dp", "tensor"),
            P(("dp", "tensor"), None),
            P("dp", None, "tensor"),
            P("dp", None, "tensor"),
            P("dp", "tensor", None),
            P(("dp", "tensor"), None),
            P(("dp", "tensor"), None),
        ),
        out_specs=(
            P(("dp", "tensor"), None),
            P(("dp", "tensor"), None),
            P(("dp", "tensor")),
            P(("dp", "tensor")),
            P(("dp", "tensor")),
            P(("dp", "tensor")),
            P("tensor", "dp"),
            P("tensor", "dp"),
            P("tensor", "dp"),
            P("dp", "tensor"),
            P(("dp", "tensor"), None),
            P("dp", None, "tensor"),
            P("dp", None, "tensor"),
            P("dp", "tensor", None),
        ),
        check_vma=False,
    )
```

profile of v0, /device:TPU:0, one launch (start us, length us, event | category | flops | bytes accessed | tf_op | source)
XLA Modules:
  0.0 3147.4 jit_solution(7730949092006251708)
XLA Ops:
  12.1 42.2 %all-reduce.13 = (bf16[2048]{0:T(1024)(128)(2,1)S(1)}, bf16[128]{0:T(256)(128)(2,1)S(1)}, bf16[128]{0:T(256)(128)(2,1)S(1)}, bf16[2048]{0:T(1024)(128)(2,1)S(1)}) all-reduce(bf16[2048]{0:T(1024)(128)(2,1)S(1)} %dynamic-update-slice, bf16[128]{0:T(256)(128)(2,1)S(1)} %dynamic-update-slice.1, ...), channel_id=1, replica_groups=mesh['dp'=16,'tensor'=2] {'dp','tensor'}, use_global_device_ids=true, to_apply=%add.2 | all-reduce | flops 4352 | bytes 17408
  78.1 38.8 %all-gather.20.cloned.1.call-done = bf16[256,2048]{1,0:T(8,128)(2,1)} async-done(((bf16[256,128]{1,0:T(8,128)(2,1)}), bf16[256,2048]{1,0:T(8,128)(2,1)}) %all-gather.20.cloned.1.call-update) | async-done | bytes 1048592 | tf_op jit(solution)/shard_map/all_gather | solution.py:109
  120.4 35.0 %all-gather.18.cloned.1.call-done = bf16[256,2048]{1,0:T(8,128)(2,1)} async-done(((bf16[256,128]{1,0:T(8,128)(2,1)}), bf16[256,2048]{1,0:T(8,128)(2,1)}) %all-gather.18.cloned.1.call-update) | async-done | bytes 1048592 | tf_op jit(solution)/shard_map/all_gather | solution.py:110
  158.1 76.7 %all-gather.22.cloned.1.call-done = bf16[2048,2048]{1,0:T(8,128)(2,1)} async-done(((bf16[2048,128]{1,0:T(8,128)(2,1)}), bf16[2048,2048]{1,0:T(8,128)(2,1)}) %all-gather.22.cloned.1.call-update) | async-done | bytes 8388624 | tf_op jit(solution)/shard_map/all_gather | solution.py:108
  256.4 52.8 %all-gather.24.cloned.1.call-done = bf16[2048,2048]{1,0:T(8,128)(2,1)} async-done(((bf16[128,2048]{1,0:T(8,128)(2,1)}), bf16[2048,2048]{1,0:T(8,128)(2,1)}) %all-gather.24.cloned.1.call-update) | async-done | bytes 8388624 | tf_op jit(solution)/shard_map/all_gather | solution.py:111
  363.4 202.0 %all-gather.2 = bf16[32,64,32]{1,2,0:T(8,128)(2,1)S(1)} all-gather(bf16[1,64,32]{1,2,0:T(8,128)(2,1)S(1)} %bitcast.328), channel_id=1, replica_groups=mesh['dp'=16,'tensor'=2] {'dp','tensor'}, dimensions={0}, use_global_device_ids=true | all-gather | bytes 135168 | tf_op jit(solution)/shard_map/all_gather | solution.py:93
  594.7 215.5 %all_to_all.20 = bf16[16,128,2048]{2,1,0:T(8,128)(2,1)} all-to-all(bf16[16,128,2048]{2,1,0:T(8,128)(2,1)} %bitcast.299), channel_id=1, replica_groups=mesh['dp'=16,'tensor'=2] {'dp'}, dimensions={0} | all-to-all | bytes 16777216 | tf_op jit(solution)/shard_map/all_to_all | solution.py:59
  840.6 168.8 %all-gather.38.cloned.1.call-done = bf16[32,128,2048]{2,1,0:T(8,128)(2,1)} async-done(((bf16[16,128,2048]{2,1,0:T(8,128)(2,1)}), bf16[32,128,2048]{2,1,0:T(8,128)(2,1)}) %all-gather.38.cloned.1.call-update) | async-done | bytes 16777232 | tf_op jit(solution)/shard_map/all_gather | solution.py:64
  1009.3 19.3 fusion.20
  1058.6 20.0 fusion
  1079.9 736.6 %all-reduce.17.cloned.1.call-done = (bf16[2,16,2,64,2048]{4,3,1,0,2:T(8,128)(2,1)}, bf16[2,16,2,64,2048]{4,3,1,0,2:T(8,128)(2,1)}) async-done(((bf16[2,16,2,64,2048]{4,3,1,0,2:T(8,128)(2,1)}, bf16[2,16,2,64,2048]{4,3,1,0,2:T(8,128)(2,1)}), (bf16[2,16,2,64,2048]{4,3,1,0,2:T(8,128)(2,1)}, bf16[2,16,2,64,2048]{4,3,1,0,2:T(8,128)(2,1)})) %all-reduce.17.cloned.1.call-update) | async-done | bytes 33554448
  1851.4 142.2 %all-to-all-done.3 = bf16[16,128,2048]{2,1,0:T(8,128)(2,1)} async-done(((bf16[16,128,2048]{2,1,0:T(8,128)(2,1)}), bf16[16,128,2048]{2,1,0:T(8,128)(2,1)}, u32[]{:S(2)}, u32[]{:S(2)}) %all-to-all-start.3) | async-done | bytes 8388640 | tf_op jit(solution)/shard_map/all_to_all | solution.py:59
  1993.6 36.7 %all-to-all-start.1 = ((bf16[16,128,2048]{2,1,0:T(8,128)(2,1)}), bf16[16,128,2048]{2,1,0:T(8,128)(2,1)}, u32[]{:S(2)}, u32[]{:S(2)}) async-start(bf16[16,128,2048]{2,1,0:T(8,128)(2,1)} %bitcast.300), calls=%async_computation.2 | async-start | bytes 16777216 | tf_op jit(solution)/shard_map/all_to_all | solution.py:59
  2050.1 130.8 %all-to-all-done.1 = bf16[16,128,2048]{2,1,0:T(8,128)(2,1)} async-done(((bf16[16,128,2048]{2,1,0:T(8,128)(2,1)}), bf16[16,128,2048]{2,1,0:T(8,128)(2,1)}, u32[]{:S(2)}, u32[]{:S(2)}) %all-to-all-start.1) | async-done | bytes 8388640 | tf_op jit(solution)/shard_map/all_to_all | solution.py:59
  2206.5 53.7 %all-gather.26.cloned.1.call-done = bf16[256,2048]{1,0:T(8,128)(2,1)} async-done(((bf16[128,2048]{1,0:T(8,128)(2,1)}), bf16[256,2048]{1,0:T(8,128)(2,1)}) %all-gather.26.cloned.1.call-update) | async-done | bytes 1048592 | tf_op jit(solution)/shard_map/all_gather | solution.py:49
  2271.0 65.7 %all-gather.28.cloned.1.call-done = bf16[2048,2048]{1,0:T(8,128)(2,1)} async-done(((bf16[128,2048]{1,0:T(8,128)(2,1)}), bf16[2048,2048]{1,0:T(8,128)(2,1)}) %all-gather.28.cloned.1.call-update) | async-done | bytes 8388624 | tf_op jit(solution)/shard_map/all_gather | solution.py:285
  2386.8 28.1 all-gather.30.cloned.1.call-done
  2421.0 31.0 all-gather.32.cloned.1.call-done
  2455.7 34.6 %all-gather.34.cloned.1.call-done = bf16[256,2048]{1,0:T(8,128)(2,1)} async-done(((bf16[256,128]{1,0:T(8,128)(2,1)}), bf16[256,2048]{1,0:T(8,128)(2,1)}) %all-gather.34.cloned.1.call-update) | async-done | bytes 1048592 | tf_op jit(solution)/shard_map/all_gather | solution.py:284
  2557.2 71.3 %reduce-scatter.28.cloned.1.call-done = f32[64,32]{1,0:T(8,128)} async-done(((f32[2048,32]{1,0:T(8,128)}), f32[64,32]{1,0:T(8,128)}) %reduce-scatter.28.cloned.1.call-update) | async-done | bytes 8208
  2648.7 39.9 %all-reduce.12 = (f32[2048]{0:T(1024)S(1)}, f32[2048]{0:T(1024)S(1)}, f32[128]{0:T(128)S(1)}, f32[128]{0:T(128)S(1)}) all-reduce(f32[2048]{0:T(1024)S(1)} %get-tuple-element.73, f32[2048]{0:T(1024)S(1)} %copy-done.65, f32[128]{0:T(128)S(1)} %copy-done.84, ...), channel_id=8, replica_groups=mesh['dp'=16,'tensor'=2] {'dp','tensor'}, use_global_device_ids=true, to_apply=%region_28.29.clone | all-reduce | flops 4352 | bytes 34816
  2713.5 65.0 %reduce-scatter.22.cloned.1.call-done = f32[256,128]{1,0:T(8,128)} async-done(((f32[256,2048]{1,0:T(8,128)}), f32[256,128]{1,0:T(8,128)}) %reduce-scatter.22.cloned.1.call-update) | async-done | bytes 131088 | tf_op jit(solution)/shard_map/reduce_scatter | solution.py:365
  2778.5 181.0 %reduce-scatter.26.cloned.1.call-done = f32[128,2048]{1,0:T(8,128)} async-done(((f32[2048,2048]{1,0:T(8,128)}), f32[128,2048]{1,0:T(8,128)}) %reduce-scatter.26.cloned.1.call-update) | async-done | bytes 1048592 | tf_op jit(solution)/shard_map/reduce_scatter | solution.py:367
  2959.5 180.8 %reduce-scatter.20.cloned.1.call-done = f32[2048,128]{1,0:T(8,128)} async-done(((f32[2048,2048]{1,0:T(8,128)}), f32[2048,128]{1,0:T(8,128)}) %reduce-scatter.20.cloned.1.call-update) | async-done | bytes 1048592 | tf_op jit(solution)/shard_map/reduce_scatter | solution.py:364
  (364 shorter events, 463.3 us)
Async XLA Ops:
  7.2 1002.2 %copy-start = (bf16[2,384,2048]{2,1,0:T(8,128)(2,1)S(1)}, bf16[2,384,2048]{2,1,0:T(8,128)(2,1)}, u32[]{:S(2)}) copy-start(bf16[2,384,2048]{2,1,0:T(8,128)(2,1)} %param.27) | copy-start | bytes 9437188
  7.2 70.9 %all-gather.16.cloned.1.call-start = ((), (), s32[]{:S(2)}) async-start(), calls=%async_computation.11 | async-start | bytes 1572864 | tf_op jit(solution)/shard_map/all_gather | solution.py:49
  56.9 60.1 %all-gather.20.cloned.1.call-start = ((), (), s32[]{:S(2)}) async-start(), calls=%async_computation.13 | async-start | bytes 1114112 | tf_op jit(solution)/shard_map/all_gather | solution.py:109
  57.6 97.8 %all-gather.18.cloned.1.call-start = ((), (), s32[]{:S(2)}) async-start(), calls=%async_computation.12 | async-start | bytes 1114112 | tf_op jit(solution)/shard_map/all_gather | solution.py:110
  58.3 176.4 %all-gather.22.cloned.1.call-start = ((), (), s32[]{:S(2)}) async-start(), calls=%async_computation.14 | async-start | bytes 8912896 | tf_op jit(solution)/shard_map/all_gather | solution.py:108
  58.9 250.3 %all-gather.24.cloned.1.call-start = ((), (), s32[]{:S(2)}) async-start(), calls=%async_computation.15 | async-start | bytes 8912896 | tf_op jit(solution)/shard_map/all_gather | solution.py:111
  59.5 276.0 %reduce-scatter.16.cloned.1.call-start = ((), (), s32[]{:S(2)}) async-start(), calls=%async_computation.16 | async-start | bytes 1572864 | tf_op jit(solution)/shard_map/reduce_scatter | solution.py:53
  357.5 210.4 %all-to-all-start = ((bf16[16,128,2048]{2,1,0:T(8,128)(2,1)}), bf16[16,128,2048]{2,1,0:T(8,128)(2,1)}, u32[]{:S(2)}, u32[]{:S(2)}) async-start(bf16[16,128,2048]{2,1,0:T(8,128)(2,1)} %bitcast.298), calls=%async_computation.1 | async-start | bytes 16777216 | tf_op jit(solution)/shard_map/all_to_all | solution.py:59
  363.3 446.9 %all-gather.36.cloned.1.call-start = ((), (), s32[]{:S(2)}) async-start(), calls=%async_computation.27 | async-start | bytes 25165824 | tf_op jit(solution)/shard_map/all_gather | solution.py:64
  568.0 441.3 %all-gather.38.cloned.1.call-start = ((), (), s32[]{:S(2)}) async-start(), calls=%async_computation.28 | async-start | bytes 25165824 | tf_op jit(solution)/shard_map/all_gather | solution.py:64
  810.2 1006.3 %all-reduce.17.cloned.1.call-start = ((), (), s32[]{:S(2)}) async-start(), calls=%async_computation.30 | async-start | bytes 67108864
  1837.4 156.2 %all-to-all-start.3 = ((bf16[16,128,2048]{2,1,0:T(8,128)(2,1)}), bf16[16,128,2048]{2,1,0:T(8,128)(2,1)}, u32[]{:S(2)}, u32[]{:S(2)}) async-start(bf16[16,128,2048]{2,1,0:T(8,128)(2,1)} %bitcast.301), calls=%async_computation.4 | async-start | bytes 16777216 | tf_op jit(solution)/shard_map/all_to_all | solution.py:59
  1993.6 187.3 %all-to-all-start.1 = ((bf16[16,128,2048]{2,1,0:T(8,128)(2,1)}), bf16[16,128,2048]{2,1,0:T(8,128)(2,1)}, u32[]{:S(2)}, u32[]{:S(2)}) async-start(bf16[16,128,2048]{2,1,0:T(8,128)(2,1)} %bitcast.300), calls=%async_computation.2 | async-start | bytes 16777216 | tf_op jit(solution)/shard_map/all_to_all | solution.py:59
  2030.3 229.8 %all-gather.26.cloned.1.call-start = ((), (), s32[]{:S(2)}) async-start(), calls=%async_computation.17 | async-start | bytes 1572864 | tf_op jit(solution)/shard_map/all_gather | solution.py:49
  2206.4 130.2 %all-gather.28.cloned.1.call-start = ((), (), s32[]{:S(2)}) async-start(), calls=%async_computation.18 | async-start | bytes 8912896 | tf_op jit(solution)/shard_map/all_gather | solution.py:285
  2260.2 154.8 %all-gather.30.cloned.1.call-start = ((), (), s32[]{:S(2)}) async-start(), calls=%async_computation.19 | async-start | bytes 8912896 | tf_op jit(solution)/shard_map/all_gather | solution.py:282
  2260.8 191.2 %all-gather.32.cloned.1.call-start = ((), (), s32[]{:S(2)}) async-start(), calls=%async_computation.20 | async-start | bytes 1114112 | tf_op jit(solution)/shard_map/all_gather | solution.py:283
  2261.5 228.8 %all-gather.34.cloned.1.call-start = ((), (), s32[]{:S(2)}) async-start(), calls=%async_computation.21 | async-start | bytes 1114112 | tf_op jit(solution)/shard_map/all_gather | solution.py:284
  2262.1 366.4 %reduce-scatter.28.cloned.1.call-start = ((), (), s32[]{:S(2)}) async-start(), calls=%async_computation.29 | async-start | bytes 1081344
  2270.8 376.3 %reduce-scatter.18.cloned.1.call-start = ((), (), s32[]{:S(2)}) async-start(), calls=%async_computation.22 | async-start | bytes 1572864 | tf_op jit(solution)/shard_map/reduce_scatter | solution.py:53
  2493.7 219.9 %reduce-scatter.24.cloned.1.call-start = ((), (), s32[]{:S(2)}) async-start(), calls=%async_computation.25 | async-start | bytes 2228224 | tf_op jit(solution)/shard_map/reduce_scatter | solution.py:366
  2495.6 282.9 %reduce-scatter.22.cloned.1.call-start = ((), (), s32[]{:S(2)}) async-start(), calls=%async_computation.24 | async-start | bytes 2228224 | tf_op jit(solution)/shard_map/reduce_scatter | solution.py:365
  2497.4 462.1 %reduce-scatter.26.cloned.1.call-start = ((), (), s32[]{:S(2)}) async-start(), calls=%async_computation.26 | async-start | bytes 17825792 | tf_op jit(solution)/shard_map/reduce_scatter | solution.py:367
  2505.7 634.6 %reduce-scatter.20.cloned.1.call-start = ((), (), s32[]{:S(2)}) async-start(), calls=%async_computation.23 | async-start | bytes 17825792 | tf_op jit(solution)/shard_map/reduce_scatter | solution.py:364
  (85 other events, 3504.0 us)
Sparse Core Ops, SparseCore 0:
  57.0 21.0 all-gather.15
  80.3 36.6 all-gather.19
  119.1 36.2 all-gather.17
  157.4 77.3 all-gather.21
  236.8 72.4 all-gather.23
  316.5 18.9 reduce-scatter.15
  568.1 224.4 all-gather.35
  810.3 198.9 all-gather.37
  1078.8 737.6 all-reduce.16
  2206.5 53.5 all-gather.25
  2262.3 74.2 all-gather.27
  2338.7 76.2 all-gather.29
  2417.1 34.8 all-gather.31
  2454.0 36.2 all-gather.33
  2492.4 136.1 reduce-scatter.27
  2630.6 16.3 reduce-scatter.17
  2651.2 62.2 reduce-scatter.23
  2717.7 60.7 reduce-scatter.21
  2783.2 176.2 reduce-scatter.25
  2964.0 176.2 reduce-scatter.19
where the time goes:
time: 3150 us
  waiting for transfers between devices  2150 us (68%)
  blocking collectives  500 us (16%)
  matrix products  214 us (7%)
  local copies, waits for them, and re-layouts  144 us (5%)
  other arithmetic  70.8 us (2%)
  starting transfers between devices  49.5 us (2%)
    unnamed x22, waiting for transfers between devices  812 us
    all_to_all x3, waiting for transfers between devices, move_rows(): return lax.all_to_all(rows, 'dp', split_axis=0, concat_axis=0, tiled=True)  273 us
    all_to_all x1, blocking collectives, move_rows(): return lax.all_to_all(rows, 'dp', split_axis=0, concat_axis=0, tiled=True)  215 us
    all_gather x1, blocking collectives, on_device(): lax.all_gather(router_weight, ('dp', 'tensor'), axis=0, tiled=True)  202 us
    reduce_scatter x1, waiting for transfers between devices, on_device(): lax.psum_scatter(grad_output_w, 'dp', scatter_dimension=0, tiled=True)  181 us
    reduce_scatter x1, waiting for transfers between devices, on_device(): lax.psum_scatter(grad_query_w, 'dp', scatter_dimension=1, tiled=True)  181 us
    all_gather x2, waiting for transfers between devices, to_slots(): return lax.all_gather(routed[None], 'tensor', axis=0, tiled=True)  169 us
    unnamed x2, blocking collectives  82 us
  transfers between devices with their start and end apart: 23, of which 21 were waited for; matrix products, arithmetic and copies ran while one was open for 9% of the time, Pallas kernels for 0%

commit v1 on v0

v1 whole, which is shorter than its diff:
```python
import functools
import math

import jax
import jax.numpy as jnp
import numpy as np
from jax import lax
from jax.experimental import pallas as pl
from jax.experimental.pallas import tpu as pltpu
from jax.sharding import PartitionSpec as P

HEAD_SIZE = 128
LANES = 128
EPSILON = 1e-06
ROPE_BASE = 1000000.0
BOTH = ("dp", "tensor")
BF16 = jnp.bfloat16
F32 = jnp.float32
STEP_BLOCKS = 4
VMEM_BYTES = 60 * 1024 * 1024


def norm_rows(values, weights):
    inverse = lax.rsqrt(jnp.mean(values * values, axis=-1, keepdims=True) + EPSILON)
    normalized_rows = values * inverse
    return (normalized_rows * weights, normalized_rows, inverse)


def norm_back(upstream, weights, normalized_rows, inverse):
    scaled = upstream * weights
    inner_term = jnp.mean(scaled * normalized_rows, axis=-1, keepdims=True)
    return (inverse * (scaled - normalized_rows * inner_term), upstream * normalized_rows)


def rope_tables(length, head_width):
    half_width = head_width // 2
    frequency = jnp.exp(
        jnp.arange(half_width, dtype=F32) * (-2.0 * math.log(ROPE_BASE) / head_width)
    )
    angles = jnp.arange(length, dtype=F32)[:, None] * frequency[None, :]
    angles = jnp.concatenate([angles, angles], axis=-1)
    return (jnp.cos(angles), jnp.sin(angles))


def rotate_half(values):
    half_width = values.shape[-1] // 2
    return jnp.concatenate([-values[..., half_width:], values[..., :half_width]], axis=-1)


def rotate_back(values):
    half_width = values.shape[-1] // 2
    return jnp.concatenate([values[..., half_width:], -values[..., :half_width]], axis=-1)


def dot(left, right, left_dim=1, right_dim=0):
    return lax.dot_general(
        left, right, (((left_dim,), (right_dim,)), ((), ())), preferred_element_type=F32
    )


LATTICE = {"z": 4, "x": 2, "core": 2, "y": 2}


def is_lattice(dp_count, tensor_count):
    return dp_count == 16 and tensor_count == 2


def hop(values, axis, step=1):
    sizes = tuple(LATTICE.values())
    place = list(LATTICE).index(axis)
    pairs = []
    for source in range(math.prod(sizes)):
        spot = list(np.unravel_index(source, sizes))
        spot[place] = (spot[place] + step) % sizes[place]
        pairs.append((source, int(np.ravel_multi_index(spot, sizes))))
    return lax.ppermute(values, BOTH, pairs)


def my_spot():
    chip_core = lax.axis_index("dp")
    return {
        "z": chip_core // 4,
        "x": (chip_core // 2) % 2,
        "core": chip_core % 2,
        "y": lax.axis_index("tensor"),
    }


def add_low(first, second):
    return (first.astype(F32) + second.astype(F32)).astype(BF16)


class Pending:
    def __init__(self, first, second):
        self.parts = (first, second)

    def piece(self, place, dim):
        first, second = (lax.index_in_dim(part, place, dim, keepdims=False) for part in self.parts)
        return add_low(first, second)


def reduce_home(partner, own, dims, order):
    dims = list(dims)
    pending = Pending(own, hop(partner, "core"))
    for axis in order:
        dim = dims.index(axis)
        dims.remove(axis)
        if axis == "z":
            moving = pending.piece(3, dim)
            for place in (2, 1):
                moving = add_low(hop(moving, "z", -1), pending.piece(place, dim))
            pending = Pending(pending.piece(0, dim), hop(moving, "z", -1))
        else:
            pending = Pending(pending.piece(0, dim), hop(pending.piece(1, dim), axis))
    first, second = pending.parts
    return first.astype(F32) + second.astype(F32)


def reduce_small(values):
    device_count = values.shape[0]
    number = lax.axis_index("dp") * lax.axis_size("tensor") + lax.axis_index("tensor")
    bit = device_count // 2
    while bit:
        halves = values.reshape((2, bit) + values.shape[1:])
        mine = (number // bit) % 2
        pairs = [(source, source ^ bit) for source in range(device_count)]
        sent = lax.dynamic_index_in_dim(halves, 1 - mine, 0, keepdims=False)
        kept = lax.dynamic_index_in_dim(halves, mine, 0, keepdims=False)
        values = kept + lax.ppermute(sent, BOTH, pairs)
        bit //= 2
    return values[0]


def swap_tensor(values):
    return lax.ppermute(values, "tensor", [(0, 1), (1, 0)])


def in_order(mine, other):
    first = lax.axis_index("tensor") == 0
    return jnp.where(
        first, jnp.concatenate([mine, other], axis=0), jnp.concatenate([other, mine], axis=0)
    )


def sum_tokens(terms):
    low = terms.astype(BF16).reshape((2, terms.shape[0] // 2) + terms.shape[1:])
    half = lax.axis_index("tensor")
    sent = lax.dynamic_index_in_dim(low, 1 - half, 0, keepdims=False)
    kept = lax.dynamic_index_in_dim(low, half, 0, keepdims=False)
    return kept.astype(F32) + swap_tensor(sent).astype(F32)


def choose(position_row, capacity):
    slot = lax.broadcasted_iota(jnp.int32, (capacity, position_row.shape[1]), 0).astype(F32)
    picks = [
        (slot == position_row[e : e + 1, :]).astype(F32) for e in range(position_row.shape[0])
    ]
    return picks


def expert_kernel(capacity, widths, perm, first, *refs):
    blocks = STEP_BLOCKS
    token_refs, grad_refs = refs[:blocks], refs[blocks : 2 * blocks]
    position_ref, mask_ref, router_ref, up_ref, up_t_ref, down_t_ref = refs[
        2 * blocks : 2 * blocks + 6
    ]
    rows_ref, grad_rows_ref, gated_ref, grad_gate_ref, grad_up_ref = refs[
        2 * blocks + 6 : 2 * blocks + 11
    ]
    out_refs = refs[2 * blocks + 11 : 2 * blocks + 14]
    packed_ref = refs[2 * blocks + 14]
    experts_here = up_ref.shape[0]
    hidden_units = down_t_ref.shape[2]
    width = token_refs[0].shape[2]
    first_expert = first[0]
    gates = [[] for _ in range(experts_here)]
    choices = []
    for j in range(blocks):
        tokens = token_refs[j][0]
        grads = grad_refs[j][0]
        picks = choose(position_ref[j], capacity)
        choice = jnp.concatenate(picks, axis=0).astype(BF16)
        choices.append(choice)
        rows = dot(choice, tokens).astype(BF16)
        grad_rows = dot(choice, grads).astype(BF16)
        logits = dot(router_ref[...], tokens, 1, 1)
        chosen = mask_ref[j].astype(F32) > 0.5
        top = jnp.max(jnp.where(chosen, logits, -3e38), axis=0, keepdims=True)
        powers = jnp.where(chosen, jnp.exp(jnp.minimum(logits - top, 0.0)), 0.0)
        gate_all = powers / jnp.sum(powers, axis=0, keepdims=True)
        expert_number = lax.broadcasted_iota(jnp.int32, gate_all.shape, 0)
        for e in range(experts_here):
            here = slice(j * capacity, (j + 1) * capacity)
            rows_ref[e, here, :] = rows[e * capacity : (e + 1) * capacity]
            grad_rows_ref[e, here, :] = grad_rows[e * capacity : (e + 1) * capacity]
            gate_row = jnp.sum(
                jnp.where(expert_number == first_expert + e, gate_all, 0.0), axis=0, keepdims=True
            )
            gates[e].append(jnp.sum(picks[e] * gate_row, axis=1, keepdims=True))
    for e in range(experts_here):
        both = dot(rows_ref[e], up_ref[e])
        gate_pre = both[:, :hidden_units]
        up_pre = both[:, hidden_units:]
        raw = dot(grad_rows_ref[e], down_t_ref[e])
        sigmoid = 1.0 / (1.0 + jnp.exp(-gate_pre))
        silu = gate_pre * sigmoid
        hidden = silu * up_pre
        gate = jnp.concatenate(gates[e], axis=0)
        grad_gate = jnp.sum(hidden * raw, axis=1, keepdims=True)
        grad_hidden = gate * raw
        grad_gate_pre = (
            grad_hidden * up_pre * sigmoid * (1.0 + gate_pre * (1.0 - sigmoid))
        ).astype(BF16)
        grad_up_pre = (grad_hidden * silu).astype(BF16)
        gated_ref[e] = (gate * hidden).astype(BF16)
        grad_gate_ref[e] = grad_gate_pre
        grad_up_ref[e] = grad_up_pre
        back = dot(grad_gate_pre, up_t_ref[e, :hidden_units, :]) + dot(
            grad_up_pre, up_t_ref[e, hidden_units:, :]
        )
        lane = lax.broadcasted_iota(jnp.int32, (blocks * capacity, LANES), 1)
        extra = jnp.where(lane == first_expert + e, grad_gate, 0.0).astype(BF16)
        back = back.astype(BF16)
        for j in range(blocks):
            packed_ref[j, e * capacity : (e + 1) * capacity, :width] = back[
                j * capacity : (j + 1) * capacity
            ]
            packed_ref[j, e * capacity : (e + 1) * capacity, width:] = extra[
                j * capacity : (j + 1) * capacity
            ]
    for j in range(blocks):
        home = dot(choices[j], packed_ref[j], 0, 0).astype(BF16)
        start = 0
        for out_ref, size in zip(out_refs, widths):
            out_ref[j] = home[:, start : start + size]
            start += size


def block_spec(width, place):
    return pl.BlockSpec(
        (1, LANES, width), lambda i, perm, first: (perm[i * STEP_BLOCKS + place], 0, 0)
    )


def whole(shape):
    return pl.BlockSpec(
        shape, lambda i, *scalars: (0,) * len(shape), pipeline_mode=pl.Buffered(1)
    )


def stepped(shape, dim):
    return pl.BlockSpec(
        shape, lambda i, *scalars: tuple(i if d == dim else 0 for d in range(len(shape)))
    )


def expert_grads(
    perm, first, tokens, grads, position, mask, router_t, up_both, up_both_t, down_t, capacity, widths
):
    count = perm.shape[0]
    width = tokens.shape[2]
    experts_here, hidden_units = down_t.shape[0], down_t.shape[2]
    slots = STEP_BLOCKS * capacity
    expert_count = router_t.shape[0]
    slot_shape = lambda size: jax.ShapeDtypeStruct((experts_here, count * capacity, size), BF16)
    flops = 2 * count * capacity * experts_here * (7 * hidden_units * width + 3 * LANES * width)
    call = pl.pallas_call(
        functools.partial(expert_kernel, capacity, widths),
        grid_spec=pltpu.PrefetchScalarGridSpec(
            num_scalar_prefetch=2,
            grid=(count // STEP_BLOCKS,),
            in_specs=[block_spec(width, j) for j in range(STEP_BLOCKS)] * 2
            + [
                stepped((STEP_BLOCKS, experts_here, LANES), 0),
                stepped((STEP_BLOCKS, expert_count, LANES), 0),
                whole(router_t.shape),
                whole(up_both.shape),
                whole(up_both_t.shape),
                whole(down_t.shape),
            ],
            out_specs=[stepped((experts_here, slots, width), 1)] * 2
            + [stepped((experts_here, slots, hidden_units), 1)] * 3
            + [stepped((STEP_BLOCKS, LANES, size), 0) for size in widths],
            scratch_shapes=[
                pltpu.VMEM((STEP_BLOCKS, experts_here * capacity, sum(widths)), BF16)
            ],
        ),
        out_shape=[slot_shape(width)] * 2
        + [slot_shape(hidden_units)] * 3
        + [jax.ShapeDtypeStruct((count, LANES, size), BF16) for size in widths],
        compiler_params=pltpu.CompilerParams(vmem_limit_bytes=VMEM_BYTES),
        cost_estimate=pl.CostEstimate(
            flops=flops, transcendentals=0, bytes_accessed=6 * count * LANES * width * 2
        ),
        name="expert_grads",
    )
    return call(
        perm, first, *([tokens] * STEP_BLOCKS), *([grads] * STEP_BLOCKS),
        position, mask, router_t, up_both, up_both_t, down_t,
    )


def output_kernel(capacity, widths, gated_ref, position_ref, down_ref, *refs):
    out_refs = refs[: len(widths)]
    packed_ref = refs[len(widths)]
    for e in range(down_ref.shape[0]):
        rows = dot(gated_ref[e], down_ref[e]).astype(BF16)
        for j in range(STEP_BLOCKS):
            packed_ref[j, e * capacity : (e + 1) * capacity, :] = rows[
                j * capacity : (j + 1) * capacity
            ]
    for j in range(STEP_BLOCKS):
        choice = jnp.concatenate(choose(position_ref[j], capacity), axis=0).astype(BF16)
        home = dot(choice, packed_ref[j], 0, 0).astype(BF16)
        start = 0
        for out_ref, size in zip(out_refs, widths):
            out_ref[j] = home[:, start : start + size]
            start += size


def expert_outputs(gated, position, down, capacity, widths):
    count = position.shape[0]
    experts_here, hidden_units, width = down.shape
    slots = STEP_BLOCKS * capacity
    call = pl.pallas_call(
        functools.partial(output_kernel, capacity, widths),
        grid=(count // STEP_BLOCKS,),
        in_specs=[
            stepped((experts_here, slots, hidden_units), 1),
            stepped((STEP_BLOCKS, experts_here, LANES), 0),
            whole(down.shape),
        ],
        out_specs=[stepped((STEP_BLOCKS, LANES, size), 0) for size in widths],
        out_shape=[jax.ShapeDtypeStruct((count, LANES, size), BF16) for size in widths],
        scratch_shapes=[pltpu.VMEM((STEP_BLOCKS, experts_here * capacity, width), BF16)],
        compiler_params=pltpu.CompilerParams(vmem_limit_bytes=VMEM_BYTES),
        cost_estimate=pl.CostEstimate(
            flops=2 * count * capacity * experts_here * (hidden_units * width + LANES * width),
            transcendentals=0,
            bytes_accessed=2 * count * LANES * width * 2,
        ),
        name="expert_outputs",
    )
    return call(gated, position, down)


def chunk_kernel(widths, perm, *refs):
    left = jnp.concatenate([ref[...] for ref in refs[:STEP_BLOCKS]], axis=1)
    product = dot(left, refs[STEP_BLOCKS][...], 0, 0).astype(BF16)
    start = 0
    for out_ref, size in zip(refs[STEP_BLOCKS + 1 :], widths):
        for j in range(STEP_BLOCKS):
            out_ref[j] = product[j * LANES : (j + 1) * LANES, start : start + size]
        start += size


def chunk_products(perm, left, right, widths):
    count = perm.shape[0]
    tokens = left.shape[0]

    def column_block(place):
        return pl.BlockSpec((tokens, LANES), lambda i, perm: (0, perm[i * STEP_BLOCKS + place]))

    call = pl.pallas_call(
        functools.partial(chunk_kernel, widths),
        grid_spec=pltpu.PrefetchScalarGridSpec(
            num_scalar_prefetch=1,
            grid=(count // STEP_BLOCKS,),
            in_specs=[column_block(j) for j in range(STEP_BLOCKS)] + [whole(right.shape)],
            out_specs=[stepped((STEP_BLOCKS, LANES, size), 0) for size in widths],
        ),
        out_shape=[jax.ShapeDtypeStruct((count, LANES, size), BF16) for size in widths],
        compiler_params=pltpu.CompilerParams(vmem_limit_bytes=VMEM_BYTES),
        cost_estimate=pl.CostEstimate(
            flops=2 * count * LANES * tokens * right.shape[1],
            transcendentals=0,
            bytes_accessed=count * LANES * right.shape[1] * 2,
        ),
        name="chunk_products",
    )
    return call(perm, *([left] * STEP_BLOCKS), right)


def block_orders(lattice, device_count):
    if not lattice:
        numbers = jnp.arange(device_count, dtype=jnp.int32)
        return numbers[: device_count // 2], numbers[device_count // 2 :]
    spot = my_spot()
    dz, dx, dy = (grid.reshape(-1) for grid in np.indices((4, 2, 2)).astype(np.int32))
    chip = (spot["z"] - dz + 4) % 4 * 2 + (spot["x"] + dx) % 2
    orders = []
    for dc in (1, 0):
        core = (spot["core"] + dc) % 2
        orders.append(((chip * 2 + core) * 2 + (spot["y"] + dy) % 2).astype(jnp.int32))
    return orders


def chunk_orders():
    spot = my_spot()
    dz, dx = (grid.reshape(-1) for grid in np.indices((4, 2)).astype(np.int32))
    chip = (spot["z"] - dz + 4) % 4 * 2 + (spot["x"] + dx) % 2
    return [(chip * 2 + (spot["core"] + dc) % 2).astype(jnp.int32) for dc in (1, 0)]


TOKEN_ORDERS = (("x", "y", "z"), ("y", "z", "x"), ("z", "x", "y"))
CHUNK_ORDERS = (("x", "z"), ("z", "x"))


def tokens_home(lattice, partner, own):
    groups = []
    for first, second, order in zip(partner, own, TOKEN_ORDERS):
        if lattice:
            shape = (4, 2, 2) + first.shape[1:]
            groups.append(
                reduce_home(first.reshape(shape), second.reshape(shape), ("z", "x", "y"), order)
            )
        else:
            everything = jnp.concatenate([first, second], axis=0)
            total = lax.psum_scatter(everything, BOTH, scatter_dimension=0, tiled=True)
            groups.append(total[0].astype(F32))
    return groups


def weight_grads_home(lattice, left, right, widths):
    if not lattice:
        product = dot(left, right, 0, 0).astype(BF16)
        return lax.psum_scatter(product, "dp", scatter_dimension=0, tiled=True).astype(F32)
    partner, own = (chunk_products(order, left, right, widths) for order in chunk_orders())
    groups = []
    for first, second, order in zip(partner, own, CHUNK_ORDERS):
        shape = (4, 2) + first.shape[1:]
        groups.append(reduce_home(first.reshape(shape), second.reshape(shape), ("z", "x"), order))
    return jnp.concatenate(groups, axis=1)


def on_device(
    inputs,
    input_gain,
    post_gain,
    query_gain,
    key_gain,
    query_weight,
    key_projection_matrix,
    value_projection_matrix,
    output_weight,
    router_weight,
    gate_weight,
    up_weight,
    down_weight,
    routes,
    cotangent,
):
    dp_count, tensor_count = lax.axis_size("dp"), lax.axis_size("tensor")
    device_count = dp_count * tensor_count
    lattice = is_lattice(dp_count, tensor_count)
    row_count, width = inputs.shape
    experts = router_weight.shape[1]
    experts_here = gate_weight.shape[0]
    capacity = 2 * row_count * routes.shape[1] // experts

    projections = jnp.concatenate(
        [query_weight, key_projection_matrix, value_projection_matrix], axis=0
    )
    query_rows, key_rows = query_weight.shape[0], key_projection_matrix.shape[0]
    projections_full = lax.all_gather(projections, "dp", axis=1, tiled=True)
    output_held, _ = lax.optimization_barrier((output_weight, projections_full[:8, :128]))
    output_full = lax.all_gather(output_held, "dp", axis=0, tiled=True)
    cotangent_held, _ = lax.optimization_barrier((cotangent, output_full[:8, :128]))
    all_grads = lax.all_gather(cotangent_held[None], BOTH, axis=0, tiled=True)
    other_inputs = swap_tensor(inputs)

    expert_ids = jnp.arange(experts, dtype=jnp.int32)
    chosen_mask = jnp.any(routes[:, :, None] == expert_ids[None, None, :], axis=1)
    small = [input_gain, post_gain, query_gain, key_gain]
    sizes = [item.shape[0] for item in small]
    flat = jnp.concatenate(small)
    padded = -(-flat.shape[0] // LANES) * LANES
    flat = jnp.pad(flat, (0, padded - flat.shape[0]))
    router_lines = router_weight.size // LANES
    payload = jnp.concatenate(
        [
            router_weight.reshape(router_lines, LANES),
            flat.reshape(-1, LANES),
            chosen_mask.T.astype(BF16),
        ],
        axis=0,
    )
    gathered = lax.all_gather(payload[None], BOTH, axis=0, tiled=True)
    router_full = gathered[:, :router_lines].reshape(width, experts)
    flat_all = gathered[:, router_lines : router_lines + padded // LANES].reshape(
        device_count, padded
    )
    starts = np.cumsum([0] + sizes)
    input_scale, post_scale, query_scale, key_scale = (
        flat_all[:, starts[n] : starts[n + 1]].reshape(-1).astype(F32) for n in range(4)
    )
    mask_all = gathered[:, router_lines + padded // LANES :]
    first_expert = lax.axis_index("dp") * experts_here
    mask_here = lax.dynamic_slice_in_dim(mask_all, first_expert, experts_here, axis=1)
    earlier = jnp.asarray(np.triu(np.ones((row_count, row_count), np.float32), 1), BF16)
    rank = jnp.einsum("bet,tu->beu", mask_here, earlier, preferred_element_type=F32)
    position = jnp.where(mask_here > 0.5, rank, -1.0)
    orders = block_orders(lattice, device_count)
    positions = [position[order] for order in orders]
    masks = [mask_all[order] for order in orders]
    router_t = router_full.T
    up_both = jnp.concatenate([gate_weight, up_weight], axis=2)
    up_both_t = jnp.swapaxes(up_both, 1, 2)
    down_t = jnp.swapaxes(down_weight, 1, 2)

    both_inputs = in_order(inputs, other_inputs).astype(F32)
    residual_in = inputs.astype(F32)
    sequence = norm_rows(both_inputs, input_scale)[0].astype(BF16)
    _, input_hat, input_inv = norm_rows(residual_in, input_scale)
    seq_len = sequence.shape[0]
    local_heads = query_rows // HEAD_SIZE
    local_groups = key_rows // HEAD_SIZE
    per_group = local_heads // local_groups
    projected = dot(sequence, projections_full, 1, 1)
    query_raw = projected[:, :query_rows].reshape(seq_len, local_heads, HEAD_SIZE)
    key_raw = projected[:, query_rows : query_rows + key_rows].reshape(
        seq_len, local_groups, HEAD_SIZE
    )
    value_low = (
        projected[:, query_rows + key_rows :]
        .astype(BF16)
        .reshape(seq_len, local_groups, HEAD_SIZE)
    )
    cosine_table, sine_table = rope_tables(seq_len, HEAD_SIZE)
    cosine, sine = cosine_table[:, None, :], sine_table[:, None, :]
    query_norm, query_hat, query_inv = norm_rows(query_raw, query_scale)
    query_low = (query_norm * cosine + rotate_half(query_norm) * sine).astype(BF16)
    key_norm, key_hat, key_inv = norm_rows(key_raw, key_scale)
    key_low = (key_norm * cosine + rotate_half(key_norm) * sine).astype(BF16)
    score_scale = 1.0 / math.sqrt(HEAD_SIZE)
    query_groups = query_low.reshape(seq_len, local_groups, per_group, HEAD_SIZE)
    scores = (
        jnp.einsum("qhgd,khd->hgqk", query_groups, key_low, preferred_element_type=F32)
        * score_scale
    )
    row_index = jnp.arange(seq_len, dtype=jnp.int32)
    scores = jnp.where(row_index[None, :] <= row_index[:, None], scores, -1e30)
    attend = jax.nn.softmax(scores, axis=-1)
    attend_low = attend.astype(BF16)
    mixed_low = (
        jnp.einsum("hgqk,khd->qhgd", attend_low, value_low, preferred_element_type=F32)
        .astype(BF16)
        .reshape(seq_len, query_rows)
    )
    residual_mid = residual_in + sum_tokens(dot(mixed_low, output_full, 1, 1))
    post_norm, post_hat, post_inv = norm_rows(residual_mid, post_scale)
    post_low = post_norm.astype(BF16)
    all_tokens = lax.all_gather(post_low[None], BOTH, axis=0, tiled=True)

    logits = dot(post_low, router_full)
    top = jnp.max(jnp.where(chosen_mask, logits, -3e38), axis=-1, keepdims=True)
    powers = jnp.where(chosen_mask, jnp.exp(jnp.minimum(logits - top, 0.0)), 0.0)
    gates = powers / jnp.sum(powers, axis=-1, keepdims=True)

    wide = width // 8 * 3
    widths = (wide, wide, width - 2 * wide + LANES)
    first_scalar = first_expert.astype(jnp.int32).reshape(1)
    results = [
        expert_grads(
            order, first_scalar, all_tokens, all_grads, positions[n], masks[n],
            router_t, up_both, up_both_t, down_t, capacity, widths,
        )
        for n, order in enumerate(orders)
    ]
    home = tokens_home(lattice, results[0][5:], results[1][5:])
    out_widths = (wide, wide, width - 2 * wide)
    outputs = [
        expert_outputs(results[n][2], positions[n], down_weight, capacity, out_widths)
        for n in range(2)
    ]
    rows, grad_rows, gated, grad_gate_pre, grad_up_pre = (
        [results[n][place] for n in range(2)] for place in range(5)
    )

    def slot_product(left, right):
        return sum(
            jnp.einsum("esd,esf->edf", left[n], right[n], preferred_element_type=F32)
            for n in range(2)
        )

    grad_down = slot_product(gated, grad_rows)
    grad_gate_w = slot_product(rows, grad_gate_pre)
    grad_up_w = slot_product(rows, grad_up_pre)
    out_home = jnp.concatenate(tokens_home(lattice, outputs[0], outputs[1]), axis=1)
    result = (residual_mid + out_home).astype(BF16)

    grad_out = cotangent.astype(F32)
    grad_post = jnp.concatenate([home[0], home[1], home[2][:, : width - 2 * wide]], axis=1)
    start = width - 2 * wide
    grad_gates = home[2][:, start : start + experts]
    grad_logits = (
        gates * (grad_gates - jnp.sum(gates * grad_gates, axis=-1, keepdims=True))
    ).astype(BF16)
    grad_post = grad_post + dot(grad_logits, router_full, 1, 1)
    grad_router = dot(post_low, grad_logits, 0, 0)
    grad_mid_norm, post_terms = norm_back(grad_post, post_scale, post_hat, post_inv)
    grad_post_gain = jnp.sum(post_terms, axis=0)
    grad_mid = grad_out + grad_mid_norm
    grad_mid_low = grad_mid.astype(BF16)
    grad_attention = in_order(grad_mid_low, swap_tensor(grad_mid_low))
    early = reduce_small(
        jnp.concatenate(
            [
                grad_router.reshape(device_count, -1),
                grad_post_gain.reshape(device_count, -1),
                jnp.zeros((device_count, LANES - sizes[1]), F32),
            ],
            axis=1,
        ).reshape(device_count, -1, LANES)
    ).reshape(-1)
    grad_router = early[: router_weight.size].reshape(router_weight.shape)
    grad_post_gain = early[router_weight.size : router_weight.size + sizes[1]]

    grad_mixed = dot(grad_attention, output_full).astype(BF16)
    out_split = (query_rows // 8 * 5, query_rows - query_rows // 8 * 5)
    grad_output_w = weight_grads_home(lattice, grad_attention, mixed_low, out_split)
    grad_groups = grad_mixed.reshape(seq_len, local_groups, per_group, HEAD_SIZE)
    grad_attend = jnp.einsum(
        "qhgd,khd->hgqk", grad_groups, value_low, preferred_element_type=F32
    )
    grad_value = jnp.einsum(
        "hgqk,qhgd->khd", attend_low, grad_groups, preferred_element_type=F32
    )
    row_inner = jnp.sum(attend * grad_attend, axis=-1, keepdims=True)
    grad_scores = (attend * (grad_attend - row_inner)).astype(BF16)
    grad_query_rot = (
        jnp.einsum("hgqk,khd->qhgd", grad_scores, key_low, preferred_element_type=F32)
        * score_scale
    ).reshape(seq_len, local_heads, HEAD_SIZE)
    grad_key_rot = (
        jnp.einsum("hgqk,qhgd->khd", grad_scores, query_groups, preferred_element_type=F32)
        * score_scale
    )
    grad_query_norm = grad_query_rot * cosine + rotate_back(grad_query_rot * sine)
    grad_query_raw, query_terms = norm_back(grad_query_norm, query_scale, query_hat, query_inv)
    grad_query_gain = jnp.sum(query_terms, axis=(0, 1))
    grad_key_norm = grad_key_rot * cosine + rotate_back(grad_key_rot * sine)
    grad_key_raw, key_terms = norm_back(grad_key_norm, key_scale, key_hat, key_inv)
    grad_key_gain = jnp.sum(key_terms, axis=(0, 1))
    grad_projected = jnp.concatenate(
        [
            grad_query_raw.reshape(seq_len, query_rows).astype(BF16),
            grad_key_raw.reshape(seq_len, key_rows).astype(BF16),
            grad_value.reshape(seq_len, key_rows).astype(BF16),
        ],
        axis=1,
    )
    total_rows = query_rows + 2 * key_rows
    split = total_rows // LANES * 3 // 5 * LANES
    grad_projections = weight_grads_home(
        lattice, sequence, grad_projected, (split, total_rows - split)
    ).T
    grad_query_w = grad_projections[:query_rows]
    grad_key_w = grad_projections[query_rows : query_rows + key_rows]
    grad_value_w = grad_projections[query_rows + key_rows :]
    grad_normed = sum_tokens(dot(grad_projected, projections_full))
    grad_in_norm, input_terms = norm_back(grad_normed, input_scale, input_hat, input_inv)
    grad_input_gain = jnp.sum(input_terms, axis=0)
    grad_inputs = (grad_mid + grad_in_norm).astype(BF16)
    late_parts = [grad_input_gain, grad_query_gain, grad_key_gain]
    late_sizes = [sizes[0], sizes[2], sizes[3]]
    late = reduce_small(
        jnp.concatenate(
            [part.reshape(device_count, -1) for part in late_parts]
            + [jnp.zeros((device_count, LANES - sum(late_sizes)), F32)],
            axis=1,
        ).reshape(device_count, 1, LANES)
    ).reshape(-1)
    bounds = np.cumsum([0] + late_sizes)
    grad_input_gain, grad_query_gain, grad_key_gain = (
        late[bounds[n] : bounds[n + 1]] for n in range(3)
    )
    return (
        result,
        grad_inputs,
        grad_input_gain,
        grad_post_gain,
        grad_query_gain,
        grad_key_gain,
        grad_query_w,
        grad_key_w,
        grad_value_w,
        grad_output_w,
        grad_router,
        grad_gate_w,
        grad_up_w,
        grad_down,
    )


def solution(mesh):
    return jax.shard_map(
        on_device,
        mesh=mesh,
        in_specs=(
            P(("dp", "tensor"), None),
            P(("dp", "tensor")),
            P(("dp", "tensor")),
            P(("dp", "tensor")),
            P(("dp", "tensor")),
            P("tensor", "dp"),
            P("tensor", "dp"),
            P("tensor", "dp"),
            P("dp", "tensor"),
            P(("dp", "tensor"), None),
            P("dp", None, "tensor"),
            P("dp", None, "tensor"),
            P("dp", "tensor", None),
            P(("dp", "tensor"), None),
            P(("dp", "tensor"), None),
        ),
        out_specs=(
            P(("dp", "tensor"), None),
            P(("dp", "tensor"), None),
            P(("dp", "tensor")),
            P(("dp", "tensor")),
            P(("dp", "tensor")),
            P(("dp", "tensor")),
            P("tensor", "dp"),
            P("tensor", "dp"),
            P("tensor", "dp"),
            P("dp", "tensor"),
            P(("dp", "tensor"), None),
            P("dp", None, "tensor"),
            P("dp", None, "tensor"),
            P("dp", "tensor", None),
        ),
        check_vma=False,
    )
```

time: 3150 us -> 1170 us (0.37)
  waiting for transfers between devices: 2150 us -> 489 us
  blocking collectives: 500 us -> 80.4 us
  Pallas kernels: 0 us -> 125 us
  matrix products: 214 us -> 107 us
  other arithmetic: 70.8 us -> 131 us
  starting transfers between devices: 49.5 us -> 99.9 us
  local copies, waits for them, and re-layouts: 144 us -> 112 us
    unnamed x22 -> x4, waiting for transfers between devices: 812 us -> 1.41 us
    reduce_scatter x6 -> x0, waiting for transfers between devices: 467 us -> none  [the longest x1 181 us: on_device(): lax.psum_scatter(grad_output_w, 'dp', scatter_dimension=0, tiled=True)]
    all_gather x12 -> x4, waiting for transfers between devices: 602 us -> 202 us  [the longest x1 116 us: on_device(): all_tokens = lax.all_gather(post_low[None], BOTH, axis=0, tiled=True)]
    ppermute x0 -> x70, waiting for transfers between devices: none -> 286 us  [the longest x56 239 us: hop(): return lax.ppermute(values, BOTH, pairs)]
    all_to_all x3 -> x0, waiting for transfers between devices: 273 us -> none  [move_rows(): return lax.all_to_all(rows, 'dp', split_axis=0, concat_axis=0, tiled=True)]
    all_to_all x1 -> x0, blocking collectives: 215 us -> none  [move_rows(): return lax.all_to_all(rows, 'dp', split_axis=0, concat_axis=0, tiled=True)]
    pallas_call x0 -> x8, Pallas kernels: none -> 125 us  [the longest x2 83 us: expert_grads(): call(perm, first, *[tokens] * STEP_BLOCKS, *[grads] * STEP_BLOCKS, positi...]
    all_gather x1, blocking collectives: 202 us -> 80.4 us  [on_device(): gathered = lax.all_gather(payload[None], BOTH, axis=0, tiled=True)]
  transfers between devices with their start and end apart: 23 -> 74, of which waited for: 21 -> 34; matrix products, arithmetic and copies ran while one was open for 9% -> 23% of each run, Pallas kernels for 0% -> 6%
where the time goes in v1:
time: 1170 us; the launch traced here: 1160 us
  waiting for transfers between devices  489 us (42%)
  other arithmetic  131 us (11%)
  Pallas kernels  125 us (11%)
  local copies, waits for them, and re-layouts  112 us (10%)
  matrix products  107 us (9%)
  starting transfers between devices  99.9 us (9%)
  blocking collectives  80.4 us (7%)
  between operations  16 us (1%)
    ppermute x56, waiting for transfers between devices, hop(): return lax.ppermute(values, BOTH, pairs)  239 us
    all_gather x1, waiting for transfers between devices, on_device(): all_tokens = lax.all_gather(post_low[None], BOTH, axis=0, tiled=True)  116 us
    ppermute x56, starting transfers between devices, hop(): return lax.ppermute(values, BOTH, pairs)  86.9 us
    pallas_call x2, Pallas kernels, expert_grads(): call(perm, first, *[tokens] * STEP_BLOCKS, *[grads] * STEP_BLOCKS, positi...  83 us
    all_gather x1, blocking collectives, on_device(): gathered = lax.all_gather(payload[None], BOTH, axis=0, tiled=True)  80.4 us
    dot_general x6, matrix products, slot_product(): jnp.einsum('esd,esf->edf', left[n], right[n], preferred_element_type=F32)  65.1 us
    convert_element_type x46, other arithmetic, add_low(): return (first.astype(F32) + second.astype(F32)).astype(BF16)  64 us
    all_gather x1, waiting for transfers between devices, on_device(): output_full = lax.all_gather(output_held, 'dp', axis=0, tiled=True)  44.3 us
  transfers between devices with their start and end apart: 74, of which 34 were waited for; matrix products, arithmetic and copies ran while one was open for 23% of the time, Pallas kernels for 6%

profile of v1, /device:TPU:0, one launch (start us, length us, event | category | flops | bytes accessed | tf_op | source)
XLA Modules:
  0.0 1160.3 jit_solution(4243087527418704494)
XLA Ops:
  14.4 80.4 %all-gather.3 = bf16[32,50,128]{2,1,0:T(8,128)(2,1)S(1)} all-gather(bf16[1,50,128]{2,1,0:T(8,128)(2,1)S(1)} %maximum_bitcast_fusion.1), channel_id=2, replica_groups=mesh['dp'=16,'tensor'=2] {'dp','tensor'}, dimensions={0}, use_global_device_ids=true | all-gather | bytes 422400 | tf_op jit(solution)/shard_map/all_gather | solution.py:488
  136.6 44.3 %all-gather.11.cloned.1.call-done = bf16[2048,2048]{1,0:T(8,128)(2,1)} async-done(((bf16[128,2048]{1,0:T(8,128)(2,1)}), bf16[2048,2048]{1,0:T(8,128)(2,1)}) %all-gather.11.cloned.1.call-update) | async-done | bytes 8388624 | tf_op jit(solution)/shard_map/all_gather | solution.py:467
  190.4 16.6 %collective-permute-done.1 = bf16[128,2048]{1,0:T(8,128)(2,1)} collective-permute-done((bf16[128,2048]{1,0:T(8,128)(2,1)}, bf16[128,2048]{1,0:T(8,128)(2,1)}, u32[]{:S(2)}, u32[]{:S(2)}) %collective-permute-start.1) | collective-permute-done | bytes 524320 | tf_op jit(solution)/shard_map/ppermute | solution.py:135
  230.1 9.8 fusion.184
  265.2 34.6 %all-gather.15.cloned.1.call-done = bf16[4096,2048]{1,0:T(8,128)(2,1)} async-done(((bf16[128,2048]{1,0:T(8,128)(2,1)}), bf16[4096,2048]{1,0:T(8,128)(2,1)}) %all-gather.15.cloned.1.call-update) | async-done | bytes 16777232 | tf_op jit(solution)/shard_map/all_gather | solution.py:469
  299.8 115.9 %all-gather.13.cloned.1.call-done = bf16[4096,2048]{1,0:T(8,128)(2,1)} async-done(((bf16[128,2048]{1,0:T(8,128)(2,1)}), bf16[4096,2048]{1,0:T(8,128)(2,1)}) %all-gather.13.cloned.1.call-update) | async-done | bytes 16777232 | tf_op jit(solution)/shard_map/all_gather | solution.py:553
  415.7 41.2 %expert_grads.3 = (bf16[2,1024,2048]{2,1,0:T(8,128)(2,1)}, bf16[2,1024,2048]{2,1,0:T(8,128)(2,1)}, bf16[2,1024,384]{2,1,0:T(8,128)(2,1)}, bf16[2,1024,384]{2,1,0...) custom-call(s32[16]{0:T(128)} %get-tuple-element.185.perm, ...), custom_call_target="tpu_custom_call" | custom-call | flops 25769803776 | bytes 50331648 | tf_op jit(solution)/shard_map/expert_grads/pallas_call | solution.py:297
  456.9 10.9 expert_outputs.3
  467.9 9.6 fusion.199
  492.9 41.8 %expert_grads.2 = (bf16[2,1024,2048]{2,1,0:T(8,128)(2,1)}, bf16[2,1024,2048]{2,1,0:T(8,128)(2,1)}, bf16[2,1024,384]{2,1,0:T(8,128)(2,1)}, bf16[2,1024,384]{2,1,0...) custom-call(s32[16]{0:T(128)} %get-tuple-element.189.perm, ...), custom_call_target="tpu_custom_call" | custom-call | flops 25769803776 | bytes 50331648 | tf_op jit(solution)/shard_map/expert_grads/pallas_call | solution.py:297
  534.7 11.8 %convolution_add_fusion = f32[2,384,2048]{2,1,0:T(8,128)} fusion(f32[2,384,2048]{2,1,0:T(8,128)} %fusion.199, bf16[2,1024,384]{2,1,0:T(8,128)(2,1)} %get-tuple-element.44.gated_ref, bf16[2,1024,2048]{2,1,0:T(8,128)(2,1)} %get-tuple-element.73), kind=kOutput, calls=%fused_computation.13 | convolution fusion | flops 3222798336 | bytes 22544384 | tf_op jit(solution)/shard_map/esd,esf->edf/dot_general | solution.py:582
  546.5 13.0 %convolution_add_fusion.1 = f32[2,2048,384]{2,1,0:T(8,128)} fusion(f32[2,2048,384]{2,1,0:T(8,128)} %fusion.198, bf16[2,1024,2048]{2,1,0:T(8,128)(2,1)} %get-tuple-element.68, bf16[2,1024,384]{2,1,0:T(8,128)(2,1)} %get-tuple-element.71), kind=kOutput, calls=%fused_computation.14 | convolution fusion | flops 3222798336 | bytes 22544384 | tf_op jit(solution)/shard_map/esd,esf->edf/dot_general | solution.py:582
  561.5 10.9 expert_outputs.2
  572.4 11.2 fusion.197
  588.6 10.9 collective-permute-done.15
  613.4 14.0 %collective-permute-done.16 = bf16[2,2,128,512]{3,2,1,0:T(8,128)(2,1)S(1)} collective-permute-done((bf16[2,2,128,512]{3,2,1,0:T(8,128)(2,1)S(1)}, bf16[2,2,128,512]{3,2,1,0:T(8,128)(2,1)S(1)}, u32[]{:S(2)}, u32[]{:S(2)}) %collective-permute-start.16) | collective-permute-done | bytes 524320 | tf_op jit(solution)/shard_map/ppermute | solution.py:76
  651.5 31.5 %collective-permute-done.18 = bf16[2,128,512]{2,1,0:T(8,128)(2,1)S(1)} collective-permute-done((bf16[2,128,512]{2,1,0:T(8,128)(2,1)S(1)}, bf16[2,128,512]{2,1,0:T(8,128)(2,1)S(1)}, u32[]{:S(2)}, u32[]{:S(2)}) %collective-permute-start.18) | collective-permute-done | bytes 262176 | tf_op jit(solution)/shard_map/ppermute | solution.py:76
  687.8 32.8 %collective-permute-done.19 = bf16[128,512]{1,0:T(8,128)(2,1)S(1)} collective-permute-done((bf16[128,512]{1,0:T(8,128)(2,1)S(1)}, bf16[128,512]{1,0:T(8,128)(2,1)S(1)}, u32[]{:S(2)}, u32[]{:S(2)}) %collective-permute-start.19) | collective-permute-done | bytes 131104 | tf_op jit(solution)/shard_map/ppermute | solution.py:76
  721.3 12.9 %convolution_add_fusion.2 = f32[2,2048,384]{2,1,0:T(8,128)} fusion(f32[2,2048,384]{2,1,0:T(8,128)} %fusion.197, bf16[2,1024,2048]{2,1,0:T(8,128)(2,1)} %get-tuple-element.68, bf16[2,1024,384]{2,1,0:T(8,128)(2,1)} %get-tuple-element.69), kind=kOutput, calls=%fused_computation.15 | convolution fusion | flops 3222798336 | bytes 22544384 | tf_op jit(solution)/shard_map/esd,esf->edf/dot_general | solution.py:582
  755.8 22.8 %collective-permute-done.37 = bf16[128,640]{1,0:T(8,128)(2,1)S(1)} collective-permute-done((bf16[128,640]{1,0:T(8,128)(2,1)S(1)}, bf16[128,640]{1,0:T(8,128)(2,1)S(1)}, u32[]{:S(2)}, u32[]{:S(2)}) %collective-permute-start.37) | collective-permute-done | bytes 163872 | tf_op jit(solution)/shard_map/ppermute | solution.py:76
  817.9 15.4 %collective-permute-done.24 = bf16[128,768]{1,0:T(8,128)(2,1)S(1)} collective-permute-done((bf16[128,768]{1,0:T(8,128)(2,1)S(1)}, bf16[128,768]{1,0:T(8,128)(2,1)S(1)}, u32[]{:S(2)}, u32[]{:S(2)}) %collective-permute-start.24) | collective-permute-done | bytes 196640 | tf_op jit(solution)/shard_map/ppermute | solution.py:76
  874.4 10.7 collective-permute-done.49
  1045.9 9.7 collective-permute-done.57
  1062.5 38.2 %collective-permute-done.69 = bf16[128,768]{1,0:T(8,128)(2,1)S(1)} collective-permute-done((bf16[128,768]{1,0:T(8,128)(2,1)S(1)}, bf16[128,768]{1,0:T(8,128)(2,1)S(1)}, u32[]{:S(2)}, u32[]{:S(2)}) %collective-permute-start.69) | collective-permute-done | bytes 196640 | tf_op jit(solution)/shard_map/ppermute | solution.py:76
  (614 shorter events, 493.2 us)
Async XLA Ops:
  7.3 98.6 %all-gather.9.cloned.1.call-start = ((), (), s32[]{:S(2)}) async-start(), calls=%async_computation | async-start | bytes 11141120 | tf_op jit(solution)/shard_map/all_gather | solution.py:465
  9.4 171.5 %all-gather.11.cloned.1.call-start = ((), (), s32[]{:S(2)}) async-start(), calls=%async_computation.1 | async-start | bytes 8912896 | tf_op jit(solution)/shard_map/all_gather | solution.py:467
  10.2 289.6 %all-gather.15.cloned.1.call-start = ((), (), s32[]{:S(2)}) async-start(), calls=%async_computation.3 | async-start | bytes 17301504 | tf_op jit(solution)/shard_map/all_gather | solution.py:469
  10.9 404.8 %all-gather.13.cloned.1.call-start = ((), (), s32[]{:S(2)}) async-start(), calls=%async_computation.2 | async-start | bytes 17301504 | tf_op jit(solution)/shard_map/all_gather | solution.py:553
  11.0 86.9 %collective-permute-start = (bf16[128,2048]{1,0:T(8,128)(2,1)S(1)}, bf16[128,2048]{1,0:T(8,128)(2,1)S(1)}, u32[]{:S(2)}, u32[]{:S(2)}) collective-permute-start(bf16[128,2048]{1,0:T(8,128)(2,1)S(1)} %copy-done.11), channel_id=1, source_target_pairs={{0,1},{1,0},{2,3},{3,2},{4,5},{5,4},{6,7},{7,6},{8,9},{9,8},{10,11... | collective-permute-start | bytes 1572872 | tf_op jit(solution)/shard_map/ppermute | solution.py:135
  477.5 107.7 %collective-permute-start.32 = (bf16[4,2,2,128,640]{4,3,2,1,0:T(8,128)(2,1)}, bf16[4,2,2,128,640]{4,3,2,1,0:T(8,128)(2,1)}, u32[]{:S(2)}, u32[]{:S(2)}) collective-permute-start(bf16[4,2,2,128,640]{4,3,2,1,0:T(8,128)(2,1)} %bitcast.91), channel_id=1, source_target_pairs={{0,2},{1,3},{2,0},{3,1},{4,6},{5,7},{6,4},{7,5},{8,10},{9,11},{10,... | collective-permute-start | bytes 7864328 | tf_op jit(solution)/shard_map/ppermute | solution.py:76
  479.7 124.2 %collective-permute-start.20 = (bf16[4,2,2,128,768]{4,3,2,0,1:T(8,128)(2,1)}, bf16[4,2,2,128,768]{4,3,2,0,1:T(8,128)(2,1)}, u32[]{:S(2)}, u32[]{:S(2)}) collective-permute-start(bf16[4,2,2,128,768]{4,3,2,0,1:T(8,128)(2,1)} %copy.521), channel_id=1, source_target_pairs={{0,2},{1,3},{2,0},{3,1},{4,6},{5,7},{6,4},{7,5},{8,10},{9,11},{10,... | collective-permute-start | bytes 9437192 | tf_op jit(solution)/shard_map/ppermute | solution.py:76
  481.2 127.0 %collective-permute-start.26 = (bf16[4,2,2,128,768]{4,3,1,2,0:T(8,128)(2,1)S(1)}, bf16[4,2,2,128,768]{4,3,1,2,0:T(8,128)(2,1)}, u32[]{:S(2)}, u32[]{:S(2)}) collective-permute-start(bf16[4,2,2,128,768]{4,3,1,2,0:T(8,128)(2,1)S(1)} %copy.524), channel_id=1, source_target_pairs={{0,2},{1,3},{2,0},{3,1},{4,6},{5,7},{6,4},{7,5},{8,10},{9,11},{10,... | collective-permute-start | bytes 9437192 | tf_op jit(solution)/shard_map/ppermute | solution.py:76
  484.7 145.9 %collective-permute-start.2 = (bf16[4,2,2,128,768]{4,3,2,0,1:T(8,128)(2,1)}, bf16[4,2,2,128,768]{4,3,2,0,1:T(8,128)(2,1)}, u32[]{:S(2)}, u32[]{:S(2)}) collective-permute-start(bf16[4,2,2,128,768]{4,3,2,0,1:T(8,128)(2,1)} %copy.515), channel_id=1, source_target_pairs={{0,2},{1,3},{2,0},{3,1},{4,6},{5,7},{6,4},{7,5},{8,10},{9,11},{10,... | collective-permute-start | bytes 9437192 | tf_op jit(solution)/shard_map/ppermute | solution.py:76
  484.9 98.7 %collective-permute-start.14 = (bf16[4,2,2,128,512]{4,3,2,1,0:T(8,128)(2,1)}, bf16[4,2,2,128,512]{4,3,2,1,0:T(8,128)(2,1)}, u32[]{:S(2)}, u32[]{:S(2)}) collective-permute-start(bf16[4,2,2,128,512]{4,3,2,1,0:T(8,128)(2,1)} %bitcast.50), channel_id=1, source_target_pairs={{0,2},{1,3},{2,0},{3,1},{4,6},{5,7},{6,4},{7,5},{8,10},{9,11},{10,... | collective-permute-start | bytes 6291464 | tf_op jit(solution)/shard_map/ppermute | solution.py:76
  583.6 65.4 %collective-permute-start.8 = (bf16[4,2,2,128,768]{4,3,1,2,0:T(8,128)(2,1)}, bf16[4,2,2,128,768]{4,3,1,2,0:T(8,128)(2,1)S(1)}, u32[]{:S(2)}, u32[]{:S(2)}) collective-permute-start(bf16[4,2,2,128,768]{4,3,1,2,0:T(8,128)(2,1)} %copy.518), channel_id=1, source_target_pairs={{0,2},{1,3},{2,0},{3,1},{4,6},{5,7},{6,4},{7,5},{8,10},{9,11},{10,... | collective-permute-start | bytes 9437192 | tf_op jit(solution)/shard_map/ppermute | solution.py:76
  608.2 130.7 %collective-permute-start.21 = (bf16[4,2,128,768]{3,2,1,0:T(8,128)(2,1)}, bf16[4,2,128,768]{3,2,1,0:T(8,128)(2,1)}, u32[]{:S(2)}, u32[]{:S(2)}) collective-permute-start(bf16[4,2,128,768]{3,2,1,0:T(8,128)(2,1)} %get-tuple-element.193), channel_id=1, source_target_pairs={{0,4},{1,5},{2,6},{3,7},{4,0},{5,1},{6,2},{7,3},{8,12},{9,13},{10,... | collective-permute-start | bytes 4718600 | tf_op jit(solution)/shard_map/ppermute | solution.py:76
  627.4 114.9 %collective-permute-start.27 = (bf16[4,2,128,768]{3,2,1,0:T(8,128)(2,1)}, bf16[4,2,128,768]{3,2,1,0:T(8,128)(2,1)}, u32[]{:S(2)}, u32[]{:S(2)}) collective-permute-start(bf16[4,2,128,768]{3,2,1,0:T(8,128)(2,1)} %get-tuple-element.195), channel_id=1, source_target_pairs={{0,1},{1,0},{2,3},{3,2},{4,5},{5,4},{6,7},{7,6},{8,9},{9,8},{10,11... | collective-permute-start | bytes 4718600 | tf_op jit(solution)/shard_map/ppermute | solution.py:76
  638.9 107.9 %collective-permute-start.3 = (bf16[4,2,128,768]{3,2,1,0:T(8,128)(2,1)}, bf16[4,2,128,768]{3,2,1,0:T(8,128)(2,1)}, u32[]{:S(2)}, u32[]{:S(2)}) collective-permute-start(bf16[4,2,128,768]{3,2,1,0:T(8,128)(2,1)} %get-tuple-element.197), channel_id=1, source_target_pairs={{0,4},{1,5},{2,6},{3,7},{4,0},{5,1},{6,2},{7,3},{8,12},{9,13},{10,... | collective-permute-start | bytes 4718600 | tf_op jit(solution)/shard_map/ppermute | solution.py:76
  683.1 69.0 %collective-permute-start.9 = (bf16[4,2,128,768]{3,2,1,0:T(8,128)(2,1)}, bf16[4,2,128,768]{3,2,1,0:T(8,128)(2,1)}, u32[]{:S(2)}, u32[]{:S(2)}) collective-permute-start(bf16[4,2,128,768]{3,2,1,0:T(8,128)(2,1)} %get-tuple-element.199), channel_id=1, source_target_pairs={{0,1},{1,0},{2,3},{3,2},{4,5},{5,4},{6,7},{7,6},{8,9},{9,8},{10,11... | collective-permute-start | bytes 4718600 | tf_op jit(solution)/shard_map/ppermute | solution.py:76
  741.8 47.3 %collective-permute-start.22 = (bf16[4,128,768]{2,1,0:T(8,128)(2,1)}, bf16[4,128,768]{2,1,0:T(8,128)(2,1)}, u32[]{:S(2)}, u32[]{:S(2)}) collective-permute-start(bf16[4,128,768]{2,1,0:T(8,128)(2,1)} %get-tuple-element.213), channel_id=1, source_target_pairs={{0,1},{1,0},{2,3},{3,2},{4,5},{5,4},{6,7},{7,6},{8,9},{9,8},{10,11... | collective-permute-start | bytes 2359304 | tf_op jit(solution)/shard_map/ppermute | solution.py:76
  749.8 41.2 %collective-permute-start.4 = (bf16[4,128,768]{2,1,0:T(8,128)(2,1)}, bf16[4,128,768]{2,1,0:T(8,128)(2,1)}, u32[]{:S(2)}, u32[]{:S(2)}) collective-permute-start(bf16[4,128,768]{2,1,0:T(8,128)(2,1)} %get-tuple-element.217), channel_id=1, source_target_pairs={{0,1},{1,0},{2,3},{3,2},{4,5},{5,4},{6,7},{7,6},{8,9},{9,8},{10,11... | collective-permute-start | bytes 2359304 | tf_op jit(solution)/shard_map/ppermute | solution.py:76
  797.3 44.1 %collective-permute-start.30 = (bf16[2,128,768]{2,1,0:T(8,128)(2,1)S(1)}, bf16[2,128,768]{2,1,0:T(8,128)(2,1)S(1)}, u32[]{:S(2)}, u32[]{:S(2)}) collective-permute-start(bf16[2,128,768]{2,1,0:T(8,128)(2,1)S(1)} %fusion.65), channel_id=1, source_target_pairs={{0,24},{1,25},{2,26},{3,27},{4,28},{5,29},{6,30},{7,31},{8,0},{9,1... | collective-permute-start | bytes 1179656 | tf_op jit(solution)/shard_map/ppermute | solution.py:76
  806.5 46.2 %collective-permute-start.12 = (bf16[2,128,768]{2,1,0:T(8,128)(2,1)}, bf16[2,128,768]{2,1,0:T(8,128)(2,1)}, u32[]{:S(2)}, u32[]{:S(2)}) collective-permute-start(bf16[2,128,768]{2,1,0:T(8,128)(2,1)} %fusion.71), channel_id=1, source_target_pairs={{0,24},{1,25},{2,26},{3,27},{4,28},{5,29},{6,30},{7,31},{8,0},{9,1... | collective-permute-start | bytes 1179656 | tf_op jit(solution)/shard_map/ppermute | solution.py:76
  975.6 56.7 %collective-permute-start.60 = (bf16[4,2,128,1280]{3,2,1,0:T(8,128)(2,1)}, bf16[4,2,128,1280]{3,2,1,0:T(8,128)(2,1)}, u32[]{:S(2)}, u32[]{:S(2)}) collective-permute-start(bf16[4,2,128,1280]{3,2,1,0:T(8,128)(2,1)} %bitcast.764), channel_id=1, source_target_pairs={{0,2},{1,3},{2,0},{3,1},{4,6},{5,7},{6,4},{7,5},{8,10},{9,11},{10,... | collective-permute-start | bytes 7864328 | tf_op jit(solution)/shard_map/ppermute | solution.py:76
  991.0 51.5 %collective-permute-start.50 = (bf16[4,2,128,1536]{2,3,1,0:T(8,128)(2,1)}, bf16[4,2,128,1536]{2,3,1,0:T(8,128)(2,1)S(1)}, u32[]{:S(2)}, u32[]{:S(2)}) collective-permute-start(bf16[4,2,128,1536]{2,3,1,0:T(8,128)(2,1)} %copy.547), channel_id=1, source_target_pairs={{0,2},{1,3},{2,0},{3,1},{4,6},{5,7},{6,4},{7,5},{8,10},{9,11},{10,... | collective-permute-start | bytes 9437192 | tf_op jit(solution)/shard_map/ppermute | solution.py:76
  1034.8 68.2 %collective-permute-start.61 = (bf16[4,128,1280]{2,1,0:T(8,128)(2,1)S(1)}, bf16[4,128,1280]{2,1,0:T(8,128)(2,1)S(1)}, u32[]{:S(2)}, u32[]{:S(2)}) collective-permute-start(bf16[4,128,1280]{2,1,0:T(8,128)(2,1)S(1)} %get-tuple-element.203), channel_id=1, source_target_pairs={{0,4},{1,5},{2,6},{3,7},{4,0},{5,1},{6,2},{7,3},{8,12},{9,13},{10,... | collective-permute-start | bytes 3932168 | tf_op jit(solution)/shard_map/ppermute | solution.py:76
  1044.4 65.7 %collective-permute-start.51 = (bf16[4,128,1536]{1,2,0:T(8,128)(2,1)}, bf16[4,128,1536]{1,2,0:T(8,128)(2,1)}, u32[]{:S(2)}, u32[]{:S(2)}) collective-permute-start(bf16[4,128,1536]{1,2,0:T(8,128)(2,1)} %get-tuple-element.209), channel_id=1, source_target_pairs={{0,4},{1,5},{2,6},{3,7},{4,0},{5,1},{6,2},{7,3},{8,12},{9,13},{10,... | collective-permute-start | bytes 4718600 | tf_op jit(solution)/shard_map/ppermute | solution.py:76
  1056.1 45.4 %collective-permute-start.58 = (bf16[2,128,1024]{2,1,0:T(8,128)(2,1)S(1)}, bf16[2,128,1024]{2,1,0:T(8,128)(2,1)S(1)}, u32[]{:S(2)}, u32[]{:S(2)}) collective-permute-start(bf16[2,128,1024]{2,1,0:T(8,128)(2,1)S(1)} %get-tuple-element.205), channel_id=1, source_target_pairs={{0,24},{1,25},{2,26},{3,27},{4,28},{5,29},{6,30},{7,31},{8,0},{9,1... | collective-permute-start | bytes 1572872 | tf_op jit(solution)/shard_map/ppermute | solution.py:76
  (170 other events, 2760.9 us)
Sparse Core Ops, SparseCore 0:
  10.8 95.0 all-gather.8
  108.1 72.8 all-gather.10
  183.8 115.8 all-gather.14
  303.1 112.5 all-gather.12

commit v2 on v1

v2 whole, which is shorter than its diff:
```python
import functools
import math

import jax
import jax.numpy as jnp
import numpy as np
from jax import lax
from jax.experimental import pallas as pl
from jax.experimental.pallas import tpu as pltpu
from jax.sharding import PartitionSpec as P

HEAD_SIZE = 128
LANES = 128
EPSILON = 1e-06
ROPE_BASE = 1000000.0
DP = ("chip", "core")
BOTH = ("chip", "core", "tensor")
BF16 = jnp.bfloat16
F32 = jnp.float32
STEP_BLOCKS = 4
VMEM_BYTES = 60 * 1024 * 1024


def norm_rows(values, weights):
    inverse = lax.rsqrt(jnp.mean(values * values, axis=-1, keepdims=True) + EPSILON)
    normalized_rows = values * inverse
    return (normalized_rows * weights, normalized_rows, inverse)


def norm_back(upstream, weights, normalized_rows, inverse):
    scaled = upstream * weights
    inner_term = jnp.mean(scaled * normalized_rows, axis=-1, keepdims=True)
    return (inverse * (scaled - normalized_rows * inner_term), upstream * normalized_rows)


def rope_tables(length, head_width):
    half_width = head_width // 2
    frequency = jnp.exp(
        jnp.arange(half_width, dtype=F32) * (-2.0 * math.log(ROPE_BASE) / head_width)
    )
    angles = jnp.arange(length, dtype=F32)[:, None] * frequency[None, :]
    angles = jnp.concatenate([angles, angles], axis=-1)
    return (jnp.cos(angles), jnp.sin(angles))


def rotate_half(values):
    half_width = values.shape[-1] // 2
    return jnp.concatenate([-values[..., half_width:], values[..., :half_width]], axis=-1)


def rotate_back(values):
    half_width = values.shape[-1] // 2
    return jnp.concatenate([values[..., half_width:], -values[..., :half_width]], axis=-1)


def dot(left, right, left_dim=1, right_dim=0):
    return lax.dot_general(
        left, right, (((left_dim,), (right_dim,)), ((), ())), preferred_element_type=F32
    )


LATTICE = {"z": 4, "x": 2, "core": 2, "y": 2}


def is_lattice(dp_count, tensor_count):
    return dp_count == 16 and tensor_count == 2


def hop(values, axis, step=1):
    sizes = tuple(LATTICE.values())
    place = list(LATTICE).index(axis)
    pairs = []
    for source in range(math.prod(sizes)):
        spot = list(np.unravel_index(source, sizes))
        spot[place] = (spot[place] + step) % sizes[place]
        pairs.append((source, int(np.ravel_multi_index(spot, sizes))))
    return lax.ppermute(values, BOTH, pairs)


def my_spot():
    chip_core = lax.axis_index(DP)
    return {
        "z": chip_core // 4,
        "x": (chip_core // 2) % 2,
        "core": chip_core % 2,
        "y": lax.axis_index("tensor"),
    }


def add_low(first, second):
    return (first.astype(F32) + second.astype(F32)).astype(BF16)


class Pending:
    def __init__(self, *parts):
        self.parts = parts

    def total(self):
        return sum(part.astype(F32) for part in self.parts)

    def piece(self, place, dim):
        picked = [lax.index_in_dim(part, place, dim, keepdims=False) for part in self.parts]
        return Pending(*picked).total().astype(BF16)


def after(values, others):
    return lax.optimization_barrier((values, others))[0]


class Links:
    def __init__(self):
        self.active = []

    def add(self, *jobs):
        places = [[None] for _ in jobs]
        for job, place in zip(jobs, places):
            self.advance(job, place, None)
        return places

    def advance(self, job, place, arrived):
        try:
            self.active.append((job, place, job.send(arrived)))
        except StopIteration as stop:
            place[0] = stop.value

    def round(self, work=None, *operands):
        sending, self.active = self.active, []
        sent = [array for _, _, sends in sending for array, _ in sends]
        result = None
        if sent:
            sent = list(lax.optimization_barrier(tuple(sent)))
        moves = [move for _, _, sends in sending for _, move in sends]
        arrived = [move(array) for move, array in zip(moves, sent)]
        if work is not None:
            result = work(*(after(operands, sent) if sent else operands))
            arrived, result = lax.optimization_barrier((arrived, result))
        for job, place, sends in sending:
            self.advance(job, place, arrived[: len(sends)])
            arrived = arrived[len(sends) :]
        return result

    def finish(self):
        while self.active:
            self.round()


def mover(axis, step=1):
    return lambda values: hop(values, axis, step)


def home_job(partner, own, axes, order, turn):
    axes = list(axes)
    if partner is None:
        pending = own
    else:
        (received,) = yield [(partner, mover("core"))]
        pending = Pending(own, received)
    for axis in order:
        dim = axes.index(axis)
        axes.remove(axis)
        if axis == "z":
            (received,) = yield [(pending.piece(2, dim), mover("z", turn))]
            near = {-1: pending.piece(1, dim), 1: pending.piece(3, dim)}
            near[turn] = add_low(near[turn], received)
            arrived = yield [(near[step], mover("z", step)) for step in (-1, 1)]
        else:
            arrived = yield [(pending.piece(1, dim), mover(axis))]
        pending = Pending(pending.piece(0, dim), *arrived)
    return pending.total()


def spread_job(own, order, turn):
    pieces = own[None, None, None]
    for axis in order:
        dim = ("z", "x", "y").index(axis)
        if axis == "z":
            near = yield [(pieces, mover("z", 1)), (pieces, mover("z", -1))]
            (far,) = yield [(near[0 if turn == 1 else 1], mover("z", turn))]
            pieces = jnp.concatenate([pieces, near[0], far, near[1]], axis=dim)
        else:
            (other,) = yield [(pieces, mover(axis))]
            pieces = jnp.concatenate([pieces, other], axis=dim)
    flat = pieces.reshape((-1,) + own.shape)
    (partner,) = yield [(flat, mover("core"))]
    return partner, flat


def flip(bits):
    count = lax.axis_size(BOTH)
    return lambda values: lax.ppermute(
        values, BOTH, [(source, source ^ bits) for source in range(count)]
    )


def gather_small_job(values):
    device_count = lax.axis_size(BOTH)
    number = lax.axis_index(BOTH)
    everything = jnp.zeros((device_count,) + values.shape, values.dtype)
    everything = lax.dynamic_update_index_in_dim(everything, values, number, 0)
    bit = 1
    while bit < device_count:
        fan = min(4, device_count // bit)
        start = number // bit * bit
        sent = lax.dynamic_slice_in_dim(everything, start, bit, 0)
        arrived = yield [(sent, flip(k * bit)) for k in range(1, fan)]
        for k, received in enumerate(arrived, 1):
            everything = lax.dynamic_update_slice_in_dim(
                everything, received, start ^ (k * bit), 0
            )
        bit *= fan
    return everything


def reduce_small_job(values):
    number = lax.axis_index(BOTH)
    count = values.shape[0]
    while count > 1:
        fan = min(4, count)
        bit = count // fan
        parts = values.reshape((fan, bit) + values.shape[1:])
        mine = (number // bit) % fan
        pick = lambda place: lax.dynamic_index_in_dim(parts, place, 0, keepdims=False)
        arrived = yield [(pick(mine ^ k), flip(k * bit)) for k in range(1, fan)]
        values = sum(arrived, pick(mine))
        count = bit
    return values[0]


def swap_tensor(values):
    return lax.ppermute(values, "tensor", [(0, 1), (1, 0)])


def swap_job(values):
    (received,) = yield [(values, swap_tensor)]
    return received


def in_order(mine, other):
    first = lax.axis_index("tensor") == 0
    return jnp.where(
        first, jnp.concatenate([mine, other], axis=0), jnp.concatenate([other, mine], axis=0)
    )


def sum_tokens_job(terms):
    low = terms.astype(BF16).reshape((2, terms.shape[0] // 2) + terms.shape[1:])
    half = lax.axis_index("tensor")
    sent = lax.dynamic_index_in_dim(low, 1 - half, 0, keepdims=False)
    kept = lax.dynamic_index_in_dim(low, half, 0, keepdims=False)
    (received,) = yield [(sent, swap_tensor)]
    return kept.astype(F32) + received.astype(F32)


def choose(position_row, capacity):
    slot = lax.broadcasted_iota(jnp.int32, (capacity, position_row.shape[1]), 0).astype(F32)
    picks = [
        (slot == position_row[e : e + 1, :]).astype(F32) for e in range(position_row.shape[0])
    ]
    return picks


def expert_kernel(capacity, widths, grad_groups, carried, perm, first, *refs):
    blocks = STEP_BLOCKS
    token_refs, grad_refs, refs = (
        refs[:blocks],
        refs[blocks : blocks + grad_groups],
        refs[blocks + grad_groups :],
    )
    position_ref, mask_ref, router_ref, up_ref, up_t_ref, down_t_ref = refs[:6]
    refs = refs[6 + carried :]
    rows_ref, grad_rows_ref, gated_ref, grad_gate_ref, grad_up_ref = refs[:5]
    out_refs, packed_ref = refs[5:-1], refs[-1]
    experts_here = up_ref.shape[0]
    hidden_units = down_t_ref.shape[2]
    width = token_refs[0].shape[2]
    first_expert = first[0]
    gates = [[] for _ in range(experts_here)]
    choices = []
    for j in range(blocks):
        tokens = token_refs[j][0]
        picks = choose(position_ref[j], capacity)
        choice = jnp.concatenate(picks, axis=0).astype(BF16)
        choices.append(choice)
        rows = dot(choice, tokens).astype(BF16)
        grad_rows = [dot(choice, grad_ref[j]).astype(BF16) for grad_ref in grad_refs]
        logits = dot(router_ref[...], tokens, 1, 1)
        chosen = mask_ref[j].astype(F32) > 0.5
        top = jnp.max(jnp.where(chosen, logits, -3e38), axis=0, keepdims=True)
        powers = jnp.where(chosen, jnp.exp(jnp.minimum(logits - top, 0.0)), 0.0)
        gate_all = powers / jnp.sum(powers, axis=0, keepdims=True)
        expert_number = lax.broadcasted_iota(jnp.int32, gate_all.shape, 0)
        for e in range(experts_here):
            here = slice(j * capacity, (j + 1) * capacity)
            rows_ref[e, here, :] = rows[e * capacity : (e + 1) * capacity]
            start = 0
            for group in grad_rows:
                grad_rows_ref[e, here, start : start + group.shape[1]] = group[
                    e * capacity : (e + 1) * capacity
                ]
                start += group.shape[1]
            gate_row = jnp.sum(
                jnp.where(expert_number == first_expert + e, gate_all, 0.0), axis=0, keepdims=True
            )
            gates[e].append(jnp.sum(picks[e] * gate_row, axis=1, keepdims=True))
    for e in range(experts_here):
        both = dot(rows_ref[e], up_ref[e])
        gate_pre = both[:, :hidden_units]
        up_pre = both[:, hidden_units:]
        raw = dot(grad_rows_ref[e], down_t_ref[e])
        sigmoid = 1.0 / (1.0 + jnp.exp(-gate_pre))
        silu = gate_pre * sigmoid
        hidden = silu * up_pre
        gate = jnp.concatenate(gates[e], axis=0)
        grad_gate = jnp.sum(hidden * raw, axis=1, keepdims=True)
        grad_hidden = gate * raw
        grad_gate_pre = (
            grad_hidden * up_pre * sigmoid * (1.0 + gate_pre * (1.0 - sigmoid))
        ).astype(BF16)
        grad_up_pre = (grad_hidden * silu).astype(BF16)
        gated_ref[e] = (gate * hidden).astype(BF16)
        grad_gate_ref[e] = grad_gate_pre
        grad_up_ref[e] = grad_up_pre
        back = dot(grad_gate_pre, up_t_ref[e, :hidden_units, :]) + dot(
            grad_up_pre, up_t_ref[e, hidden_units:, :]
        )
        lane = lax.broadcasted_iota(jnp.int32, (blocks * capacity, LANES), 1)
        extra = jnp.where(lane == first_expert + e, grad_gate, 0.0).astype(BF16)
        back = back.astype(BF16)
        for j in range(blocks):
            packed_ref[j, e * capacity : (e + 1) * capacity, :width] = back[
                j * capacity : (j + 1) * capacity
            ]
            packed_ref[j, e * capacity : (e + 1) * capacity, width:] = extra[
                j * capacity : (j + 1) * capacity
            ]
    for j in range(blocks):
        home = dot(choices[j], packed_ref[j], 0, 0).astype(BF16)
        start = 0
        for out_ref, size in zip(out_refs, widths):
            out_ref[j] = home[:, start : start + size]
            start += size


def block_spec(width, place):
    return pl.BlockSpec(
        (1, LANES, width), lambda i, perm, first: (perm[i * STEP_BLOCKS + place], 0, 0)
    )


def whole(shape):
    return pl.BlockSpec(
        shape, lambda i, *scalars: (0,) * len(shape), pipeline_mode=pl.Buffered(1)
    )


def stepped(shape, dim):
    return pl.BlockSpec(
        shape, lambda i, *scalars: tuple(i if d == dim else 0 for d in range(len(shape)))
    )


def expert_grads(
    half, carry, perm, first, tokens, grads, grad_start, position, mask,
    router_t, up_both, up_both_t, down_t, capacity, widths,
):
    count = perm.shape[0]
    width = tokens.shape[2]
    experts_here, hidden_units = down_t.shape[0], down_t.shape[2]
    slots = STEP_BLOCKS * capacity
    expert_count = router_t.shape[0]
    slot_shape = lambda size: jax.ShapeDtypeStruct((experts_here, 2 * count * capacity, size), BF16)
    steps = count // STEP_BLOCKS
    slot_spec = lambda size: pl.BlockSpec(
        (experts_here, slots, size), lambda i, *scalars: (0, i + half * steps, 0)
    )
    before = 2 + STEP_BLOCKS + len(grads) + 6
    flops = 2 * count * capacity * experts_here * (7 * hidden_units * width + 3 * LANES * width)
    call = pl.pallas_call(
        functools.partial(expert_kernel, capacity, widths, len(grads), len(carry)),
        grid_spec=pltpu.PrefetchScalarGridSpec(
            num_scalar_prefetch=2,
            grid=(count // STEP_BLOCKS,),
            in_specs=[block_spec(width, j) for j in range(STEP_BLOCKS)]
            + [
                pl.BlockSpec(
                    (STEP_BLOCKS, LANES, group.shape[2]),
                    lambda i, *scalars: (i + grad_start // STEP_BLOCKS, 0, 0),
                )
                for group in grads
            ]
            + [
                stepped((STEP_BLOCKS, experts_here, LANES), 0),
                stepped((STEP_BLOCKS, expert_count, LANES), 0),
                whole(router_t.shape),
                whole(up_both.shape),
                whole(up_both_t.shape),
                whole(down_t.shape),
            ]
            + [pl.BlockSpec(memory_space=pl.ANY)] * len(carry),
            out_specs=[slot_spec(width)] * 2
            + [slot_spec(hidden_units)] * 3
            + [stepped((STEP_BLOCKS, LANES, size), 0) for size in widths],
            scratch_shapes=[
                pltpu.VMEM((STEP_BLOCKS, experts_here * capacity, sum(widths)), BF16)
            ],
        ),
        out_shape=[slot_shape(width)] * 2
        + [slot_shape(hidden_units)] * 3
        + [jax.ShapeDtypeStruct((count, LANES, size), BF16) for size in widths],
        compiler_params=pltpu.CompilerParams(vmem_limit_bytes=VMEM_BYTES),
        cost_estimate=pl.CostEstimate(
            flops=flops, transcendentals=0, bytes_accessed=6 * count * LANES * width * 2
        ),
        input_output_aliases={before + n: n for n in range(len(carry))},
        name="expert_grads",
    )
    return call(
        perm, first, *([tokens] * STEP_BLOCKS), *grads,
        position, mask, router_t, up_both, up_both_t, down_t, *carry,
    )


def output_kernel(capacity, widths, gated_ref, position_ref, down_ref, *refs):
    out_refs, packed_ref = refs[:-1], refs[-1]
    for e in range(down_ref.shape[0]):
        rows = dot(gated_ref[e], down_ref[e]).astype(BF16)
        for j in range(STEP_BLOCKS):
            packed_ref[j, e * capacity : (e + 1) * capacity, :] = rows[
                j * capacity : (j + 1) * capacity
            ]
    for j in range(STEP_BLOCKS):
        choice = jnp.concatenate(choose(position_ref[j], capacity), axis=0).astype(BF16)
        home = dot(choice, packed_ref[j], 0, 0).astype(BF16)
        start = 0
        for out_ref, size in zip(out_refs, widths):
            out_ref[j] = home[:, start : start + size]
            start += size


def expert_outputs(half, gated, position, down, capacity, widths):
    count = position.shape[0]
    experts_here, hidden_units, width = down.shape
    slots = STEP_BLOCKS * capacity
    steps = count // STEP_BLOCKS
    call = pl.pallas_call(
        functools.partial(output_kernel, capacity, widths),
        grid=(steps,),
        in_specs=[
            pl.BlockSpec(
                (experts_here, slots, hidden_units), lambda i: (0, i + half * steps, 0)
            ),
            stepped((STEP_BLOCKS, experts_here, LANES), 0),
            whole(down.shape),
        ],
        out_specs=[stepped((STEP_BLOCKS, LANES, size), 0) for size in widths],
        out_shape=[jax.ShapeDtypeStruct((count, LANES, size), BF16) for size in widths],
        scratch_shapes=[pltpu.VMEM((STEP_BLOCKS, experts_here * capacity, width), BF16)],
        compiler_params=pltpu.CompilerParams(vmem_limit_bytes=VMEM_BYTES),
        cost_estimate=pl.CostEstimate(
            flops=2 * count * capacity * experts_here * (hidden_units * width + LANES * width),
            transcendentals=0,
            bytes_accessed=2 * count * LANES * width * 2,
        ),
        name="expert_outputs",
    )
    return call(gated, position, down)


def chunk_kernel(widths, perm, *refs):
    left = jnp.concatenate([ref[...] for ref in refs[:STEP_BLOCKS]], axis=1)
    product = dot(left, refs[STEP_BLOCKS][...], 0, 0).astype(BF16)
    start = 0
    for out_ref, size in zip(refs[STEP_BLOCKS + 1 :], widths):
        for j in range(STEP_BLOCKS):
            out_ref[j] = product[j * LANES : (j + 1) * LANES, start : start + size]
        start += size


def chunk_products(perm, left, right, widths):
    count = perm.shape[0]
    tokens = left.shape[0]

    def column_block(place):
        return pl.BlockSpec((tokens, LANES), lambda i, perm: (0, perm[i * STEP_BLOCKS + place]))

    call = pl.pallas_call(
        functools.partial(chunk_kernel, widths),
        grid_spec=pltpu.PrefetchScalarGridSpec(
            num_scalar_prefetch=1,
            grid=(count // STEP_BLOCKS,),
            in_specs=[column_block(j) for j in range(STEP_BLOCKS)] + [whole(right.shape)],
            out_specs=[stepped((STEP_BLOCKS, LANES, size), 0) for size in widths],
        ),
        out_shape=[jax.ShapeDtypeStruct((count, LANES, size), BF16) for size in widths],
        compiler_params=pltpu.CompilerParams(vmem_limit_bytes=VMEM_BYTES),
        cost_estimate=pl.CostEstimate(
            flops=2 * count * LANES * tokens * right.shape[1],
            transcendentals=0,
            bytes_accessed=count * LANES * right.shape[1] * 2,
        ),
        name="chunk_products",
    )
    return call(perm, *([left] * STEP_BLOCKS), right)


def block_orders(lattice, device_count):
    if not lattice:
        numbers = jnp.arange(device_count, dtype=jnp.int32)
        return numbers[: device_count // 2], numbers[device_count // 2 :]
    spot = my_spot()
    dz, dx, dy = (grid.reshape(-1) for grid in np.indices((4, 2, 2)).astype(np.int32))
    chip = (spot["z"] - dz + 4) % 4 * 2 + (spot["x"] + dx) % 2
    orders = []
    for dc in (1, 0):
        core = (spot["core"] + dc) % 2
        orders.append(((chip * 2 + core) * 2 + (spot["y"] + dy) % 2).astype(jnp.int32))
    return orders


def chunk_orders():
    spot = my_spot()
    dz, dx = (grid.reshape(-1) for grid in np.indices((4, 2)).astype(np.int32))
    chip = (spot["z"] - dz + 4) % 4 * 2 + (spot["x"] + dx) % 2
    return [(chip * 2 + (spot["core"] + dc) % 2).astype(jnp.int32) for dc in (1, 0)]


TOKEN_ORDERS = (("x", "y", "z"), ("y", "z", "x"), ("z", "x", "y"))
GATHER_ORDERS = (("z", "y", "x"), ("x", "z", "y"), ("y", "x", "z"))
CHUNK_ORDERS = (("x", "z"), ("z", "x"))
TURNS = (1, -1, 1)


def scatter_job(partner, own):
    everything = jnp.concatenate([partner, own], axis=0)
    total = lax.psum_scatter(everything, BOTH, scatter_dimension=0, tiled=True)
    return total[0].astype(F32)
    yield


def tokens_home_jobs(lattice, partner, own, received=None):
    jobs = []
    for n, order in enumerate(TOKEN_ORDERS):
        if not lattice:
            jobs.append(scatter_job(partner[n], own[n]))
            continue
        shape = (4, 2, 2) + own[n].shape[1:]
        mine = own[n].reshape(shape)
        if received is None:
            jobs.append(home_job(partner[n].reshape(shape), mine, "zxy", order, TURNS[n]))
        else:
            both = Pending(mine, received[n].reshape(shape))
            jobs.append(home_job(None, both, "zxy", order, TURNS[n]))
    return jobs


def product_job(left, right):
    product = dot(left, right, 0, 0).astype(BF16)
    return lax.psum_scatter(product, DP, scatter_dimension=0, tiled=True).astype(F32)
    yield


def weight_grads_chunks(lattice, left, right, widths):
    if not lattice:
        return left, right
    return tuple(chunk_products(order, left, right, widths) for order in chunk_orders())


def weight_grads_jobs(lattice, first, second):
    if not lattice:
        return [product_job(first, second)]
    jobs = []
    for n, order in enumerate(CHUNK_ORDERS):
        shape = (4, 2) + first[n].shape[1:]
        jobs.append(
            home_job(first[n].reshape(shape), second[n].reshape(shape), "zx", order, TURNS[n])
        )
    return jobs


def on_device(
    inputs,
    input_gain,
    post_gain,
    query_gain,
    key_gain,
    query_weight,
    key_projection_matrix,
    value_projection_matrix,
    output_weight,
    router_weight,
    gate_weight,
    up_weight,
    down_weight,
    routes,
    cotangent,
):
    dp_count, tensor_count = lax.axis_size(DP), lax.axis_size("tensor")
    device_count = dp_count * tensor_count
    lattice = is_lattice(dp_count, tensor_count)
    row_count, width = inputs.shape
    experts = router_weight.shape[1]
    experts_here = gate_weight.shape[0]
    capacity = 2 * row_count * routes.shape[1] // experts

    links = Links()
    projections = jnp.concatenate(
        [query_weight, key_projection_matrix, value_projection_matrix], axis=0
    )
    query_rows, key_rows = query_weight.shape[0], key_projection_matrix.shape[0]
    projections_full = lax.all_gather(projections, DP, axis=1, tiled=True)

    expert_ids = jnp.arange(experts, dtype=jnp.int32)
    chosen_mask = jnp.any(routes[:, :, None] == expert_ids[None, None, :], axis=1)
    small = [input_gain, post_gain, query_gain, key_gain]
    sizes = [item.shape[0] for item in small]
    flat = jnp.concatenate(small)
    padded = -(-flat.shape[0] // LANES) * LANES
    flat = jnp.pad(flat, (0, padded - flat.shape[0]))
    router_lines = router_weight.size // LANES
    payload = jnp.concatenate(
        [
            router_weight.reshape(router_lines, LANES),
            flat.reshape(-1, LANES),
            chosen_mask.T.astype(BF16),
        ],
        axis=0,
    )
    gathered_at, other_inputs_at = links.add(gather_small_job(payload), swap_job(inputs))
    if lattice:
        cuts = (width // 8 * 3, width // 16 * 11)
        grad_at = links.add(
            *(
                spread_job(group, order, turn)
                for group, order, turn in zip(
                    jnp.split(cotangent, cuts, axis=1), GATHER_ORDERS, TURNS
                )
            )
        )

    def join_up(gate, up):
        return jnp.concatenate([gate, up], axis=2)

    def turn_last(values):
        return jnp.swapaxes(values, 1, 2)

    up_both = links.round(join_up, gate_weight, up_weight)
    output_held = after(output_weight, up_both[0, :8, :LANES])
    output_full = lax.all_gather(output_held, DP, axis=0, tiled=True)
    up_both_t = links.round(turn_last, up_both)
    down_t = links.round(turn_last, down_weight)
    other_inputs, gathered = other_inputs_at[0], None
    while gathered_at[0] is None:
        links.round()
    gathered = gathered_at[0]

    router_full = gathered[:, :router_lines].reshape(width, experts)
    flat_all = gathered[:, router_lines : router_lines + padded // LANES].reshape(
        device_count, padded
    )
    starts = np.cumsum([0] + sizes)
    input_scale, post_scale, query_scale, key_scale = (
        flat_all[:, starts[n] : starts[n + 1]].reshape(-1).astype(F32) for n in range(4)
    )
    mask_all = gathered[:, router_lines + padded // LANES :]
    first_expert = lax.axis_index(DP) * experts_here
    mask_here = lax.dynamic_slice_in_dim(mask_all, first_expert, experts_here, axis=1)
    earlier = jnp.asarray(np.triu(np.ones((row_count, row_count), np.float32), 1), BF16)
    rank = jnp.einsum("bet,tu->beu", mask_here, earlier, preferred_element_type=F32)
    position = jnp.where(mask_here > 0.5, rank, -1.0)
    orders = block_orders(lattice, device_count)
    positions = [position[order] for order in orders]
    masks = [mask_all[order] for order in orders]
    router_t = router_full.T

    both_inputs = in_order(inputs, other_inputs).astype(F32)
    residual_in = inputs.astype(F32)
    sequence = norm_rows(both_inputs, input_scale)[0].astype(BF16)
    _, input_hat, input_inv = norm_rows(residual_in, input_scale)
    seq_len = sequence.shape[0]
    local_heads = query_rows // HEAD_SIZE
    local_groups = key_rows // HEAD_SIZE
    per_group = local_heads // local_groups
    cosine_table, sine_table = rope_tables(seq_len, HEAD_SIZE)
    cosine, sine = cosine_table[:, None, :], sine_table[:, None, :]
    score_scale = 1.0 / math.sqrt(HEAD_SIZE)

    def attention(projections_full):
        projected = dot(sequence, projections_full, 1, 1)
        query_raw = projected[:, :query_rows].reshape(seq_len, local_heads, HEAD_SIZE)
        key_raw = projected[:, query_rows : query_rows + key_rows].reshape(
            seq_len, local_groups, HEAD_SIZE
        )
        value_low = (
            projected[:, query_rows + key_rows :]
            .astype(BF16)
            .reshape(seq_len, local_groups, HEAD_SIZE)
        )
        query_norm, query_hat, query_inv = norm_rows(query_raw, query_scale)
        query_low = (query_norm * cosine + rotate_half(query_norm) * sine).astype(BF16)
        key_norm, key_hat, key_inv = norm_rows(key_raw, key_scale)
        key_low = (key_norm * cosine + rotate_half(key_norm) * sine).astype(BF16)
        query_groups = query_low.reshape(seq_len, local_groups, per_group, HEAD_SIZE)
        scores = (
            jnp.einsum("qhgd,khd->hgqk", query_groups, key_low, preferred_element_type=F32)
            * score_scale
        )
        row_index = jnp.arange(seq_len, dtype=jnp.int32)
        scores = jnp.where(row_index[None, :] <= row_index[:, None], scores, -1e30)
        attend = jax.nn.softmax(scores, axis=-1)
        attend_low = attend.astype(BF16)
        mixed_low = (
            jnp.einsum("hgqk,khd->qhgd", attend_low, value_low, preferred_element_type=F32)
            .astype(BF16)
            .reshape(seq_len, query_rows)
        )
        return (
            query_hat, query_inv, query_groups, key_hat, key_inv, key_low, value_low,
            attend, attend_low, mixed_low, projections_full,
        )

    (
        query_hat, query_inv, query_groups, key_hat, key_inv, key_low, value_low,
        attend, attend_low, mixed_low, projections_full,
    ) = links.round(attention, projections_full)
    mixed_out = links.round(lambda mixed: dot(mixed, output_full, 1, 1), mixed_low)
    links.finish()
    if lattice:
        all_grads = [[place[0][n] for place in grad_at] for n in range(2)]
        grad_starts = (0, 0)
    else:
        all_grads = ([lax.all_gather(cotangent[None], BOTH, axis=0, tiled=True)],) * 2
        grad_starts = (0, device_count // 2)
    (mixed_home,) = links.add(sum_tokens_job(mixed_out))
    links.finish()
    residual_mid = residual_in + mixed_home[0]
    post_norm, post_hat, post_inv = norm_rows(residual_mid, post_scale)
    post_low = post_norm.astype(BF16)
    all_tokens = lax.all_gather(post_low[None], BOTH, axis=0, tiled=True)

    logits = dot(post_low, router_full)
    top = jnp.max(jnp.where(chosen_mask, logits, -3e38), axis=-1, keepdims=True)
    powers = jnp.where(chosen_mask, jnp.exp(jnp.minimum(logits - top, 0.0)), 0.0)
    gates = powers / jnp.sum(powers, axis=-1, keepdims=True)

    wide = width // 8 * 3
    widths = (wide, wide, width - 2 * wide + LANES)
    first_scalar = first_expert.astype(jnp.int32).reshape(1)

    def half_grads(half, carry):
        return expert_grads(
            half, carry, orders[half], first_scalar, all_tokens, all_grads[half],
            grad_starts[half], positions[half], masks[half],
            router_t, up_both, up_both_t, down_t, capacity, widths,
        )

    results = half_grads(0, ())
    partner = results[5:]
    received = [hop(group, "core") for group in partner] if lattice else None
    results = half_grads(1, results[:5])
    rows, grad_rows, gated, grad_gate_pre, grad_up_pre = results[:5]
    own = results[5:]

    def slot_product(left, right):
        return jnp.einsum("esd,esf->edf", left, right, preferred_element_type=F32)

    out_widths = (wide, wide, width - 2 * wide)

    def outputs(gated):
        return [
            expert_outputs(n, gated, positions[n], down_weight, capacity, out_widths)
            for n in range(2)
        ]

    home = links.add(*tokens_home_jobs(lattice, partner, own, received))
    out_parts = links.round(outputs, gated)
    grad_gate_w = links.round(slot_product, rows, grad_gate_pre)
    grad_down = links.round(slot_product, gated, grad_rows)
    links.finish()
    home = [place[0] for place in home]

    grad_out = cotangent.astype(F32)
    grad_post = jnp.concatenate([home[0], home[1], home[2][:, : width - 2 * wide]], axis=1)
    start = width - 2 * wide
    grad_gates = home[2][:, start : start + experts]
    grad_logits = (
        gates * (grad_gates - jnp.sum(gates * grad_gates, axis=-1, keepdims=True))
    ).astype(BF16)
    grad_post = grad_post + dot(grad_logits, router_full, 1, 1)
    grad_mid_norm, post_terms = norm_back(grad_post, post_scale, post_hat, post_inv)
    grad_mid = grad_out + grad_mid_norm
    grad_mid_low = grad_mid.astype(BF16)
    out_home = links.add(*tokens_home_jobs(lattice, *out_parts))
    (other_grads,) = links.add(swap_job(grad_mid_low))
    grad_up_w = links.round(slot_product, rows, grad_up_pre)
    grad_attention = in_order(grad_mid_low, other_grads[0])

    out_split = (query_rows // 8 * 3, query_rows - query_rows // 8 * 3)

    def back_scores(grad_attention):
        grad_mixed = dot(grad_attention, output_full).astype(BF16)
        chunks = weight_grads_chunks(lattice, grad_attention, mixed_low, out_split)
        grad_groups = grad_mixed.reshape(seq_len, local_groups, per_group, HEAD_SIZE)
        grad_attend = jnp.einsum(
            "qhgd,khd->hgqk", grad_groups, value_low, preferred_element_type=F32
        )
        row_inner = jnp.sum(attend * grad_attend, axis=-1, keepdims=True)
        grad_scores = (attend * (grad_attend - row_inner)).astype(BF16)
        return grad_groups, grad_scores, chunks

    grad_groups, grad_scores, chunks = links.round(back_scores, grad_attention)
    grad_output_at = links.add(*weight_grads_jobs(lattice, *chunks))
    grad_router = dot(post_low, grad_logits, 0, 0)
    grad_post_gain = jnp.sum(post_terms, axis=0)
    (early,) = links.add(
        reduce_small_job(
            jnp.concatenate(
                [
                    grad_router.reshape(device_count, -1),
                    grad_post_gain.reshape(device_count, -1),
                    jnp.zeros((device_count, LANES - sizes[1]), F32),
                ],
                axis=1,
            ).reshape(device_count, -1, LANES)
        )
    )

    def back_heads(grad_groups, grad_scores):
        grad_value = jnp.einsum(
            "hgqk,qhgd->khd", attend_low, grad_groups, preferred_element_type=F32
        )
        grad_key_rot = (
            jnp.einsum("hgqk,qhgd->khd", grad_scores, query_groups, preferred_element_type=F32)
            * score_scale
        )
        grad_query_rot = (
            jnp.einsum("hgqk,khd->qhgd", grad_scores, key_low, preferred_element_type=F32)
            * score_scale
        ).reshape(seq_len, local_heads, HEAD_SIZE)
        return grad_value, grad_key_rot, grad_query_rot

    grad_value, grad_key_rot, grad_query_rot = links.round(back_heads, grad_groups, grad_scores)

    def back_norms(grad_value, grad_key_rot, grad_query_rot):
        grad_query_norm = grad_query_rot * cosine + rotate_back(grad_query_rot * sine)
        grad_query_raw, query_terms = norm_back(grad_query_norm, query_scale, query_hat, query_inv)
        grad_query_gain = jnp.sum(query_terms, axis=(0, 1))
        grad_key_norm = grad_key_rot * cosine + rotate_back(grad_key_rot * sine)
        grad_key_raw, key_terms = norm_back(grad_key_norm, key_scale, key_hat, key_inv)
        grad_key_gain = jnp.sum(key_terms, axis=(0, 1))
        grad_projected = jnp.concatenate(
            [
                grad_query_raw.reshape(seq_len, query_rows).astype(BF16),
                grad_key_raw.reshape(seq_len, key_rows).astype(BF16),
                grad_value.reshape(seq_len, key_rows).astype(BF16),
            ],
            axis=1,
        )
        return grad_projected, grad_query_gain, grad_key_gain

    grad_projected, grad_query_gain, grad_key_gain = links.round(
        back_norms, grad_value, grad_key_rot, grad_query_rot
    )
    total_rows = query_rows + 2 * key_rows
    split = total_rows // LANES * 2 // 5 * LANES
    chunks = weight_grads_chunks(
        lattice, sequence, grad_projected, (split, total_rows - split)
    )
    grad_projections_at = links.add(*weight_grads_jobs(lattice, *chunks))
    normed_parts = links.round(
        lambda grad: dot(grad, projections_full), grad_projected
    )
    (grad_normed,) = links.add(sum_tokens_job(normed_parts))
    links.round()
    grad_in_norm, input_terms = norm_back(grad_normed[0], input_scale, input_hat, input_inv)
    grad_input_gain = jnp.sum(input_terms, axis=0)
    grad_inputs = (grad_mid + grad_in_norm).astype(BF16)
    late_parts = [grad_input_gain, grad_query_gain, grad_key_gain]
    late_sizes = [sizes[0], sizes[2], sizes[3]]
    (late,) = links.add(
        reduce_small_job(
            jnp.concatenate(
                [part.reshape(device_count, -1) for part in late_parts]
                + [jnp.zeros((device_count, LANES - sum(late_sizes)), F32)],
                axis=1,
            ).reshape(device_count, 1, LANES)
        )
    )
    links.finish()
    result = (residual_mid + jnp.concatenate([p[0] for p in out_home], axis=1)).astype(BF16)
    early, late = early[0].reshape(-1), late[0].reshape(-1)
    grad_router = early[: router_weight.size].reshape(router_weight.shape)
    grad_post_gain = early[router_weight.size : router_weight.size + sizes[1]]
    grad_output_w = jnp.concatenate([place[0] for place in grad_output_at], axis=1)
    grad_projections = jnp.concatenate([place[0] for place in grad_projections_at], axis=1).T
    grad_query_w = grad_projections[:query_rows]
    grad_key_w = grad_projections[query_rows : query_rows + key_rows]
    grad_value_w = grad_projections[query_rows + key_rows :]
    bounds = np.cumsum([0] + late_sizes)
    grad_input_gain, grad_query_gain, grad_key_gain = (
        late[bounds[n] : bounds[n + 1]] for n in range(3)
    )
    return (
        result,
        grad_inputs,
        grad_input_gain,
        grad_post_gain,
        grad_query_gain,
        grad_key_gain,
        grad_query_w,
        grad_key_w,
        grad_value_w,
        grad_output_w,
        grad_router,
        grad_gate_w,
        grad_up_w,
        grad_down,
    )


def solution(mesh):
    dp_count, tensor_count = mesh.devices.shape
    split = jax.sharding.Mesh(
        mesh.devices.reshape(dp_count // 2, 2, tensor_count), ("chip", "core", "tensor")
    )
    tokens, line = P(BOTH, None), P(BOTH)
    gated = P(DP, None, "tensor")
    weights = (P("tensor", DP),) * 3 + (P(DP, "tensor"), tokens, gated, gated, P(DP, "tensor", None))
    return jax.shard_map(
        on_device,
        mesh=split,
        in_specs=(tokens,) + (line,) * 4 + weights + (tokens, tokens),
        out_specs=(tokens, tokens) + (line,) * 4 + weights,
        check_vma=False,
    )
```

time: 1170 us -> 1000 us (0.85)
  blocking collectives: 80.4 us -> 0 us
  waiting for transfers between devices: 489 us -> 423 us
  local copies, waits for them, and re-layouts: 112 us -> 69.3 us
  matrix products: 107 us -> 78.4 us
  other arithmetic: 131 us -> 159 us
  starting transfers between devices: 99.9 us -> 121 us
    all_gather x1 -> x0, blocking collectives: 80.4 us -> none  [on_device(): gathered = lax.all_gather(payload[None], BOTH, axis=0, tiled=True)]
    ppermute x10 -> x21, waiting for transfers between devices: 30.1 us -> 105 us  [flip(): lax.ppermute(values, BOTH, [(source, source ^ bits) for source in range(c...]
    convert_element_type x6 -> x35, other arithmetic: 10.8 us -> 74.8 us  [the longest x30 68.7 us: piece(): return Pending(*picked).total().astype(BF16)]
    ppermute x56 -> x74, waiting for transfers between devices: 239 us -> 175 us  [hop(): return lax.ppermute(values, BOTH, pairs)]
    all_gather x3 -> x2, waiting for transfers between devices: 86 us -> 29.2 us  [the longest x1 29.2 us: on_device(): output_full = lax.all_gather(output_held, DP, axis=0, tiled=True)]
    convert_element_type x46 -> x7, other arithmetic: 64 us -> 10.9 us  [add_low(): return (first.astype(F32) + second.astype(F32)).astype(BF16)]
    optimization_barrier x0 -> x7, local copies, waits for them, and re-layouts: none -> 29.8 us  [the longest x3 14.1 us: after(): return lax.optimization_barrier((values, others))[0]]
    dot_general x11 -> x8, matrix products: 74 us -> 49.6 us  [the longest x3 42 us: slot_product(): return jnp.einsum('esd,esf->edf', left, right, preferred_element_type=F32)]
  transfers between devices with their start and end apart: 74 -> 102, of which waited for: 34 -> 34; matrix products, arithmetic and copies ran while one was open for 23% -> 22% of each run, Pallas kernels for 6% -> 8%
where the time goes in v2:
time: 1000 us; the launch traced here: 992 us
  waiting for transfers between devices  423 us (42%)
  other arithmetic  159 us (16%)
  Pallas kernels  125 us (12%)
  starting transfers between devices  121 us (12%)
  matrix products  78.4 us (8%)
  local copies, waits for them, and re-layouts  69.3 us (7%)
  between operations  16.4 us (2%)
    ppermute x74, waiting for transfers between devices, hop(): return lax.ppermute(values, BOTH, pairs)  175 us
    ppermute x21, waiting for transfers between devices, flip(): lax.ppermute(values, BOTH, [(source, source ^ bits) for source in range(c...  105 us
    ppermute x74, starting transfers between devices, hop(): return lax.ppermute(values, BOTH, pairs)  99.4 us
    all_gather x1, waiting for transfers between devices, on_device(): all_tokens = lax.all_gather(post_low[None], BOTH, axis=0, tiled=True)  99.3 us
    pallas_call x2, Pallas kernels, expert_grads(): call(perm, first, *[tokens] * STEP_BLOCKS, *grads, position, mask, router...  83 us
    convert_element_type x30, other arithmetic, piece(): return Pending(*picked).total().astype(BF16)  68.7 us
    dot_general x3, matrix products, slot_product(): return jnp.einsum('esd,esf->edf', left, right, preferred_element_type=F32)  42 us
    all_gather x1, waiting for transfers between devices, on_device(): output_full = lax.all_gather(output_held, DP, axis=0, tiled=True)  29.2 us
  transfers between devices with their start and end apart: 102, of which 34 were waited for; matrix products, arithmetic and copies ran while one was open for 22% of the time, Pallas kernels for 8%

profile of v2, /device:TPU:0, one launch (start us, length us, event | category | flops | bytes accessed | tf_op | source)
XLA Modules:
  0.0 991.5 jit_solution(4412081751980167201)
XLA Ops:
  49.7 18.0 %collective-permute-done.10 = bf16[4,50,128]{2,0,1:T(4,128)(2,1)S(1)} collective-permute-done((bf16[4,50,128]{2,0,1:T(4,128)(2,1)S(1)}, bf16[4,50,128]{2,0,1:T(4,128)(2,1)S(1)}, u32[]{:S(2)}, u32[]{:S(2)}) %collective-permute-start.10) | collective-permute-done | bytes 51232 | tf_op jit(solution)/shard_map/ppermute | solution.py:190
  99.8 57.6 %collective-permute-done.15 = bf16[16,50,128]{2,0,1:T(8,128)(2,1)} collective-permute-done((bf16[16,50,128]{2,0,1:T(8,128)(2,1)}, bf16[16,50,128]{2,0,1:T(8,128)(2,1)}, u32[]{:S(2)}, u32[]{:S(2)}) %collective-permute-start.15) | collective-permute-done | bytes 204832 | tf_op jit(solution)/shard_map/ppermute | solution.py:190
  199.7 8.1 collective-permute-done.20
  215.8 29.2 %all-gather.7.cloned.1.call-done = bf16[2048,2048]{1,0:T(8,128)(2,1)} async-done(((bf16[128,2048]{1,0:T(8,128)(2,1)}), bf16[2048,2048]{1,0:T(8,128)(2,1)}) %all-gather.7.cloned.1.call-update) | async-done | bytes 8388624 | tf_op jit(solution)/shard_map/all_gather | solution.py:648
  252.4 12.5 %collective-permute-done.26 = bf16[128,2048]{1,0:T(8,128)(2,1)S(1)} collective-permute-done((bf16[128,2048]{1,0:T(8,128)(2,1)S(1)}, bf16[128,2048]{1,0:T(8,128)(2,1)S(1)}, u32[]{:S(2)}, u32[]{:S(2)}) %collective-permute-start.26) | collective-permute-done | bytes 524320 | tf_op jit(solution)/shard_map/ppermute | solution.py:230
  267.9 8.7 copy.516.refs_10_
  280.5 99.3 %all-gather.9.cloned.1.call-done = bf16[4096,2048]{1,0:T(8,128)(2,1)} async-done(((bf16[128,2048]{1,0:T(8,128)(2,1)}), bf16[4096,2048]{1,0:T(8,128)(2,1)}) %all-gather.9.cloned.1.call-update) | async-done | bytes 16777232 | tf_op jit(solution)/shard_map/all_gather | solution.py:738
  379.8 41.6 %expert_grads.2 = (bf16[2,2048,2048]{2,1,0:T(8,128)(2,1)}, bf16[2,2048,2048]{2,1,0:T(8,128)(2,1)}, bf16[2,2048,384]{2,1,0:T(8,128)(2,1)}, bf16[2,2048,384]{2,1,0...) custom-call(s32[16]{0:T(128)} %get-tuple-element.650.perm, ...), custom_call_target="tpu_custom_call" | custom-call | flops 25769803776 | bytes 50331648 | tf_op jit(solution)/shard_map/expert_grads/pallas_call | solution.py:417
  424.9 41.4 %expert_grads.3 = (bf16[2,2048,2048]{2,1,0:T(8,128)(2,1)}, bf16[2,2048,2048]{2,1,0:T(8,128)(2,1)}, bf16[2,2048,384]{2,1,0:T(8,128)(2,1)}, bf16[2,2048,384]{2,1,0...) custom-call(s32[16]{0:T(128)} %get-tuple-element.646.perm, ...), custom_call_target="tpu_custom_call", output_to_operand_aliasing={{0}: (15, {}), {1}: (16, {}), {2}: (17, {}), {3}: (18, {}),... | custom-call | flops 25769803776 | bytes 50331648 | tf_op jit(solution)/shard_map/expert_grads/pallas_call | solution.py:417
  482.5 10.8 %expert_outputs.3 = (bf16[16,128,768]{2,1,0:T(8,128)(2,1)}, bf16[16,128,768]{2,1,0:T(8,128)(2,1)}, bf16[16,128,512]{2,1,0:T(8,128)(2,1)}) custom-call(bf16[2,2048,384]{2,1,0:T(8,128)(2,1)} %get-tuple-element.376.gated_ref, f32[16,2,128]{2,1,0:T(2,128)} %gather_fusion, bf16[2,384,2048]{2,1,0:T(8,128)(2,1)} %down_ref.3), custom_call_target="tpu_custom_call" | custom-call | flops 4294967296 | bytes 16777216 | tf_op jit(solution)/shard_map/expert_outputs/pallas_call | solution.py:466
  495.6 10.6 %expert_outputs.2 = (bf16[16,128,768]{2,1,0:T(8,128)(2,1)}, bf16[16,128,768]{2,1,0:T(8,128)(2,1)}, bf16[16,128,512]{2,1,0:T(8,128)(2,1)}) custom-call(bf16[2,2048,384]{2,1,0:T(8,128)(2,1)} %get-tuple-element.376.gated_ref, f32[16,2,128]{2,1,0:T(2,128)} %gather_fusion.2, bf16[2,384,2048]{2,1,0:T(8,128)(2,1)} %down_ref.3), custom_call_target="tpu_custom_call" | custom-call | flops 4294967296 | bytes 16777216 | tf_op jit(solution)/shard_map/expert_outputs/pallas_call | solution.py:466
  506.2 9.3 collective-permute-done.30
  527.8 14.2 %fusion.213 = f32[2,2048,384]{2,1,0:T(8,128)} fusion(bf16[2,2048,2048]{2,1,0:T(8,128)(2,1)} %get-tuple-element.391, bf16[2,2048,384]{2,1,0:T(8,128)(2,1)S(1)} %copy-done.43), kind=kOutput, calls=%fused_computation.497 | convolution fusion | flops 6442450944 | bytes 26214400 | tf_op jit(solution)/shard_map/esd,esf->edf/dot_general | solution.py:764
  542.0 18.5 %collective-permute-done.34 = bf16[2,128,768]{2,1,0:T(8,128)(2,1)} collective-permute-done((bf16[2,128,768]{2,1,0:T(8,128)(2,1)S(1)}, bf16[2,128,768]{2,1,0:T(8,128)(2,1)}, u32[]{:S(2)}, u32[]{:S(2)}) %collective-permute-start.34) | collective-permute-done | bytes 393248 | tf_op jit(solution)/shard_map/ppermute | solution.py:77
  568.0 12.6 %fusion.214 = f32[2,384,2048]{2,1,0:T(8,128)} fusion(bf16[2,2048,384]{2,1,0:T(8,128)(2,1)S(1)} %copy-done.42, bf16[2,2048,2048]{2,1,0:T(8,128)(2,1)} %get-tuple-element.377), kind=kOutput, calls=%fused_computation.498 | convolution fusion | flops 6442450944 | bytes 26214400 | tf_op jit(solution)/shard_map/esd,esf->edf/dot_general | solution.py:764
  617.4 15.2 %fusion.215 = f32[2,2048,384]{2,1,0:T(8,128)} fusion(bf16[2,2048,2048]{2,1,0:T(8,128)(2,1)} %get-tuple-element.391, bf16[2,2048,384]{2,1,0:T(8,128)(2,1)} %get-tuple-element.392), kind=kOutput, calls=%fused_computation.499 | convolution fusion | flops 6442450944 | bytes 26214400 | tf_op jit(solution)/shard_map/esd,esf->edf/dot_general | solution.py:764
  676.2 9.3 collective-permute-done.49
  701.7 8.1 collective-permute-done.58
  721.3 10.9 %collective-permute-done.54 = bf16[2,2,128,512]{3,2,1,0:T(8,128)(2,1)S(1)} collective-permute-done((bf16[2,2,128,512]{3,2,1,0:T(8,128)(2,1)}, bf16[2,2,128,512]{3,2,1,0:T(8,128)(2,1)S(1)}, u32[]{:S(2)}, u32[]{:S(2)}) %collective-permute-start.54) | collective-permute-done | bytes 524320 | tf_op jit(solution)/shard_map/ppermute | solution.py:77
  732.2 9.9 collective-permute-done.55
  761.4 9.3 collective-permute-done.68
  774.9 14.4 %collective-permute-done.61 = bf16[128,768]{1,0:T(8,128)(2,1)} collective-permute-done((bf16[128,768]{1,0:T(8,128)(2,1)}, bf16[128,768]{1,0:T(8,128)(2,1)}, u32[]{:S(2)}, u32[]{:S(2)}) %collective-permute-start.61) | collective-permute-done | bytes 196640 | tf_op jit(solution)/shard_map/ppermute | solution.py:77
  846.1 15.0 %collective-permute-done.74 = bf16[128,768]{1,0:T(8,128)(2,1)} collective-permute-done((bf16[128,768]{1,0:T(8,128)(2,1)}, bf16[128,768]{1,0:T(8,128)(2,1)}, u32[]{:S(2)}, u32[]{:S(2)}) %collective-permute-start.74) | collective-permute-done | bytes 196640 | tf_op jit(solution)/shard_map/ppermute | solution.py:77
  921.4 34.4 %collective-permute-done.86 = bf16[128,1024]{1,0:T(8,128)(2,1)S(1)} collective-permute-done((bf16[128,1024]{1,0:T(8,128)(2,1)S(1)}, bf16[128,1024]{1,0:T(8,128)(2,1)S(1)}, u32[]{:S(2)}, u32[]{:S(2)}) %collective-permute-start.86) | collective-permute-done | bytes 262176 | tf_op jit(solution)/shard_map/ppermute | solution.py:77
  (697 shorter events, 456.3 us)
Async XLA Ops:
  7.3 162.8 %all-gather.5.cloned.1.call-start = ((), (), s32[]{:S(2)}) async-start(), calls=%async_computation | async-start | bytes 11141120 | tf_op jit(solution)/shard_map/all_gather | solution.py:610
  9.4 235.5 %all-gather.7.cloned.1.call-start = ((), (), s32[]{:S(2)}) async-start(), calls=%async_computation.1 | async-start | bytes 8912896 | tf_op jit(solution)/shard_map/all_gather | solution.py:648
  10.2 369.7 %all-gather.9.cloned.1.call-start = ((), (), s32[]{:S(2)}) async-start(), calls=%async_computation.2 | async-start | bytes 17301504 | tf_op jit(solution)/shard_map/all_gather | solution.py:738
  82.9 74.5 %collective-permute-start.16 = (bf16[4,1,1,128,768]{4,3,2,1,0:T(8,128)(2,1)}, bf16[4,1,1,128,768]{4,3,2,1,0:T(8,128)(2,1)S(1)}, u32[]{:S(2)}, u32[]{:S(2)}) collective-permute-start(bf16[4,1,1,128,768]{4,3,2,1,0:T(8,128)(2,1)} %pad_maximum_fusion.8), channel_id=1, source_target_pairs={{0,1},{1,0},{2,3},{3,2},{4,5},{5,4},{6,7},{7,6},{8,9},{9,8},{10,11... | collective-permute-start | bytes 2359304 | tf_op jit(solution)/shard_map/ppermute | solution.py:77
  84.3 73.1 %collective-permute-start.18 = (bf16[1,2,2,128,640]{4,3,2,1,0:T(8,128)(2,1)}, bf16[1,2,2,128,640]{4,3,2,1,0:T(8,128)(2,1)}, u32[]{:S(2)}, u32[]{:S(2)}) collective-permute-start(bf16[1,2,2,128,640]{4,3,2,1,0:T(8,128)(2,1)} %pad_maximum_fusion.9), channel_id=1, source_target_pairs={{0,8},{1,9},{2,10},{3,11},{4,12},{5,13},{6,14},{7,15},{8,16},{9,17... | collective-permute-start | bytes 1966088 | tf_op jit(solution)/shard_map/ppermute | solution.py:77
  84.4 73.0 %collective-permute-start.19 = (bf16[1,2,2,128,640]{4,3,2,1,0:T(8,128)(2,1)}, bf16[1,2,2,128,640]{4,3,2,1,0:T(8,128)(2,1)}, u32[]{:S(2)}, u32[]{:S(2)}) collective-permute-start(bf16[1,2,2,128,640]{4,3,2,1,0:T(8,128)(2,1)} %pad_maximum_fusion.9), channel_id=1, source_target_pairs={{0,24},{1,25},{2,26},{3,27},{4,28},{5,29},{6,30},{7,31},{8,0},{9,1... | collective-permute-start | bytes 1966088 | tf_op jit(solution)/shard_map/ppermute | solution.py:77
  92.6 64.8 %collective-permute-start.17 = (bf16[1,2,1,128,640]{4,3,2,1,0:T(8,128)(2,1)}, bf16[1,2,1,128,640]{4,3,2,1,0:T(8,128)(2,1)}, u32[]{:S(2)}, u32[]{:S(2)}) collective-permute-start(bf16[1,2,1,128,640]{4,3,2,1,0:T(8,128)(2,1)} %collective-permute-done.13), channel_id=1, source_target_pairs={{0,24},{1,25},{2,26},{3,27},{4,28},{5,29},{6,30},{7,31},{8,0},{9,1... | collective-permute-start | bytes 983048 | tf_op jit(solution)/shard_map/ppermute | solution.py:77
  95.0 62.4 %collective-permute-start.15 = (bf16[16,50,128]{2,0,1:T(8,128)(2,1)}, bf16[16,50,128]{2,0,1:T(8,128)(2,1)}, u32[]{:S(2)}, u32[]{:S(2)}) collective-permute-start(bf16[16,50,128]{2,0,1:T(8,128)(2,1)} %constant_dynamic-slice_fusion.15), channel_id=1, source_target_pairs={{0,16},{1,17},{2,18},{3,19},{4,20},{5,21},{6,22},{7,23},{8,24},{9,... | collective-permute-start | bytes 614408 | tf_op jit(solution)/shard_map/ppermute | solution.py:190
  165.2 42.6 %collective-permute-start.20 = (bf16[4,1,2,128,768]{4,3,2,1,0:T(8,128)(2,1)}, bf16[4,1,2,128,768]{4,3,2,1,0:T(8,128)(2,1)}, u32[]{:S(2)}, u32[]{:S(2)}) collective-permute-start(bf16[4,1,2,128,768]{4,3,2,1,0:T(8,128)(2,1)} %pad_maximum_fusion.4), channel_id=1, source_target_pairs={{0,4},{1,5},{2,6},{3,7},{4,0},{5,1},{6,2},{7,3},{8,12},{9,13},{10,... | collective-permute-start | bytes 4718600 | tf_op jit(solution)/shard_map/ppermute | solution.py:77
  421.4 49.5 %collective-permute-start.28 = (bf16[16,128,768]{2,1,0:T(8,128)(2,1)}, bf16[16,128,768]{2,1,0:T(8,128)(2,1)}, u32[]{:S(2)}, u32[]{:S(2)}) collective-permute-start(bf16[16,128,768]{2,1,0:T(8,128)(2,1)} %get-tuple-element.338), channel_id=1, source_target_pairs={{0,2},{1,3},{2,0},{3,1},{4,6},{5,7},{6,4},{7,5},{8,10},{9,11},{10,... | collective-permute-start | bytes 9437192 | tf_op jit(solution)/shard_map/ppermute | solution.py:77
  421.7 44.6 %collective-permute-start.29 = (bf16[16,128,640]{2,1,0:T(8,128)(2,1)}, bf16[16,128,640]{2,1,0:T(8,128)(2,1)}, u32[]{:S(2)}, u32[]{:S(2)}) collective-permute-start(bf16[16,128,640]{2,1,0:T(8,128)(2,1)} %get-tuple-element.340), channel_id=1, source_target_pairs={{0,2},{1,3},{2,0},{3,1},{4,6},{5,7},{6,4},{7,5},{8,10},{9,11},{10,... | collective-permute-start | bytes 7864328 | tf_op jit(solution)/shard_map/ppermute | solution.py:77
  422.1 51.9 %collective-permute-start.27 = (bf16[16,128,768]{2,1,0:T(8,128)(2,1)}, bf16[16,128,768]{2,1,0:T(8,128)(2,1)}, u32[]{:S(2)}, u32[]{:S(2)}) collective-permute-start(bf16[16,128,768]{2,1,0:T(8,128)(2,1)} %get-tuple-element.336), channel_id=1, source_target_pairs={{0,2},{1,3},{2,0},{3,1},{4,6},{5,7},{6,4},{7,5},{8,10},{9,11},{10,... | collective-permute-start | bytes 9437192 | tf_op jit(solution)/shard_map/ppermute | solution.py:77
  478.6 36.9 %collective-permute-start.30 = (bf16[4,2,128,768]{3,2,1,0:T(8,128)(2,1)}, bf16[4,2,128,768]{3,2,1,0:T(8,128)(2,1)}, u32[]{:S(2)}, u32[]{:S(2)}) collective-permute-start(bf16[4,2,128,768]{3,2,1,0:T(8,128)(2,1)} %get-tuple-element.341), channel_id=1, source_target_pairs={{0,4},{1,5},{2,6},{3,7},{4,0},{5,1},{6,2},{7,3},{8,12},{9,13},{10,... | collective-permute-start | bytes 4718600 | tf_op jit(solution)/shard_map/ppermute | solution.py:77
  479.8 36.6 %collective-permute-start.31 = (bf16[4,2,128,768]{3,2,1,0:T(8,128)(2,1)}, bf16[4,2,128,768]{3,2,1,0:T(8,128)(2,1)}, u32[]{:S(2)}, u32[]{:S(2)}) collective-permute-start(bf16[4,2,128,768]{3,2,1,0:T(8,128)(2,1)} %fusion.15), channel_id=1, source_target_pairs={{0,1},{1,0},{2,3},{3,2},{4,5},{5,4},{6,7},{7,6},{8,9},{9,8},{10,11... | collective-permute-start | bytes 4718600 | tf_op jit(solution)/shard_map/ppermute | solution.py:77
  521.6 38.9 %collective-permute-start.33 = (bf16[4,128,768]{2,1,0:T(8,128)(2,1)S(1)}, bf16[4,128,768]{2,1,0:T(8,128)(2,1)S(1)}, u32[]{:S(2)}, u32[]{:S(2)}) collective-permute-start(bf16[4,128,768]{2,1,0:T(8,128)(2,1)S(1)} %get-tuple-element.359), channel_id=1, source_target_pairs={{0,1},{1,0},{2,3},{3,2},{4,5},{5,4},{6,7},{7,6},{8,9},{9,8},{10,11... | collective-permute-start | bytes 2359304 | tf_op jit(solution)/shard_map/ppermute | solution.py:77
  522.4 38.1 %collective-permute-start.35 = (bf16[2,2,128,640]{3,2,1,0:T(8,128)(2,1)S(1)}, bf16[2,2,128,640]{3,2,1,0:T(8,128)(2,1)S(1)}, u32[]{:S(2)}, u32[]{:S(2)}) collective-permute-start(bf16[2,2,128,640]{3,2,1,0:T(8,128)(2,1)S(1)} %bitcast.676), channel_id=1, source_target_pairs={{0,24},{1,25},{2,26},{3,27},{4,28},{5,29},{6,30},{7,31},{8,0},{9,1... | collective-permute-start | bytes 1966088 | tf_op jit(solution)/shard_map/ppermute | solution.py:77
  695.0 47.1 %collective-permute-start.57 = (bf16[4,2,128,1280]{3,2,1,0:T(8,128)(2,1)}, bf16[4,2,128,1280]{3,2,1,0:T(8,128)(2,1)}, u32[]{:S(2)}, u32[]{:S(2)}) collective-permute-start(bf16[4,2,128,1280]{3,2,1,0:T(8,128)(2,1)} %bitcast.88), channel_id=1, source_target_pairs={{0,2},{1,3},{2,0},{3,1},{4,6},{5,7},{6,4},{7,5},{8,10},{9,11},{10,... | collective-permute-start | bytes 7864328 | tf_op jit(solution)/shard_map/ppermute | solution.py:77
  695.0 47.1 %collective-permute-start.56 = (bf16[4,2,128,768]{3,2,1,0:T(8,128)(2,1)}, bf16[4,2,128,768]{3,2,1,0:T(8,128)(2,1)}, u32[]{:S(2)}, u32[]{:S(2)}) collective-permute-start(bf16[4,2,128,768]{3,2,1,0:T(8,128)(2,1)} %bitcast.87), channel_id=1, source_target_pairs={{0,2},{1,3},{2,0},{3,1},{4,6},{5,7},{6,4},{7,5},{8,10},{9,11},{10,... | collective-permute-start | bytes 4718600 | tf_op jit(solution)/shard_map/ppermute | solution.py:77
  752.6 43.2 %collective-permute-start.65 = (bf16[4,128,768]{2,1,0:T(8,128)(2,1)}, bf16[4,128,768]{2,1,0:T(8,128)(2,1)}, u32[]{:S(2)}, u32[]{:S(2)}) collective-permute-start(bf16[4,128,768]{2,1,0:T(8,128)(2,1)} %get-tuple-element.445), channel_id=1, source_target_pairs={{0,4},{1,5},{2,6},{3,7},{4,0},{5,1},{6,2},{7,3},{8,12},{9,13},{10,... | collective-permute-start | bytes 2359304 | tf_op jit(solution)/shard_map/ppermute | solution.py:77
  753.2 42.7 %collective-permute-start.66 = (bf16[2,128,1280]{2,1,0:T(8,128)(2,1)}, bf16[2,128,1280]{2,1,0:T(8,128)(2,1)}, u32[]{:S(2)}, u32[]{:S(2)}) collective-permute-start(bf16[2,128,1280]{2,1,0:T(8,128)(2,1)} %fusion.31), channel_id=1, source_target_pairs={{0,24},{1,25},{2,26},{3,27},{4,28},{5,29},{6,30},{7,31},{8,0},{9,1... | collective-permute-start | bytes 1966088 | tf_op jit(solution)/shard_map/ppermute | solution.py:77
  811.6 49.6 %collective-permute-start.79 = (bf16[4,2,128,1536]{3,2,1,0:T(8,128)(2,1)}, bf16[4,2,128,1536]{3,2,1,0:T(8,128)(2,1)}, u32[]{:S(2)}, u32[]{:S(2)}) collective-permute-start(bf16[4,2,128,1536]{3,2,1,0:T(8,128)(2,1)} %bitcast.140), channel_id=1, source_target_pairs={{0,2},{1,3},{2,0},{3,1},{4,6},{5,7},{6,4},{7,5},{8,10},{9,11},{10,... | collective-permute-start | bytes 9437192 | tf_op jit(solution)/shard_map/ppermute | solution.py:77
  811.6 49.6 %collective-permute-start.78 = (bf16[4,2,128,1024]{3,2,1,0:T(8,128)(2,1)}, bf16[4,2,128,1024]{3,2,1,0:T(8,128)(2,1)}, u32[]{:S(2)}, u32[]{:S(2)}) collective-permute-start(bf16[4,2,128,1024]{3,2,1,0:T(8,128)(2,1)} %bitcast.139), channel_id=1, source_target_pairs={{0,2},{1,3},{2,0},{3,1},{4,6},{5,7},{6,4},{7,5},{8,10},{9,11},{10,... | collective-permute-start | bytes 6291464 | tf_op jit(solution)/shard_map/ppermute | solution.py:77
  918.0 39.0 %collective-permute-start.87 = (bf16[2,128,1536]{2,1,0:T(8,128)(2,1)S(1)}, bf16[2,128,1536]{2,1,0:T(8,128)(2,1)S(1)}, u32[]{:S(2)}, u32[]{:S(2)}) collective-permute-start(bf16[2,128,1536]{2,1,0:T(8,128)(2,1)S(1)} %get-tuple-element.505), channel_id=1, source_target_pairs={{0,24},{1,25},{2,26},{3,27},{4,28},{5,29},{6,30},{7,31},{8,0},{9,1... | collective-permute-start | bytes 2359304 | tf_op jit(solution)/shard_map/ppermute | solution.py:77
  918.2 38.7 %collective-permute-start.88 = (bf16[2,128,1536]{2,1,0:T(8,128)(2,1)S(1)}, bf16[2,128,1536]{2,1,0:T(8,128)(2,1)S(1)}, u32[]{:S(2)}, u32[]{:S(2)}) collective-permute-start(bf16[2,128,1536]{2,1,0:T(8,128)(2,1)S(1)} %get-tuple-element.506), channel_id=1, source_target_pairs={{0,8},{1,9},{2,10},{3,11},{4,12},{5,13},{6,14},{7,15},{8,16},{9,17... | collective-permute-start | bytes 2359304 | tf_op jit(solution)/shard_map/ppermute | solution.py:77
  (218 other events, 4407.3 us)
Sparse Core Ops, SparseCore 0:
  10.8 136.7 all-gather.4
  149.8 95.1 all-gather.6
  266.9 112.9 all-gather.8

commit v3 on v2

--- a/solution.py
+++ b/solution.py
@@ -110,6 +110,7 @@
 class Links:
     def __init__(self):
         self.active = []
+        self.marks = []
 
     def add(self, *jobs):
         places = [[None] for _ in jobs]
@@ -119,24 +120,26 @@
 
     def advance(self, job, place, arrived):
         try:
-            self.active.append((job, place, job.send(arrived)))
+            sends = job.send(arrived)
         except StopIteration as stop:
             place[0] = stop.value
+            return
+        sent = lax.optimization_barrier(tuple(array for array, _ in sends))
+        self.marks += sent
+        moved = [move(array) for (_, move), array in zip(sends, sent)]
+        self.active.append((job, place, moved))
 
     def round(self, work=None, *operands):
-        sending, self.active = self.active, []
-        sent = [array for _, _, sends in sending for array, _ in sends]
+        moving, self.active = self.active, []
         result = None
-        if sent:
-            sent = list(lax.optimization_barrier(tuple(sent)))
-        moves = [move for _, _, sends in sending for _, move in sends]
-        arrived = [move(array) for move, array in zip(moves, sent)]
         if work is not None:
-            result = work(*(after(operands, sent) if sent else operands))
-            arrived, result = lax.optimization_barrier((arrived, result))
-        for job, place, sends in sending:
-            self.advance(job, place, arrived[: len(sends)])
-            arrived = arrived[len(sends) :]
+            result = work(*(after(operands, self.marks) if self.marks else operands))
+            self.marks = jax.tree.leaves(result)[:1]
+        for job, place, moved in moving:
+            if self.marks:
+                moved = after(moved, self.marks)
+            self.marks = []
+            self.advance(job, place, moved)
         return result
 
     def finish(self):
@@ -811,19 +814,6 @@
     grad_output_at = links.add(*weight_grads_jobs(lattice, *chunks))
     grad_router = dot(post_low, grad_logits, 0, 0)
     grad_post_gain = jnp.sum(post_terms, axis=0)
-    (early,) = links.add(
-        reduce_small_job(
-            jnp.concatenate(
-                [
-                    grad_router.reshape(device_count, -1),
-                    grad_post_gain.reshape(device_count, -1),
-                    jnp.zeros((device_count, LANES - sizes[1]), F32),
-                ],
-                axis=1,
-            ).reshape(device_count, -1, LANES)
-        )
-    )
-
     def back_heads(grad_groups, grad_scores):
         grad_value = jnp.einsum(
             "hgqk,qhgd->khd", attend_low, grad_groups, preferred_element_type=F32
@@ -874,31 +864,23 @@
     grad_in_norm, input_terms = norm_back(grad_normed[0], input_scale, input_hat, input_inv)
     grad_input_gain = jnp.sum(input_terms, axis=0)
     grad_inputs = (grad_mid + grad_in_norm).astype(BF16)
-    late_parts = [grad_input_gain, grad_query_gain, grad_key_gain]
-    late_sizes = [sizes[0], sizes[2], sizes[3]]
-    (late,) = links.add(
-        reduce_small_job(
-            jnp.concatenate(
-                [part.reshape(device_count, -1) for part in late_parts]
-                + [jnp.zeros((device_count, LANES - sum(late_sizes)), F32)],
-                axis=1,
-            ).reshape(device_count, 1, LANES)
-        )
-    )
+    late_parts = [grad_router, grad_post_gain, grad_input_gain, grad_query_gain, grad_key_gain]
+    flat = jnp.concatenate([part.reshape(device_count, -1) for part in late_parts], axis=1)
+    flat = jnp.pad(flat, ((0, 0), (0, -flat.shape[1] % LANES)))
+    (late,) = links.add(reduce_small_job(flat.reshape(device_count, -1, LANES)))
     links.finish()
     result = (residual_mid + jnp.concatenate([p[0] for p in out_home], axis=1)).astype(BF16)
-    early, late = early[0].reshape(-1), late[0].reshape(-1)
-    grad_router = early[: router_weight.size].reshape(router_weight.shape)
-    grad_post_gain = early[router_weight.size : router_weight.size + sizes[1]]
     grad_output_w = jnp.concatenate([place[0] for place in grad_output_at], axis=1)
     grad_projections = jnp.concatenate([place[0] for place in grad_projections_at], axis=1).T
     grad_query_w = grad_projections[:query_rows]
     grad_key_w = grad_projections[query_rows : query_rows + key_rows]
     grad_value_w = grad_projections[query_rows + key_rows :]
-    bounds = np.cumsum([0] + late_sizes)
-    grad_input_gain, grad_query_gain, grad_key_gain = (
-        late[bounds[n] : bounds[n + 1]] for n in range(3)
-    )
+    bounds = np.cumsum([0, router_weight.size, sizes[1], sizes[0], sizes[2], sizes[3]])
+    late = late[0].reshape(-1)
+    grad_router, grad_post_gain, grad_input_gain, grad_query_gain, grad_key_gain = (
+        late[bounds[n] : bounds[n + 1]] for n in range(5)
+    )
+    grad_router = grad_router.reshape(router_weight.shape)
     return (
         result,
         grad_inputs,

time: 1000 us -> 916 us (0.916)
  waiting for transfers between devices: 423 us -> 330 us
  local copies, waits for them, and re-layouts: 69.3 us -> 81.6 us
  other arithmetic: 159 us -> 148 us
    ppermute x21 -> x14, waiting for transfers between devices: 105 us -> 15.5 us  [flip(): lax.ppermute(values, BOTH, [(source, source ^ bits) for source in range(c...]
    all_gather x1, waiting for transfers between devices: 99.3 us -> 83.3 us  [on_device(): all_tokens = lax.all_gather(post_low[None], BOTH, axis=0, tiled=True)]
    convert_element_type x30 -> x28, other arithmetic: 68.7 us -> 56.1 us  [piece(): return Pending(*picked).total().astype(BF16)]
    all_gather x1, waiting for transfers between devices: 29.2 us -> 39.4 us  [on_device(): output_full = lax.all_gather(output_held, DP, axis=0, tiled=True)]
    ppermute x21 -> x14, starting transfers between devices: 15.5 us -> 25.2 us  [flip(): lax.ppermute(values, BOTH, [(source, source ^ bits) for source in range(c...]
  transfers between devices with their start and end apart: 102 -> 95, of which waited for: 34 -> 31; matrix products, arithmetic and copies ran while one was open for 22% -> 32% of each run, Pallas kernels for 8% -> 9%
where the time goes in v3:
time: 916 us; the launch traced here: 904 us
  waiting for transfers between devices  330 us (36%)
  other arithmetic  148 us (16%)
  starting transfers between devices  127 us (14%)
  Pallas kernels  125 us (14%)
  local copies, waits for them, and re-layouts  81.6 us (9%)
  matrix products  77.2 us (8%)
  between operations  16.2 us (2%)
    ppermute x74, waiting for transfers between devices, hop(): return lax.ppermute(values, BOTH, pairs)  178 us
    ppermute x74, starting transfers between devices, hop(): return lax.ppermute(values, BOTH, pairs)  97.9 us
    all_gather x1, waiting for transfers between devices, on_device(): all_tokens = lax.all_gather(post_low[None], BOTH, axis=0, tiled=True)  83.3 us
    pallas_call x2, Pallas kernels, expert_grads(): call(perm, first, *[tokens] * STEP_BLOCKS, *grads, position, mask, router...  82.7 us
    convert_element_type x28, other arithmetic, piece(): return Pending(*picked).total().astype(BF16)  56.1 us
    dot_general x3, matrix products, slot_product(): return jnp.einsum('esd,esf->edf', left, right, preferred_element_type=F32)  42 us
    all_gather x1, waiting for transfers between devices, on_device(): output_full = lax.all_gather(output_held, DP, axis=0, tiled=True)  39.4 us
    ppermute x14, starting transfers between devices, flip(): lax.ppermute(values, BOTH, [(source, source ^ bits) for source in range(c...  25.2 us
  transfers between devices with their start and end apart: 95, of which 31 were waited for; matrix products, arithmetic and copies ran while one was open for 32% of the time, Pallas kernels for 9%

profile of v3, /device:TPU:0, one launch (start us, length us, event | category | flops | bytes accessed | tf_op | source)
XLA Modules:
  0.0 904.5 jit_solution(1405241356798424037)
XLA Ops:
  52.9 8.1 collective-permute-start.13
  73.2 12.3 %collective-permute-done.13 = bf16[1,2,1,128,640]{4,3,2,1,0:T(8,128)(2,1)} collective-permute-done((bf16[1,2,1,128,640]{4,3,2,1,0:T(8,128)(2,1)}, bf16[1,2,1,128,640]{4,3,2,1,0:T(8,128)(2,1)}, u32[]{:S(2)}, u32[]{:S(2)}) %collective-permute-start.13) | collective-permute-done | bytes 327712 | tf_op jit(solution)/shard_map/ppermute | solution.py:77
  96.9 6.9 collective-permute-done.10
  114.9 13.0 %collective-permute-done.18 = bf16[1,2,1,128,640]{4,3,2,1,0:T(8,128)(2,1)} collective-permute-done((bf16[1,2,1,128,640]{4,3,2,1,0:T(8,128)(2,1)}, bf16[1,2,1,128,640]{4,3,2,1,0:T(8,128)(2,1)}, u32[]{:S(2)}, u32[]{:S(2)}) %collective-permute-start.18) | collective-permute-done | bytes 327712 | tf_op jit(solution)/shard_map/ppermute | solution.py:77
  131.9 23.3 %collective-permute-done.17 = bf16[1,2,2,128,640]{4,3,2,1,0:T(8,128)(2,1)} collective-permute-done((bf16[1,2,2,128,640]{4,3,2,1,0:T(8,128)(2,1)}, bf16[1,2,2,128,640]{4,3,2,1,0:T(8,128)(2,1)}, u32[]{:S(2)}, u32[]{:S(2)}) %collective-permute-start.17) | collective-permute-done | bytes 655392 | tf_op jit(solution)/shard_map/ppermute | solution.py:77
  196.4 39.4 %all-gather.7.cloned.1.call-done = bf16[2048,2048]{1,0:T(8,128)(2,1)} async-done(((bf16[128,2048]{1,0:T(8,128)(2,1)}), bf16[2048,2048]{1,0:T(8,128)(2,1)}) %all-gather.7.cloned.1.call-update) | async-done | bytes 8388624 | tf_op jit(solution)/shard_map/all_gather | solution.py:651
  244.2 12.6 %collective-permute-done.23 = bf16[128,2048]{1,0:T(8,128)(2,1)} collective-permute-done((bf16[128,2048]{1,0:T(8,128)(2,1)S(1)}, bf16[128,2048]{1,0:T(8,128)(2,1)}, u32[]{:S(2)}, u32[]{:S(2)}) %collective-permute-start.23) | collective-permute-done | bytes 524320 | tf_op jit(solution)/shard_map/ppermute | solution.py:233
  261.2 8.7 copy.496.refs_10_
  290.4 83.3 %all-gather.9.cloned.1.call-done = bf16[4096,2048]{1,0:T(8,128)(2,1)} async-done(((bf16[128,2048]{1,0:T(8,128)(2,1)}), bf16[4096,2048]{1,0:T(8,128)(2,1)}) %all-gather.9.cloned.1.call-update) | async-done | bytes 16777232 | tf_op jit(solution)/shard_map/all_gather | solution.py:741
  373.6 41.3 %expert_grads.2 = (bf16[2,2048,2048]{2,1,0:T(8,128)(2,1)}, bf16[2,2048,2048]{2,1,0:T(8,128)(2,1)}, bf16[2,2048,384]{2,1,0:T(8,128)(2,1)}, bf16[2,2048,384]{2,1,0...) custom-call(s32[16]{0:T(128)} %get-tuple-element.460.perm, ...), custom_call_target="tpu_custom_call" | custom-call | flops 25769803776 | bytes 50331648 | tf_op jit(solution)/shard_map/expert_grads/pallas_call | solution.py:420
  417.1 41.4 %expert_grads.3 = (bf16[2,2048,2048]{2,1,0:T(8,128)(2,1)}, bf16[2,2048,2048]{2,1,0:T(8,128)(2,1)}, bf16[2,2048,384]{2,1,0:T(8,128)(2,1)}, bf16[2,2048,384]{2,1,0...) custom-call(s32[16]{0:T(128)} %get-tuple-element.464.perm, ...), custom_call_target="tpu_custom_call", output_to_operand_aliasing={{0}: (15, {}), {1}: (16, {}), {2}: (17, {}), {3}: (18, {}),... | custom-call | flops 25769803776 | bytes 50331648 | tf_op jit(solution)/shard_map/expert_grads/pallas_call | solution.py:420
  473.5 10.8 %expert_outputs.3 = (bf16[16,128,768]{2,1,0:T(8,128)(2,1)}, bf16[16,128,768]{2,1,0:T(8,128)(2,1)}, bf16[16,128,512]{2,1,0:T(8,128)(2,1)}) custom-call(bf16[2,2048,384]{2,1,0:T(8,128)(2,1)} %get-tuple-element.248.gated_ref, f32[16,2,128]{2,1,0:T(2,128)} %gather_fusion.2, bf16[2,384,2048]{2,1,0:T(8,128)(2,1)} %down_ref.3), custom_call_target="tpu_custom_call" | custom-call | flops 4294967296 | bytes 16777216 | tf_op jit(solution)/shard_map/expert_outputs/pallas_call | solution.py:469
  491.2 10.6 %expert_outputs.2 = (bf16[16,128,768]{2,1,0:T(8,128)(2,1)}, bf16[16,128,768]{2,1,0:T(8,128)(2,1)}, bf16[16,128,512]{2,1,0:T(8,128)(2,1)}) custom-call(bf16[2,2048,384]{2,1,0:T(8,128)(2,1)} %get-tuple-element.248.gated_ref, f32[16,2,128]{2,1,0:T(2,128)} %gather_fusion, bf16[2,384,2048]{2,1,0:T(8,128)(2,1)} %down_ref.3), custom_call_target="tpu_custom_call" | custom-call | flops 4294967296 | bytes 16777216 | tf_op jit(solution)/shard_map/expert_outputs/pallas_call | solution.py:469
  519.5 14.2 %fusion.194 = f32[2,2048,384]{2,1,0:T(8,128)} fusion(bf16[2,2048,2048]{2,1,0:T(8,128)(2,1)} %get-tuple-element.258, bf16[2,2048,384]{2,1,0:T(8,128)(2,1)S(1)} %copy-done.41), kind=kOutput, calls=%fused_computation.471 | convolution fusion | flops 6442450944 | bytes 26214400 | tf_op jit(solution)/shard_map/esd,esf->edf/dot_general | solution.py:767
  543.5 10.3 %collective-permute-done.37 = bf16[2,2,128,640]{3,2,1,0:T(8,128)(2,1)S(1)} collective-permute-done((bf16[2,2,128,640]{3,2,1,0:T(8,128)(2,1)}, bf16[2,2,128,640]{3,2,1,0:T(8,128)(2,1)S(1)}, u32[]{:S(2)}, u32[]{:S(2)}) %collective-permute-start.37) | collective-permute-done | bytes 655392 | tf_op jit(solution)/shard_map/ppermute | solution.py:77
  556.0 12.5 %fusion.195 = f32[2,384,2048]{2,1,0:T(8,128)} fusion(bf16[2,2048,384]{2,1,0:T(8,128)(2,1)S(1)} %copy-done.40, bf16[2,2048,2048]{2,1,0:T(8,128)(2,1)} %get-tuple-element.249), kind=kOutput, calls=%fused_computation.472 | convolution fusion | flops 6442450944 | bytes 26214400 | tf_op jit(solution)/shard_map/esd,esf->edf/dot_general | solution.py:767
  602.0 15.3 %fusion.196 = f32[2,2048,384]{2,1,0:T(8,128)} fusion(bf16[2,2048,2048]{2,1,0:T(8,128)(2,1)} %get-tuple-element.258, bf16[2,2048,384]{2,1,0:T(8,128)(2,1)} %get-tuple-element.259), kind=kOutput, calls=%fused_computation.473 | convolution fusion | flops 6442450944 | bytes 26214400 | tf_op jit(solution)/shard_map/esd,esf->edf/dot_general | solution.py:767
  649.9 7.0 fusion.3
  692.6 7.8 collective-permute-done.57
  760.4 6.8 fusion.197
  767.5 24.7 %collective-permute-done.60 = bf16[128,768]{1,0:T(8,128)(2,1)S(1)} collective-permute-done((bf16[128,768]{1,0:T(8,128)(2,1)S(1)}, bf16[128,768]{1,0:T(8,128)(2,1)S(1)}, u32[]{:S(2)}, u32[]{:S(2)}) %collective-permute-start.60) | collective-permute-done | bytes 196640 | tf_op jit(solution)/shard_map/ppermute | solution.py:77
  811.4 16.3 %collective-permute-done.75 = bf16[4,128,1024]{2,1,0:T(8,128)(2,1)S(1)} collective-permute-done((bf16[4,128,1024]{2,1,0:T(8,128)(2,1)S(1)}, bf16[4,128,1024]{2,1,0:T(8,128)(2,1)S(1)}, u32[]{:S(2)}, u32[]{:S(2)}) %collective-permute-start.75) | collective-permute-done | bytes 1048608 | tf_op jit(solution)/shard_map/ppermute | solution.py:77
  845.3 10.6 %collective-permute-start.78 = (f32[8,18,128]{2,0,1:T(8,128)S(1)}, f32[8,18,128]{2,0,1:T(8,128)S(1)}, u32[]{:S(2)}, u32[]{:S(2)}) collective-permute-start(f32[8,18,128]{2,0,1:T(8,128)S(1)} %get-tuple-element.317), channel_id=1, source_target_pairs={{0,24},{1,25},{2,26},{3,27},{4,28},{5,29},{6,30},{7,31},{8,16},{9,... | collective-permute-start | bytes 221192 | tf_op jit(solution)/shard_map/ppermute | solution.py:193
  857.2 14.5 %collective-permute-done.79 = bf16[2,128,1536]{2,1,0:T(8,128)(2,1)} collective-permute-done((bf16[2,128,1536]{2,1,0:T(8,128)(2,1)}, bf16[2,128,1536]{2,1,0:T(8,128)(2,1)}, u32[]{:S(2)}, u32[]{:S(2)}) %collective-permute-start.79) | collective-permute-done | bytes 786464 | tf_op jit(solution)/shard_map/ppermute | solution.py:77
  (654 shorter events, 436.5 us)
Async XLA Ops:
  7.3 152.1 %all-gather.5.cloned.1.call-start = ((), (), s32[]{:S(2)}) async-start(), calls=%async_computation | async-start | bytes 11141120 | tf_op jit(solution)/shard_map/all_gather | solution.py:613
  9.4 226.4 %all-gather.7.cloned.1.call-start = ((), (), s32[]{:S(2)}) async-start(), calls=%async_computation.1 | async-start | bytes 8912896 | tf_op jit(solution)/shard_map/all_gather | solution.py:651
  10.1 363.5 %all-gather.9.cloned.1.call-start = ((), (), s32[]{:S(2)}) async-start(), calls=%async_computation.2 | async-start | bytes 17301504 | tf_op jit(solution)/shard_map/all_gather | solution.py:741
  36.7 53.4 %collective-permute-start = (bf16[128,2048]{1,0:T(8,128)(2,1)S(1)}, bf16[128,2048]{1,0:T(8,128)(2,1)S(1)}, u32[]{:S(2)}, u32[]{:S(2)}) collective-permute-start(bf16[128,2048]{1,0:T(8,128)(2,1)S(1)} %copy-done.3), channel_id=1, source_target_pairs={{0,1},{1,0},{2,3},{3,2},{4,5},{5,4},{6,7},{7,6},{8,9},{9,8},{10,11... | collective-permute-start | bytes 1572872 | tf_op jit(solution)/shard_map/ppermute | solution.py:233
  64.3 39.4 %collective-permute-start.10 = (bf16[16,50,128]{2,0,1:T(8,128)(2,1)}, bf16[16,50,128]{2,0,1:T(8,128)(2,1)}, u32[]{:S(2)}, u32[]{:S(2)}) collective-permute-start(bf16[16,50,128]{2,0,1:T(8,128)(2,1)} %constant_dynamic-slice_fusion.5), channel_id=1, source_target_pairs={{0,16},{1,17},{2,18},{3,19},{4,20},{5,21},{6,22},{7,23},{8,24},{9,... | collective-permute-start | bytes 614408 | tf_op jit(solution)/shard_map/ppermute | solution.py:193
  71.7 39.0 %collective-permute-start.19 = (bf16[4,1,1,128,768]{4,3,2,1,0:T(8,128)(2,1)}, bf16[4,1,1,128,768]{4,3,2,1,0:T(8,128)(2,1)S(1)}, u32[]{:S(2)}, u32[]{:S(2)}) collective-permute-start(bf16[4,1,1,128,768]{4,3,2,1,0:T(8,128)(2,1)} %pad_maximum_fusion.8), channel_id=1, source_target_pairs={{0,1},{1,0},{2,3},{3,2},{4,5},{5,4},{6,7},{7,6},{8,9},{9,8},{10,11... | collective-permute-start | bytes 2359304 | tf_op jit(solution)/shard_map/ppermute | solution.py:77
  85.5 42.4 %collective-permute-start.18 = (bf16[1,2,1,128,640]{4,3,2,1,0:T(8,128)(2,1)}, bf16[1,2,1,128,640]{4,3,2,1,0:T(8,128)(2,1)}, u32[]{:S(2)}, u32[]{:S(2)}) collective-permute-start(bf16[1,2,1,128,640]{4,3,2,1,0:T(8,128)(2,1)} %collective-permute-done.13), channel_id=1, source_target_pairs={{0,24},{1,25},{2,26},{3,27},{4,28},{5,29},{6,30},{7,31},{8,0},{9,1... | collective-permute-start | bytes 983048 | tf_op jit(solution)/shard_map/ppermute | solution.py:77
  88.3 43.5 %collective-permute-start.16 = (bf16[1,2,2,128,640]{4,3,2,1,0:T(8,128)(2,1)}, bf16[1,2,2,128,640]{4,3,2,1,0:T(8,128)(2,1)}, u32[]{:S(2)}, u32[]{:S(2)}) collective-permute-start(bf16[1,2,2,128,640]{4,3,2,1,0:T(8,128)(2,1)} %pad_maximum_fusion.9), channel_id=1, source_target_pairs={{0,8},{1,9},{2,10},{3,11},{4,12},{5,13},{6,14},{7,15},{8,16},{9,17... | collective-permute-start | bytes 1966088 | tf_op jit(solution)/shard_map/ppermute | solution.py:77
  90.1 65.2 %collective-permute-start.17 = (bf16[1,2,2,128,640]{4,3,2,1,0:T(8,128)(2,1)}, bf16[1,2,2,128,640]{4,3,2,1,0:T(8,128)(2,1)}, u32[]{:S(2)}, u32[]{:S(2)}) collective-permute-start(bf16[1,2,2,128,640]{4,3,2,1,0:T(8,128)(2,1)} %pad_maximum_fusion.9), channel_id=1, source_target_pairs={{0,24},{1,25},{2,26},{3,27},{4,28},{5,29},{6,30},{7,31},{8,0},{9,1... | collective-permute-start | bytes 1966088 | tf_op jit(solution)/shard_map/ppermute | solution.py:77
  113.5 59.2 %collective-permute-start.22 = (bf16[4,1,2,128,768]{4,3,2,1,0:T(8,128)(2,1)}, bf16[4,1,2,128,768]{4,3,2,1,0:T(8,128)(2,1)}, u32[]{:S(2)}, u32[]{:S(2)}) collective-permute-start(bf16[4,1,2,128,768]{4,3,2,1,0:T(8,128)(2,1)} %pad_maximum_fusion.4), channel_id=1, source_target_pairs={{0,4},{1,5},{2,6},{3,7},{4,0},{5,1},{6,2},{7,3},{8,12},{9,13},{10,... | collective-permute-start | bytes 4718600 | tf_op jit(solution)/shard_map/ppermute | solution.py:77
  130.3 45.4 %collective-permute-start.21 = (bf16[4,2,1,128,640]{4,3,2,1,0:T(8,128)(2,1)}, bf16[4,2,1,128,640]{4,3,2,1,0:T(8,128)(2,1)}, u32[]{:S(2)}, u32[]{:S(2)}) collective-permute-start(bf16[4,2,1,128,640]{4,3,2,1,0:T(8,128)(2,1)} %pad_maximum_fusion.5), channel_id=1, source_target_pairs={{0,1},{1,0},{2,3},{3,2},{4,5},{5,4},{6,7},{7,6},{8,9},{9,8},{10,11... | collective-permute-start | bytes 3932168 | tf_op jit(solution)/shard_map/ppermute | solution.py:77
  415.0 48.9 %collective-permute-start.27 = (bf16[16,128,768]{2,1,0:T(8,128)(2,1)}, bf16[16,128,768]{2,1,0:T(8,128)(2,1)}, u32[]{:S(2)}, u32[]{:S(2)}) collective-permute-start(bf16[16,128,768]{2,1,0:T(8,128)(2,1)} %get-tuple-element.221), channel_id=1, source_target_pairs={{0,2},{1,3},{2,0},{3,1},{4,6},{5,7},{6,4},{7,5},{8,10},{9,11},{10,... | collective-permute-start | bytes 9437192 | tf_op jit(solution)/shard_map/ppermute | solution.py:77
  415.6 42.9 %collective-permute-start.29 = (bf16[16,128,640]{2,1,0:T(8,128)(2,1)}, bf16[16,128,640]{2,1,0:T(8,128)(2,1)}, u32[]{:S(2)}, u32[]{:S(2)}) collective-permute-start(bf16[16,128,640]{2,1,0:T(8,128)(2,1)} %get-tuple-element.225), channel_id=1, source_target_pairs={{0,2},{1,3},{2,0},{3,1},{4,6},{5,7},{6,4},{7,5},{8,10},{9,11},{10,... | collective-permute-start | bytes 7864328 | tf_op jit(solution)/shard_map/ppermute | solution.py:77
  416.6 53.3 %collective-permute-start.28 = (bf16[16,128,768]{2,1,0:T(8,128)(2,1)}, bf16[16,128,768]{2,1,0:T(8,128)(2,1)}, u32[]{:S(2)}, u32[]{:S(2)}) collective-permute-start(bf16[16,128,768]{2,1,0:T(8,128)(2,1)} %get-tuple-element.223), channel_id=1, source_target_pairs={{0,2},{1,3},{2,0},{3,1},{4,6},{5,7},{6,4},{7,5},{8,10},{9,11},{10,... | collective-permute-start | bytes 9437192 | tf_op jit(solution)/shard_map/ppermute | solution.py:77
  463.0 52.4 %collective-permute-start.33 = (bf16[2,2,128,640]{3,2,1,0:T(8,128)(2,1)}, bf16[2,2,128,640]{3,2,1,0:T(8,128)(2,1)}, u32[]{:S(2)}, u32[]{:S(2)}) collective-permute-start(bf16[2,2,128,640]{3,2,1,0:T(8,128)(2,1)} %bitcast.34), channel_id=1, source_target_pairs={{0,8},{1,9},{2,10},{3,11},{4,12},{5,13},{6,14},{7,15},{8,16},{9,17... | collective-permute-start | bytes 1966088 | tf_op jit(solution)/shard_map/ppermute | solution.py:77
  488.3 129.0 %collective-permute-start.30 = (bf16[4,2,2,128,768]{4,3,2,0,1:T(8,128)(2,1)}, bf16[4,2,2,128,768]{4,3,2,0,1:T(8,128)(2,1)}, u32[]{:S(2)}, u32[]{:S(2)}) collective-permute-start(bf16[4,2,2,128,768]{4,3,2,0,1:T(8,128)(2,1)} %copy.502), channel_id=1, source_target_pairs={{0,2},{1,3},{2,0},{3,1},{4,6},{5,7},{6,4},{7,5},{8,10},{9,11},{10,... | collective-permute-start | bytes 9437192 | tf_op jit(solution)/shard_map/ppermute | solution.py:77
  533.7 89.4 %collective-permute-start.49 = (bf16[4,2,2,128,768]{4,3,1,2,0:T(8,128)(2,1)}, bf16[4,2,2,128,768]{4,3,1,2,0:T(8,128)(2,1)}, u32[]{:S(2)}, u32[]{:S(2)}) collective-permute-start(bf16[4,2,2,128,768]{4,3,1,2,0:T(8,128)(2,1)} %copy.514), channel_id=1, source_target_pairs={{0,2},{1,3},{2,0},{3,1},{4,6},{5,7},{6,4},{7,5},{8,10},{9,11},{10,... | collective-permute-start | bytes 9437192 | tf_op jit(solution)/shard_map/ppermute | solution.py:77
  569.7 58.8 %collective-permute-start.48 = (bf16[4,2,2,128,512]{4,3,2,1,0:T(8,128)(2,1)}, bf16[4,2,2,128,512]{4,3,2,1,0:T(8,128)(2,1)}, u32[]{:S(2)}, u32[]{:S(2)}) collective-permute-start(bf16[4,2,2,128,512]{4,3,2,1,0:T(8,128)(2,1)} %bitcast.38), channel_id=1, source_target_pairs={{0,2},{1,3},{2,0},{3,1},{4,6},{5,7},{6,4},{7,5},{8,10},{9,11},{10,... | collective-permute-start | bytes 6291464 | tf_op jit(solution)/shard_map/ppermute | solution.py:77
  644.5 58.4 %collective-permute-start.55 = (bf16[4,2,128,768]{3,2,1,0:T(8,128)(2,1)}, bf16[4,2,128,768]{3,2,1,0:T(8,128)(2,1)}, u32[]{:S(2)}, u32[]{:S(2)}) collective-permute-start(bf16[4,2,128,768]{3,2,1,0:T(8,128)(2,1)} %bitcast.649), channel_id=1, source_target_pairs={{0,2},{1,3},{2,0},{3,1},{4,6},{5,7},{6,4},{7,5},{8,10},{9,11},{10,... | collective-permute-start | bytes 4718600 | tf_op jit(solution)/shard_map/ppermute | solution.py:77
  644.5 62.3 %collective-permute-start.54 = (bf16[4,2,128,1280]{3,2,1,0:T(8,128)(2,1)}, bf16[4,2,128,1280]{3,2,1,0:T(8,128)(2,1)}, u32[]{:S(2)}, u32[]{:S(2)}) collective-permute-start(bf16[4,2,128,1280]{3,2,1,0:T(8,128)(2,1)} %bitcast.647), channel_id=1, source_target_pairs={{0,2},{1,3},{2,0},{3,1},{4,6},{5,7},{6,4},{7,5},{8,10},{9,11},{10,... | collective-permute-start | bytes 7864328 | tf_op jit(solution)/shard_map/ppermute | solution.py:77
  681.8 39.1 %collective-permute-start.53 = (bf16[128,768]{1,0:T(8,128)(2,1)}, bf16[128,768]{1,0:T(8,128)(2,1)}, u32[]{:S(2)}, u32[]{:S(2)}) collective-permute-start(bf16[128,768]{1,0:T(8,128)(2,1)} %get-tuple-element.517), channel_id=1, source_target_pairs={{0,8},{1,9},{2,10},{3,11},{4,12},{5,13},{6,14},{7,15},{8,16},{9,17... | collective-permute-start | bytes 589832 | tf_op jit(solution)/shard_map/ppermute | solution.py:77
  742.7 54.4 %collective-permute-start.70 = (bf16[4,2,128,1024]{3,2,1,0:T(8,128)(2,1)}, bf16[4,2,128,1024]{3,2,1,0:T(8,128)(2,1)S(1)}, u32[]{:S(2)}, u32[]{:S(2)}) collective-permute-start(bf16[4,2,128,1024]{3,2,1,0:T(8,128)(2,1)} %bitcast.648), channel_id=1, source_target_pairs={{0,2},{1,3},{2,0},{3,1},{4,6},{5,7},{6,4},{7,5},{8,10},{9,11},{10,... | collective-permute-start | bytes 6291464 | tf_op jit(solution)/shard_map/ppermute | solution.py:77
  744.6 55.0 %collective-permute-start.69 = (bf16[4,2,128,1536]{3,2,1,0:T(8,128)(2,1)}, bf16[4,2,128,1536]{3,2,1,0:T(8,128)(2,1)S(1)}, u32[]{:S(2)}, u32[]{:S(2)}) collective-permute-start(bf16[4,2,128,1536]{3,2,1,0:T(8,128)(2,1)} %bitcast.646), channel_id=1, source_target_pairs={{0,2},{1,3},{2,0},{3,1},{4,6},{5,7},{6,4},{7,5},{8,10},{9,11},{10,... | collective-permute-start | bytes 9437192 | tf_op jit(solution)/shard_map/ppermute | solution.py:77
  796.2 39.9 %collective-permute-start.68 = (bf16[128,2048]{1,0:T(8,128)(2,1)S(1)}, bf16[128,2048]{1,0:T(8,128)(2,1)S(1)}, u32[]{:S(2)}, u32[]{:S(2)}) collective-permute-start(bf16[128,2048]{1,0:T(8,128)(2,1)S(1)} %dynamic-slice_bitcast_fusion), channel_id=1, source_target_pairs={{0,1},{1,0},{2,3},{3,2},{4,5},{5,4},{6,7},{7,6},{8,9},{9,8},{10,11... | collective-permute-start | bytes 1572872 | tf_op jit(solution)/shard_map/ppermute | solution.py:233
  (202 other events, 4068.2 us)
Sparse Core Ops, SparseCore 0:
  10.8 142.9 all-gather.4
  155.9 79.7 all-gather.6
  260.7 112.9 all-gather.8

commit v4 on v3

--- a/solution.py
+++ b/solution.py
@@ -6,6 +6,7 @@
 import numpy as np
 from jax import lax
 from jax.experimental import pallas as pl
+from jax.experimental.layout import Layout, with_layout_constraint
 from jax.experimental.pallas import tpu as pltpu
 from jax.sharding import PartitionSpec as P
 
@@ -112,13 +113,13 @@
         self.active = []
         self.marks = []
 
-    def add(self, *jobs):
+    def add(self, *jobs, rank=0):
         places = [[None] for _ in jobs]
         for job, place in zip(jobs, places):
-            self.advance(job, place, None)
+            self.advance(rank, job, place, None)
         return places
 
-    def advance(self, job, place, arrived):
+    def advance(self, rank, job, place, arrived):
         try:
             sends = job.send(arrived)
         except StopIteration as stop:
@@ -127,24 +128,29 @@
         sent = lax.optimization_barrier(tuple(array for array, _ in sends))
         self.marks += sent
         moved = [move(array) for (_, move), array in zip(sends, sent)]
-        self.active.append((job, place, moved))
+        self.active.append((rank, job, place, moved))
 
     def round(self, work=None, *operands):
-        moving, self.active = self.active, []
+        moving, self.active = sorted(self.active, key=lambda entry: entry[0]), []
         result = None
         if work is not None:
             result = work(*(after(operands, self.marks) if self.marks else operands))
             self.marks = jax.tree.leaves(result)[:1]
-        for job, place, moved in moving:
+        for rank, job, place, moved in moving:
             if self.marks:
                 moved = after(moved, self.marks)
             self.marks = []
-            self.advance(job, place, moved)
+            self.advance(rank, job, place, moved)
         return result
 
     def finish(self):
         while self.active:
             self.round()
+
+    def aside(self, main):
+        self.marks = main.marks
+        self.round()
+        main.marks = self.marks
 
 
 def mover(axis, step=1):
@@ -172,10 +178,10 @@
     return pending.total()
 
 
-def spread_job(own, order, turn):
-    pieces = own[None, None, None]
+def spread_job(own, axes, order, turn):
+    pieces = own.reshape((1,) * len(axes) + own.shape)
     for axis in order:
-        dim = ("z", "x", "y").index(axis)
+        dim = axes.index(axis)
         if axis == "z":
             near = yield [(pieces, mover("z", 1)), (pieces, mover("z", -1))]
             (far,) = yield [(near[0 if turn == 1 else 1], mover("z", turn))]
@@ -186,6 +192,15 @@
     flat = pieces.reshape((-1,) + own.shape)
     (partner,) = yield [(flat, mover("core"))]
     return partner, flat
+
+
+def spread_jobs(own, cuts, axes, orders):
+    groups = jnp.split(own, cuts, axis=1)
+    return [spread_job(*job) for job in zip(groups, [axes] * len(groups), orders, TURNS)]
+
+
+def gathered_groups(places):
+    return [[place[0][half] for place in places] for half in range(2)]
 
 
 def flip(bits):
@@ -262,45 +277,46 @@
     return picks
 
 
-def expert_kernel(capacity, widths, grad_groups, carried, perm, first, *refs):
+def expert_kernel(capacity, widths, token_groups, grad_groups, carried, first, *refs):
     blocks = STEP_BLOCKS
-    token_refs, grad_refs, refs = (
-        refs[:blocks],
-        refs[blocks : blocks + grad_groups],
-        refs[blocks + grad_groups :],
-    )
+    groups = token_groups + grad_groups
+    token_refs, grad_refs, refs = refs[:token_groups], refs[token_groups:groups], refs[groups:]
     position_ref, mask_ref, router_ref, up_ref, up_t_ref, down_t_ref = refs[:6]
     refs = refs[6 + carried :]
     rows_ref, grad_rows_ref, gated_ref, grad_gate_ref, grad_up_ref = refs[:5]
     out_refs, packed_ref = refs[5:-1], refs[-1]
     experts_here = up_ref.shape[0]
     hidden_units = down_t_ref.shape[2]
-    width = token_refs[0].shape[2]
+    width = sum(ref.shape[2] for ref in token_refs)
     first_expert = first[0]
     gates = [[] for _ in range(experts_here)]
     choices = []
     for j in range(blocks):
-        tokens = token_refs[j][0]
         picks = choose(position_ref[j], capacity)
         choice = jnp.concatenate(picks, axis=0).astype(BF16)
         choices.append(choice)
-        rows = dot(choice, tokens).astype(BF16)
-        grad_rows = [dot(choice, grad_ref[j]).astype(BF16) for grad_ref in grad_refs]
-        logits = dot(router_ref[...], tokens, 1, 1)
+        here = slice(j * capacity, (j + 1) * capacity)
+        for group_refs, kept_ref in ((token_refs, rows_ref), (grad_refs, grad_rows_ref)):
+            start = 0
+            for ref in group_refs:
+                size = ref.shape[2]
+                picked = dot(choice, ref[j]).astype(BF16)
+                for e in range(experts_here):
+                    kept_ref[e, here, start : start + size] = picked[
+                        e * capacity : (e + 1) * capacity
+                    ]
+                start += size
+        logits, start = 0.0, 0
+        for ref in token_refs:
+            size = ref.shape[2]
+            logits = logits + dot(router_ref[:, start : start + size], ref[j], 1, 1)
+            start += size
         chosen = mask_ref[j].astype(F32) > 0.5
         top = jnp.max(jnp.where(chosen, logits, -3e38), axis=0, keepdims=True)
         powers = jnp.where(chosen, jnp.exp(jnp.minimum(logits - top, 0.0)), 0.0)
         gate_all = powers / jnp.sum(powers, axis=0, keepdims=True)
         expert_number = lax.broadcasted_iota(jnp.int32, gate_all.shape, 0)
         for e in range(experts_here):
-            here = slice(j * capacity, (j + 1) * capacity)
-            rows_ref[e, here, :] = rows[e * capacity : (e + 1) * capacity]
-            start = 0
-            for group in grad_rows:
-                grad_rows_ref[e, here, start : start + group.shape[1]] = group[
-                    e * capacity : (e + 1) * capacity
-                ]
-                start += group.shape[1]
             gate_row = jnp.sum(
                 jnp.where(expert_number == first_expert + e, gate_all, 0.0), axis=0, keepdims=True
             )
@@ -344,12 +360,6 @@
             start += size
 
 
-def block_spec(width, place):
-    return pl.BlockSpec(
-        (1, LANES, width), lambda i, perm, first: (perm[i * STEP_BLOCKS + place], 0, 0)
-    )
-
-
 def whole(shape):
     return pl.BlockSpec(
         shape, lambda i, *scalars: (0,) * len(shape), pipeline_mode=pl.Buffered(1)
@@ -363,11 +373,11 @@
 
 
 def expert_grads(
-    half, carry, perm, first, tokens, grads, grad_start, position, mask,
+    half, carry, first, tokens, grads, block_start, position, mask,
     router_t, up_both, up_both_t, down_t, capacity, widths,
 ):
-    count = perm.shape[0]
-    width = tokens.shape[2]
+    count = position.shape[0]
+    width = sum(group.shape[2] for group in tokens)
     experts_here, hidden_units = down_t.shape[0], down_t.shape[2]
     slots = STEP_BLOCKS * capacity
     expert_count = router_t.shape[0]
@@ -376,20 +386,21 @@
     slot_spec = lambda size: pl.BlockSpec(
         (experts_here, slots, size), lambda i, *scalars: (0, i + half * steps, 0)
     )
-    before = 2 + STEP_BLOCKS + len(grads) + 6
+    before = 1 + len(tokens) + len(grads) + 6
     flops = 2 * count * capacity * experts_here * (7 * hidden_units * width + 3 * LANES * width)
     call = pl.pallas_call(
-        functools.partial(expert_kernel, capacity, widths, len(grads), len(carry)),
+        functools.partial(
+            expert_kernel, capacity, widths, len(tokens), len(grads), len(carry)
+        ),
         grid_spec=pltpu.PrefetchScalarGridSpec(
-            num_scalar_prefetch=2,
-            grid=(count // STEP_BLOCKS,),
-            in_specs=[block_spec(width, j) for j in range(STEP_BLOCKS)]
-            + [
+            num_scalar_prefetch=1,
+            grid=(steps,),
+            in_specs=[
                 pl.BlockSpec(
                     (STEP_BLOCKS, LANES, group.shape[2]),
-                    lambda i, *scalars: (i + grad_start // STEP_BLOCKS, 0, 0),
+                    lambda i, *scalars: (i + block_start // STEP_BLOCKS, 0, 0),
                 )
-                for group in grads
+                for group in (*tokens, *grads)
             ]
             + [
                 stepped((STEP_BLOCKS, experts_here, LANES), 0),
@@ -418,7 +429,7 @@
         name="expert_grads",
     )
     return call(
-        perm, first, *([tokens] * STEP_BLOCKS), *grads,
+        first, *tokens, *grads,
         position, mask, router_t, up_both, up_both_t, down_t, *carry,
     )
 
@@ -529,7 +540,8 @@
 
 TOKEN_ORDERS = (("x", "y", "z"), ("y", "z", "x"), ("z", "x", "y"))
 GATHER_ORDERS = (("z", "y", "x"), ("x", "z", "y"), ("y", "x", "z"))
-CHUNK_ORDERS = (("x", "z"), ("z", "x"))
+PROJECTION_ORDERS = (("x", "z"), ("z", "x"))
+OUTPUT_ORDERS = (("x", "z"),)
 TURNS = (1, -1, 1)
 
 
@@ -568,11 +580,11 @@
     return tuple(chunk_products(order, left, right, widths) for order in chunk_orders())
 
 
-def weight_grads_jobs(lattice, first, second):
+def weight_grads_jobs(lattice, first, second, orders):
     if not lattice:
         return [product_job(first, second)]
     jobs = []
-    for n, order in enumerate(CHUNK_ORDERS):
+    for n, order in enumerate(orders):
         shape = (4, 2) + first[n].shape[1:]
         jobs.append(
             home_job(first[n].reshape(shape), second[n].reshape(shape), "zx", order, TURNS[n])
@@ -605,12 +617,11 @@
     experts_here = gate_weight.shape[0]
     capacity = 2 * row_count * routes.shape[1] // experts
 
-    links = Links()
+    links, slow = Links(), Links()
     projections = jnp.concatenate(
         [query_weight, key_projection_matrix, value_projection_matrix], axis=0
     )
     query_rows, key_rows = query_weight.shape[0], key_projection_matrix.shape[0]
-    projections_full = lax.all_gather(projections, DP, axis=1, tiled=True)
 
     expert_ids = jnp.arange(experts, dtype=jnp.int32)
     chosen_mask = jnp.any(routes[:, :, None] == expert_ids[None, None, :], axis=1)
@@ -629,32 +640,25 @@
         axis=0,
     )
     gathered_at, other_inputs_at = links.add(gather_small_job(payload), swap_job(inputs))
+    projections_full = lax.all_gather(projections.T, DP, axis=0, tiled=True)
     if lattice:
         cuts = (width // 8 * 3, width // 16 * 11)
-        grad_at = links.add(
-            *(
-                spread_job(group, order, turn)
-                for group, order, turn in zip(
-                    jnp.split(cotangent, cuts, axis=1), GATHER_ORDERS, TURNS
-                )
-            )
-        )
+        grads_at = links.add(*spread_jobs(cotangent, cuts, "zxy", GATHER_ORDERS))
 
     def join_up(gate, up):
         return jnp.concatenate([gate, up], axis=2)
 
     def turn_last(values):
-        return jnp.swapaxes(values, 1, 2)
+        return with_layout_constraint(jnp.swapaxes(values, 1, 2), Layout((0, 1, 2)))
 
     up_both = links.round(join_up, gate_weight, up_weight)
     output_held = after(output_weight, up_both[0, :8, :LANES])
     output_full = lax.all_gather(output_held, DP, axis=0, tiled=True)
     up_both_t = links.round(turn_last, up_both)
     down_t = links.round(turn_last, down_weight)
-    other_inputs, gathered = other_inputs_at[0], None
     while gathered_at[0] is None:
         links.round()
-    gathered = gathered_at[0]
+    gathered, other_inputs = gathered_at[0], other_inputs_at[0]
 
     router_full = gathered[:, :router_lines].reshape(width, experts)
     flat_all = gathered[:, router_lines : router_lines + padded // LANES].reshape(
@@ -687,8 +691,8 @@
     cosine, sine = cosine_table[:, None, :], sine_table[:, None, :]
     score_scale = 1.0 / math.sqrt(HEAD_SIZE)
 
-    def attention(projections_full):
-        projected = dot(sequence, projections_full, 1, 1)
+    def project(projections_full):
+        projected = dot(sequence, projections_full)
         query_raw = projected[:, :query_rows].reshape(seq_len, local_heads, HEAD_SIZE)
         key_raw = projected[:, query_rows : query_rows + key_rows].reshape(
             seq_len, local_groups, HEAD_SIZE
@@ -703,6 +707,9 @@
         key_norm, key_hat, key_inv = norm_rows(key_raw, key_scale)
         key_low = (key_norm * cosine + rotate_half(key_norm) * sine).astype(BF16)
         query_groups = query_low.reshape(seq_len, local_groups, per_group, HEAD_SIZE)
+        return query_groups, query_hat, query_inv, key_hat, key_inv, key_low, value_low
+
+    def attention(query_groups, key_low, value_low):
         scores = (
             jnp.einsum("qhgd,khd->hgqk", query_groups, key_low, preferred_element_type=F32)
             * score_scale
@@ -716,29 +723,34 @@
             .astype(BF16)
             .reshape(seq_len, query_rows)
         )
-        return (
-            query_hat, query_inv, query_groups, key_hat, key_inv, key_low, value_low,
-            attend, attend_low, mixed_low, projections_full,
-        )
-
-    (
-        query_hat, query_inv, query_groups, key_hat, key_inv, key_low, value_low,
-        attend, attend_low, mixed_low, projections_full,
-    ) = links.round(attention, projections_full)
-    mixed_out = links.round(lambda mixed: dot(mixed, output_full, 1, 1), mixed_low)
+        return mixed_low, attend, attend_low
+
+    query_groups, query_hat, query_inv, key_hat, key_inv, key_low, value_low = links.round(
+        project, projections_full
+    )
+    mixed_low, attend, attend_low = links.round(attention, query_groups, key_low, value_low)
     links.finish()
-    if lattice:
-        all_grads = [[place[0][n] for place in grad_at] for n in range(2)]
-        grad_starts = (0, 0)
-    else:
-        all_grads = ([lax.all_gather(cotangent[None], BOTH, axis=0, tiled=True)],) * 2
-        grad_starts = (0, device_count // 2)
+    ready = (positions, masks, router_t, up_both, up_both_t, down_t)
+    mixed_low, (positions, masks, router_t, up_both, up_both_t, down_t) = (
+        lax.optimization_barrier((mixed_low, ready))
+    )
+    mixed_out = dot(after(mixed_low, links.marks), output_full, 1, 1)
     (mixed_home,) = links.add(sum_tokens_job(mixed_out))
     links.finish()
     residual_mid = residual_in + mixed_home[0]
     post_norm, post_hat, post_inv = norm_rows(residual_mid, post_scale)
     post_low = post_norm.astype(BF16)
-    all_tokens = lax.all_gather(post_low[None], BOTH, axis=0, tiled=True)
+    block_starts = (0, 0)
+    if lattice:
+        tokens_at = links.add(*spread_jobs(post_low, cuts, "zxy", GATHER_ORDERS))
+        links.finish()
+        all_tokens, all_grads = gathered_groups(tokens_at), gathered_groups(grads_at)
+    else:
+        block_starts = (0, device_count // 2)
+        all_tokens, all_grads = (
+            ([lax.all_gather(values[None], BOTH, axis=0, tiled=True)],) * 2
+            for values in (post_low, cotangent)
+        )
 
     logits = dot(post_low, router_full)
     top = jnp.max(jnp.where(chosen_mask, logits, -3e38), axis=-1, keepdims=True)
@@ -751,8 +763,8 @@
 
     def half_grads(half, carry):
         return expert_grads(
-            half, carry, orders[half], first_scalar, all_tokens, all_grads[half],
-            grad_starts[half], positions[half], masks[half],
+            half, carry, first_scalar, all_tokens[half], all_grads[half],
+            block_starts[half], positions[half], masks[half],
             router_t, up_both, up_both_t, down_t, capacity, widths,
         )
 
@@ -775,7 +787,8 @@
         ]
 
     home = links.add(*tokens_home_jobs(lattice, partner, own, received))
-    out_parts = links.round(outputs, gated)
+    out_partner, out_own = links.round(outputs, gated)
+    out_received = [hop(group, "core") for group in out_partner] if lattice else None
     grad_gate_w = links.round(slot_product, rows, grad_gate_pre)
     grad_down = links.round(slot_product, gated, grad_rows)
     links.finish()
@@ -792,26 +805,32 @@
     grad_mid_norm, post_terms = norm_back(grad_post, post_scale, post_hat, post_inv)
     grad_mid = grad_out + grad_mid_norm
     grad_mid_low = grad_mid.astype(BF16)
-    out_home = links.add(*tokens_home_jobs(lattice, *out_parts))
     (other_grads,) = links.add(swap_job(grad_mid_low))
-    grad_up_w = links.round(slot_product, rows, grad_up_pre)
+    out_jobs = tokens_home_jobs(lattice, out_partner, out_own, out_received)
+    out_home = links.add(*out_jobs)
+    grad_up_w = slot_product(*after((rows, grad_up_pre), links.marks))
+    links.marks = [grad_up_w]
+    while other_grads[0] is None:
+        swapped = links.active.pop(0)
+        links.advance(*swapped[:3], after(swapped[3], links.marks))
     grad_attention = in_order(grad_mid_low, other_grads[0])
 
-    out_split = (query_rows // 8 * 3, query_rows - query_rows // 8 * 3)
 
     def back_scores(grad_attention):
         grad_mixed = dot(grad_attention, output_full).astype(BF16)
-        chunks = weight_grads_chunks(lattice, grad_attention, mixed_low, out_split)
         grad_groups = grad_mixed.reshape(seq_len, local_groups, per_group, HEAD_SIZE)
         grad_attend = jnp.einsum(
             "qhgd,khd->hgqk", grad_groups, value_low, preferred_element_type=F32
         )
         row_inner = jnp.sum(attend * grad_attend, axis=-1, keepdims=True)
         grad_scores = (attend * (grad_attend - row_inner)).astype(BF16)
-        return grad_groups, grad_scores, chunks
-
-    grad_groups, grad_scores, chunks = links.round(back_scores, grad_attention)
-    grad_output_at = links.add(*weight_grads_jobs(lattice, *chunks))
+        return grad_groups, grad_scores
+
+    chunks = weight_grads_chunks(lattice, grad_attention, mixed_low, (query_rows,))
+    grad_output_at = slow.add(*weight_grads_jobs(lattice, *chunks, OUTPUT_ORDERS))
+    links.marks = links.marks + slow.marks
+    grad_groups, grad_scores = links.round(back_scores, grad_attention)
+    slow.aside(links)
     grad_router = dot(post_low, grad_logits, 0, 0)
     grad_post_gain = jnp.sum(post_terms, axis=0)
     def back_heads(grad_groups, grad_scores):
@@ -830,37 +849,39 @@
 
     grad_value, grad_key_rot, grad_query_rot = links.round(back_heads, grad_groups, grad_scores)
 
-    def back_norms(grad_value, grad_key_rot, grad_query_rot):
+    def back_norms(grad_query_rot):
         grad_query_norm = grad_query_rot * cosine + rotate_back(grad_query_rot * sine)
         grad_query_raw, query_terms = norm_back(grad_query_norm, query_scale, query_hat, query_inv)
-        grad_query_gain = jnp.sum(query_terms, axis=(0, 1))
-        grad_key_norm = grad_key_rot * cosine + rotate_back(grad_key_rot * sine)
-        grad_key_raw, key_terms = norm_back(grad_key_norm, key_scale, key_hat, key_inv)
-        grad_key_gain = jnp.sum(key_terms, axis=(0, 1))
-        grad_projected = jnp.concatenate(
-            [
-                grad_query_raw.reshape(seq_len, query_rows).astype(BF16),
-                grad_key_raw.reshape(seq_len, key_rows).astype(BF16),
-                grad_value.reshape(seq_len, key_rows).astype(BF16),
-            ],
-            axis=1,
-        )
-        return grad_projected, grad_query_gain, grad_key_gain
-
-    grad_projected, grad_query_gain, grad_key_gain = links.round(
-        back_norms, grad_value, grad_key_rot, grad_query_rot
+        return grad_query_raw.reshape(seq_len, query_rows).astype(BF16), query_terms
+
+    grad_query_low, query_terms = links.round(back_norms, grad_query_rot)
+    grad_query_gain = jnp.sum(query_terms, axis=(0, 1))
+    grad_key_norm = grad_key_rot * cosine + rotate_back(grad_key_rot * sine)
+    grad_key_raw, key_terms = norm_back(grad_key_norm, key_scale, key_hat, key_inv)
+    grad_key_gain = jnp.sum(key_terms, axis=(0, 1))
+    grad_projected = jnp.concatenate(
+        [
+            grad_query_low,
+            grad_key_raw.reshape(seq_len, key_rows).astype(BF16),
+            grad_value.reshape(seq_len, key_rows).astype(BF16),
+        ],
+        axis=1,
     )
     total_rows = query_rows + 2 * key_rows
     split = total_rows // LANES * 2 // 5 * LANES
     chunks = weight_grads_chunks(
         lattice, sequence, grad_projected, (split, total_rows - split)
     )
-    grad_projections_at = links.add(*weight_grads_jobs(lattice, *chunks))
+    grad_projections_at = links.add(
+        *weight_grads_jobs(lattice, *chunks, PROJECTION_ORDERS), rank=-1
+    )
+    slow.aside(links)
     normed_parts = links.round(
-        lambda grad: dot(grad, projections_full), grad_projected
-    )
-    (grad_normed,) = links.add(sum_tokens_job(normed_parts))
+        lambda grad: dot(grad, projections_full, 1, 1), grad_projected
+    )
+    (grad_normed,) = links.add(sum_tokens_job(normed_parts), rank=-1)
     links.round()
+    slow.aside(links)
     grad_in_norm, input_terms = norm_back(grad_normed[0], input_scale, input_hat, input_inv)
     grad_input_gain = jnp.sum(input_terms, axis=0)
     grad_inputs = (grad_mid + grad_in_norm).astype(BF16)
@@ -868,7 +889,9 @@
     flat = jnp.concatenate([part.reshape(device_count, -1) for part in late_parts], axis=1)
     flat = jnp.pad(flat, ((0, 0), (0, -flat.shape[1] % LANES)))
     (late,) = links.add(reduce_small_job(flat.reshape(device_count, -1, LANES)))
-    links.finish()
+    while links.active or slow.active:
+        links.round()
+        slow.aside(links)
     result = (residual_mid + jnp.concatenate([p[0] for p in out_home], axis=1)).astype(BF16)
     grad_output_w = jnp.concatenate([place[0] for place in grad_output_at], axis=1)
     grad_projections = jnp.concatenate([place[0] for place in grad_projections_at], axis=1).T

time: 916 us -> 887 us (0.968)
  local copies, waits for them, and re-layouts: 81.6 us -> 70.3 us
  other arithmetic: 148 us -> 137 us
  waiting for transfers between devices: 330 us -> 319 us
    all_gather x2 -> x1, waiting for transfers between devices: 83.3 us -> 0.01 us  [on_device(): projections_full = lax.all_gather(projections.T, DP, axis=0, tiled=True)]
    ppermute x74 -> x87, waiting for transfers between devices: 178 us -> 248 us  [hop(): return lax.ppermute(values, BOTH, pairs)]
    ppermute x74 -> x87, starting transfers between devices: 97.9 us -> 113 us  [hop(): return lax.ppermute(values, BOTH, pairs)]
    ppermute x14, starting transfers between devices: 25.2 us -> 10.4 us  [flip(): lax.ppermute(values, BOTH, [(source, source ^ bits) for source in range(c...]
    concatenate x4 -> x1, other arithmetic: 12.4 us -> 1.15 us  [on_device(): jnp.concatenate([grad_query_low, grad_key_raw.reshape(seq_len, key_rows)....]
    unnamed x266 -> x305, local copies, waits for them, and re-layouts: 9.75 us -> 20.8 us
    optimization_barrier x3 -> x1, local copies, waits for them, and re-layouts: 14.1 us -> 4.64 us  [after(): return lax.optimization_barrier((values, others))[0]]
    convert_element_type x28 -> x27, other arithmetic: 56.1 us -> 57.6 us  [piece(): return Pending(*picked).total().astype(BF16)]
  transfers between devices with their start and end apart: 95 -> 107, of which waited for: 31 -> 42; matrix products, arithmetic and copies ran while one was open for 32% -> 30% of each run, Pallas kernels for 9% -> 9%
where the time goes in v4:
time: 887 us; the launch traced here: 878 us
  waiting for transfers between devices  319 us (36%)
  other arithmetic  137 us (15%)
  starting transfers between devices  129 us (15%)
  Pallas kernels  125 us (14%)
  matrix products  81.5 us (9%)
  local copies, waits for them, and re-layouts  70.3 us (8%)
  between operations  16.7 us (2%)
    ppermute x87, waiting for transfers between devices, hop(): return lax.ppermute(values, BOTH, pairs)  248 us
    ppermute x87, starting transfers between devices, hop(): return lax.ppermute(values, BOTH, pairs)  113 us
    pallas_call x2, Pallas kernels, expert_grads(): call(first, *tokens, *grads, position, mask, router_t, up_both, up_both_t...  82.1 us
    convert_element_type x27, other arithmetic, piece(): return Pending(*picked).total().astype(BF16)  57.6 us
    dot_general x3, matrix products, slot_product(): return jnp.einsum('esd,esf->edf', left, right, preferred_element_type=F32)  42.8 us
    all_gather x1, waiting for transfers between devices, on_device(): output_full = lax.all_gather(output_held, DP, axis=0, tiled=True)  42.5 us
    dot_general x7, matrix products, dot(): lax.dot_general(left, right, (((left_dim,), (right_dim,)), ((), ())), pre...  27.8 us
    pallas_call x2, Pallas kernels, expert_outputs(): return call(gated, position, down)  21.5 us
  transfers between devices with their start and end apart: 107, of which 42 were waited for; matrix products, arithmetic and copies ran while one was open for 30% of the time, Pallas kernels for 9%

profile of v4, /device:TPU:0, one launch (start us, length us, event | category | flops | bytes accessed | tf_op | source)
XLA Modules:
  0.0 877.7 jit_solution(4628655058793957936)
XLA Ops:
  43.4 12.9 %collective-permute-start.13 = (bf16[1,2,1,128,640]{4,3,2,1,0:T(8,128)(2,1)}, bf16[1,2,1,128,640]{4,3,2,1,0:T(8,128)(2,1)}, u32[]{:S(2)}, u32[]{:S(2)}) collective-permute-start(bf16[1,2,1,128,640]{4,3,2,1,0:T(8,128)(2,1)} %pad_maximum_fusion.15), channel_id=1, source_target_pairs={{0,24},{1,25},{2,26},{3,27},{4,28},{5,29},{6,30},{7,31},{8,0},{9,1... | collective-permute-start | bytes 983048 | tf_op jit(solution)/shard_map/ppermute | solution.py:78
  56.7 8.6 copy.467.refs_10_
  112.7 10.0 %collective-permute-done.16 = bf16[1,2,2,128,640]{4,3,2,1,0:T(8,128)(2,1)} collective-permute-done((bf16[1,2,2,128,640]{4,3,2,1,0:T(8,128)(2,1)}, bf16[1,2,2,128,640]{4,3,2,1,0:T(8,128)(2,1)}, u32[]{:S(2)}, u32[]{:S(2)}) %collective-permute-start.16) | collective-permute-done | bytes 655392 | tf_op jit(solution)/shard_map/ppermute | solution.py:78
  122.6 31.3 %collective-permute-done.17 = bf16[1,2,2,128,640]{4,3,2,1,0:T(8,128)(2,1)} collective-permute-done((bf16[1,2,2,128,640]{4,3,2,1,0:T(8,128)(2,1)}, bf16[1,2,2,128,640]{4,3,2,1,0:T(8,128)(2,1)}, u32[]{:S(2)}, u32[]{:S(2)}) %collective-permute-start.17) | collective-permute-done | bytes 655392 | tf_op jit(solution)/shard_map/ppermute | solution.py:78
  192.4 42.5 %all-gather.5.cloned.1.call-done = bf16[2048,2048]{1,0:T(8,128)(2,1)} async-done(((bf16[128,2048]{1,0:T(8,128)(2,1)}), bf16[2048,2048]{1,0:T(8,128)(2,1)}) %all-gather.5.cloned.1.call-update) | async-done | bytes 8388624 | tf_op jit(solution)/shard_map/all_gather | solution.py:656
  243.3 12.6 %collective-permute-done.23 = bf16[128,2048]{1,0:T(8,128)(2,1)} collective-permute-done((bf16[128,2048]{1,0:T(8,128)(2,1)S(1)}, bf16[128,2048]{1,0:T(8,128)(2,1)}, u32[]{:S(2)}, u32[]{:S(2)}) %collective-permute-start.23) | collective-permute-done | bytes 524320 | tf_op jit(solution)/shard_map/ppermute | solution.py:248
  283.1 8.0 collective-permute-done.31
  308.9 15.6 %collective-permute-done.34 = bf16[1,2,2,128,640]{4,3,2,1,0:T(8,128)(2,1)S(1)} collective-permute-done((bf16[1,2,2,128,640]{4,3,2,1,0:T(8,128)(2,1)S(1)}, bf16[1,2,2,128,640]{4,3,2,1,0:T(8,128)(2,1)S(1)}, u32[]{:S(2)}, u32[]{:S(2)}) %collective-permute-start.34) | collective-permute-done | bytes 655392 | tf_op jit(solution)/shard_map/ppermute | solution.py:78
  324.4 8.6 collective-permute-done.35
  335.5 16.5 %collective-permute-done.38 = bf16[1,2,2,128,640]{4,3,2,1,0:T(8,128)(2,1)S(1)} collective-permute-done((bf16[1,2,2,128,640]{4,3,2,1,0:T(8,128)(2,1)S(1)}, bf16[1,2,2,128,640]{4,3,2,1,0:T(8,128)(2,1)S(1)}, u32[]{:S(2)}, u32[]{:S(2)}) %collective-permute-start.38) | collective-permute-done | bytes 655392 | tf_op jit(solution)/shard_map/ppermute | solution.py:78
  362.7 41.0 %expert_grads.2 = (bf16[2,2048,2048]{2,1,0:T(8,128)(2,1)}, bf16[2,2048,2048]{2,1,0:T(8,128)(2,1)}, bf16[2,2048,384]{2,1,0:T(8,128)(2,1)}, bf16[2,2048,384]{2,1,0...) custom-call(s32[1]{0:T(128)} %bitcast.27.first, ...), custom_call_target="tpu_custom_call" | custom-call | flops 25769803776 | bytes 50331648 | tf_op jit(solution)/shard_map/expert_grads/pallas_call | solution.py:431
  407.2 41.2 %expert_grads.3 = (bf16[2,2048,2048]{2,1,0:T(8,128)(2,1)}, bf16[2,2048,2048]{2,1,0:T(8,128)(2,1)}, bf16[2,2048,384]{2,1,0:T(8,128)(2,1)}, bf16[2,2048,384]{2,1,0...) custom-call(s32[1]{0:T(128)} %bitcast.27.first, ...), custom_call_target="tpu_custom_call", output_to_operand_aliasing={{0}: (13, {}), {1}: (14, {}), {2}: (15, {}), {3}: (16, {}),... | custom-call | flops 25769803776 | bytes 50331648 | tf_op jit(solution)/shard_map/expert_grads/pallas_call | solution.py:431
  462.8 10.8 %expert_outputs.2 = (bf16[16,128,768]{2,1,0:T(8,128)(2,1)}, bf16[16,128,768]{2,1,0:T(8,128)(2,1)}, bf16[16,128,512]{2,1,0:T(8,128)(2,1)}) custom-call(bf16[2,2048,384]{2,1,0:T(8,128)(2,1)} %get-tuple-element.296.gated_ref, f32[16,2,128]{2,1,0:T(2,128)} %gather_fusion.1, bf16[2,384,2048]{2,1,0:T(8,128)(2,1)} %down_ref.3), custom_call_target="tpu_custom_call" | custom-call | flops 4294967296 | bytes 16777216 | tf_op jit(solution)/shard_map/expert_outputs/pallas_call | solution.py:480
  473.7 10.6 %expert_outputs.3 = (bf16[16,128,768]{2,1,0:T(8,128)(2,1)}, bf16[16,128,768]{2,1,0:T(8,128)(2,1)}, bf16[16,128,512]{2,1,0:T(8,128)(2,1)}) custom-call(bf16[2,2048,384]{2,1,0:T(8,128)(2,1)} %get-tuple-element.296.gated_ref, f32[16,2,128]{2,1,0:T(2,128)} %gather_fusion, bf16[2,384,2048]{2,1,0:T(8,128)(2,1)} %down_ref.3), custom_call_target="tpu_custom_call" | custom-call | flops 4294967296 | bytes 16777216 | tf_op jit(solution)/shard_map/expert_outputs/pallas_call | solution.py:480
  500.0 15.2 %fusion.196 = f32[2,2048,384]{2,1,0:T(8,128)} fusion(bf16[2,2048,2048]{2,1,0:T(8,128)(2,1)} %get-tuple-element.311, bf16[2,2048,384]{2,1,0:T(8,128)(2,1)} %get-tuple-element.288), kind=kOutput, calls=%fused_computation.475 | convolution fusion | flops 6442450944 | bytes 26214400 | tf_op jit(solution)/shard_map/esd,esf->edf/dot_general | solution.py:779
  523.5 17.2 %collective-permute-done.55 = bf16[2,2,128,640]{3,2,1,0:T(8,128)(2,1)} collective-permute-done((bf16[2,2,128,640]{3,2,1,0:T(8,128)(2,1)}, bf16[2,2,128,640]{3,2,1,0:T(8,128)(2,1)}, u32[]{:S(2)}, u32[]{:S(2)}) %collective-permute-start.55) | collective-permute-done | bytes 655392 | tf_op jit(solution)/shard_map/ppermute | solution.py:78
  544.0 13.3 %fusion.197 = f32[2,384,2048]{2,1,0:T(8,128)} fusion(bf16[2,2048,384]{2,1,0:T(8,128)(2,1)} %get-tuple-element.296.gated_ref, bf16[2,2048,2048]{2,1,0:T(8,128)(2,1)} %get-tuple-element.297), kind=kOutput, calls=%fused_computation.476 | convolution fusion | flops 6442450944 | bytes 26214400 | tf_op jit(solution)/shard_map/esd,esf->edf/dot_general | solution.py:779
  584.1 14.3 %fusion.198 = f32[2,2048,384]{2,1,0:T(8,128)} fusion(bf16[2,2048,2048]{2,1,0:T(8,128)(2,1)} %get-tuple-element.311, bf16[2,2048,384]{2,1,0:T(8,128)(2,1)S(1)} %copy-done.148), kind=kOutput, calls=%fused_computation.477 | convolution fusion | flops 6442450944 | bytes 26214400 | tf_op jit(solution)/shard_map/esd,esf->edf/dot_general | solution.py:779
  636.2 9.9 %collective-permute-done.49 = bf16[4,2,128,768]{3,2,1,0:T(8,128)(2,1)} collective-permute-done((bf16[4,2,128,768]{3,2,1,0:T(8,128)(2,1)}, bf16[4,2,128,768]{3,2,1,0:T(8,128)(2,1)}, u32[]{:S(2)}, u32[]{:S(2)}) %collective-permute-start.49) | collective-permute-done | bytes 1572896 | tf_op jit(solution)/shard_map/ppermute | solution.py:78
  677.4 11.5 %collective-permute-done.74 = bf16[2,2,128,512]{3,2,1,0:T(8,128)(2,1)S(1)} collective-permute-done((bf16[2,2,128,512]{3,2,1,0:T(8,128)(2,1)S(1)}, bf16[2,2,128,512]{3,2,1,0:T(8,128)(2,1)S(1)}, u32[]{:S(2)}, u32[]{:S(2)}) %collective-permute-start.74) | collective-permute-done | bytes 524320 | tf_op jit(solution)/shard_map/ppermute | solution.py:78
  760.7 11.1 %collective-permute-done.88 = bf16[4,128,1024]{2,1,0:T(8,128)(2,1)S(1)} collective-permute-done((bf16[4,128,1024]{2,1,0:T(8,128)(2,1)S(1)}, bf16[4,128,1024]{2,1,0:T(8,128)(2,1)S(1)}, u32[]{:S(2)}, u32[]{:S(2)}) %collective-permute-start.88) | collective-permute-done | bytes 1048608 | tf_op jit(solution)/shard_map/ppermute | solution.py:78
  791.1 15.3 %collective-permute-done.94 = bf16[128,1024]{1,0:T(8,128)(2,1)} collective-permute-done((bf16[128,1024]{1,0:T(8,128)(2,1)}, bf16[128,1024]{1,0:T(8,128)(2,1)}, u32[]{:S(2)}, u32[]{:S(2)}) %collective-permute-start.94) | collective-permute-done | bytes 262176 | tf_op jit(solution)/shard_map/ppermute | solution.py:78
  811.7 10.9 %collective-permute-done.92 = bf16[2,128,1536]{2,1,0:T(8,128)(2,1)} collective-permute-done((bf16[2,128,1536]{2,1,0:T(8,128)(2,1)}, bf16[2,128,1536]{2,1,0:T(8,128)(2,1)}, u32[]{:S(2)}, u32[]{:S(2)}) %collective-permute-start.92) | collective-permute-done | bytes 786464 | tf_op jit(solution)/shard_map/ppermute | solution.py:78
  823.8 12.8 %collective-permute-done.93 = bf16[2,128,1536]{2,1,0:T(8,128)(2,1)} collective-permute-done((bf16[2,128,1536]{2,1,0:T(8,128)(2,1)}, bf16[2,128,1536]{2,1,0:T(8,128)(2,1)}, u32[]{:S(2)}, u32[]{:S(2)}) %collective-permute-start.93) | collective-permute-done | bytes 786464 | tf_op jit(solution)/shard_map/ppermute | solution.py:78
  (716 shorter events, 459.3 us)
Async XLA Ops:
  7.3 150.8 %all-gather.3.cloned.1.call-start = ((), (), s32[]{:S(2)}) async-start(), calls=%async_computation | async-start | bytes 11141120 | tf_op jit(solution)/shard_map/all_gather | solution.py:643
  9.4 225.5 %all-gather.5.cloned.1.call-start = ((), (), s32[]{:S(2)}) async-start(), calls=%async_computation.1 | async-start | bytes 8912896 | tf_op jit(solution)/shard_map/all_gather | solution.py:656
  27.6 50.9 %collective-permute-start = (bf16[128,2048]{1,0:T(8,128)(2,1)S(1)}, bf16[128,2048]{1,0:T(8,128)(2,1)S(1)}, u32[]{:S(2)}, u32[]{:S(2)}) collective-permute-start(bf16[128,2048]{1,0:T(8,128)(2,1)S(1)} %copy-done.5), channel_id=1, source_target_pairs={{0,1},{1,0},{2,3},{3,2},{4,5},{5,4},{6,7},{7,6},{8,9},{9,8},{10,11... | collective-permute-start | bytes 1572872 | tf_op jit(solution)/shard_map/ppermute | solution.py:248
  78.5 44.1 %collective-permute-start.16 = (bf16[1,2,2,128,640]{4,3,2,1,0:T(8,128)(2,1)}, bf16[1,2,2,128,640]{4,3,2,1,0:T(8,128)(2,1)}, u32[]{:S(2)}, u32[]{:S(2)}) collective-permute-start(bf16[1,2,2,128,640]{4,3,2,1,0:T(8,128)(2,1)} %pad_maximum_fusion.13), channel_id=1, source_target_pairs={{0,8},{1,9},{2,10},{3,11},{4,12},{5,13},{6,14},{7,15},{8,16},{9,17... | collective-permute-start | bytes 1966088 | tf_op jit(solution)/shard_map/ppermute | solution.py:78
  78.5 75.5 %collective-permute-start.17 = (bf16[1,2,2,128,640]{4,3,2,1,0:T(8,128)(2,1)}, bf16[1,2,2,128,640]{4,3,2,1,0:T(8,128)(2,1)}, u32[]{:S(2)}, u32[]{:S(2)}) collective-permute-start(bf16[1,2,2,128,640]{4,3,2,1,0:T(8,128)(2,1)} %pad_maximum_fusion.13), channel_id=1, source_target_pairs={{0,24},{1,25},{2,26},{3,27},{4,28},{5,29},{6,30},{7,31},{8,0},{9,1... | collective-permute-start | bytes 1966088 | tf_op jit(solution)/shard_map/ppermute | solution.py:78
  108.3 64.2 %collective-permute-start.22 = (bf16[4,1,2,128,768]{4,3,2,1,0:T(8,128)(2,1)}, bf16[4,1,2,128,768]{4,3,2,1,0:T(8,128)(2,1)}, u32[]{:S(2)}, u32[]{:S(2)}) collective-permute-start(bf16[4,1,2,128,768]{4,3,2,1,0:T(8,128)(2,1)} %pad_maximum_fusion.6), channel_id=1, source_target_pairs={{0,4},{1,5},{2,6},{3,7},{4,0},{5,1},{6,2},{7,3},{8,12},{9,13},{10,... | collective-permute-start | bytes 4718600 | tf_op jit(solution)/shard_map/ppermute | solution.py:78
  111.3 64.2 %collective-permute-start.21 = (bf16[4,2,1,128,640]{4,3,2,1,0:T(8,128)(2,1)}, bf16[4,2,1,128,640]{4,3,2,1,0:T(8,128)(2,1)}, u32[]{:S(2)}, u32[]{:S(2)}) collective-permute-start(bf16[4,2,1,128,640]{4,3,2,1,0:T(8,128)(2,1)} %pad_maximum_fusion.8), channel_id=1, source_target_pairs={{0,1},{1,0},{2,3},{3,2},{4,5},{5,4},{6,7},{7,6},{8,9},{9,8},{10,11... | collective-permute-start | bytes 3932168 | tf_op jit(solution)/shard_map/ppermute | solution.py:78
  283.1 69.4 %collective-permute-start.42 = (bf16[16,128,768]{2,1,0:T(8,128)(2,1)S(1)}, bf16[16,128,768]{2,1,0:T(8,128)(2,1)S(1)}, u32[]{:S(2)}, u32[]{:S(2)}) collective-permute-start(bf16[16,128,768]{2,1,0:T(8,128)(2,1)S(1)} %bitcast.609), channel_id=1, source_target_pairs={{0,2},{1,3},{2,0},{3,1},{4,6},{5,7},{6,4},{7,5},{8,10},{9,11},{10,... | collective-permute-start | bytes 9437192 | tf_op jit(solution)/shard_map/ppermute | solution.py:78
  403.7 44.7 %collective-permute-start.45 = (bf16[16,128,768]{2,1,0:T(8,128)(2,1)}, bf16[16,128,768]{2,1,0:T(8,128)(2,1)}, u32[]{:S(2)}, u32[]{:S(2)}) collective-permute-start(bf16[16,128,768]{2,1,0:T(8,128)(2,1)} %get-tuple-element.272), channel_id=1, source_target_pairs={{0,2},{1,3},{2,0},{3,1},{4,6},{5,7},{6,4},{7,5},{8,10},{9,11},{10,... | collective-permute-start | bytes 9437192 | tf_op jit(solution)/shard_map/ppermute | solution.py:78
  405.0 50.4 %collective-permute-start.46 = (bf16[16,128,768]{2,1,0:T(8,128)(2,1)}, bf16[16,128,768]{2,1,0:T(8,128)(2,1)}, u32[]{:S(2)}, u32[]{:S(2)}) collective-permute-start(bf16[16,128,768]{2,1,0:T(8,128)(2,1)} %get-tuple-element.274), channel_id=1, source_target_pairs={{0,2},{1,3},{2,0},{3,1},{4,6},{5,7},{6,4},{7,5},{8,10},{9,11},{10,... | collective-permute-start | bytes 9437192 | tf_op jit(solution)/shard_map/ppermute | solution.py:78
  407.0 52.1 %collective-permute-start.47 = (bf16[16,128,640]{2,1,0:T(8,128)(2,1)}, bf16[16,128,640]{2,1,0:T(8,128)(2,1)}, u32[]{:S(2)}, u32[]{:S(2)}) collective-permute-start(bf16[16,128,640]{2,1,0:T(8,128)(2,1)} %get-tuple-element.276), channel_id=1, source_target_pairs={{0,2},{1,3},{2,0},{3,1},{4,6},{5,7},{6,4},{7,5},{8,10},{9,11},{10,... | collective-permute-start | bytes 7864328 | tf_op jit(solution)/shard_map/ppermute | solution.py:78
  486.8 91.5 %collective-permute-start.48 = (bf16[16,128,768]{2,1,0:T(8,128)(2,1)}, bf16[16,128,768]{2,1,0:T(8,128)(2,1)}, u32[]{:S(2)}, u32[]{:S(2)}) collective-permute-start(bf16[16,128,768]{2,1,0:T(8,128)(2,1)} %get-tuple-element.279), channel_id=1, source_target_pairs={{0,2},{1,3},{2,0},{3,1},{4,6},{5,7},{6,4},{7,5},{8,10},{9,11},{10,... | collective-permute-start | bytes 9437192 | tf_op jit(solution)/shard_map/ppermute | solution.py:78
  499.2 41.5 %collective-permute-start.55 = (bf16[2,2,128,640]{3,2,1,0:T(8,128)(2,1)}, bf16[2,2,128,640]{3,2,1,0:T(8,128)(2,1)}, u32[]{:S(2)}, u32[]{:S(2)}) collective-permute-start(bf16[2,2,128,640]{3,2,1,0:T(8,128)(2,1)} %bitcast.49), channel_id=1, source_target_pairs={{0,24},{1,25},{2,26},{3,27},{4,28},{5,29},{6,30},{7,31},{8,0},{9,1... | collective-permute-start | bytes 1966088 | tf_op jit(solution)/shard_map/ppermute | solution.py:78
  519.0 56.8 %collective-permute-start.66 = (bf16[16,128,768]{2,1,0:T(8,128)(2,1)S(1)}, bf16[16,128,768]{2,1,0:T(8,128)(2,1)S(1)}, u32[]{:S(2)}, u32[]{:S(2)}) collective-permute-start(bf16[16,128,768]{2,1,0:T(8,128)(2,1)S(1)} %copy-done.141), channel_id=1, source_target_pairs={{0,2},{1,3},{2,0},{3,1},{4,6},{5,7},{6,4},{7,5},{8,10},{9,11},{10,... | collective-permute-start | bytes 9437192 | tf_op jit(solution)/shard_map/ppermute | solution.py:78
  604.7 53.4 %collective-permute-start.69 = (bf16[4,2,128,2048]{3,2,1,0:T(8,128)(2,1)}, bf16[4,2,128,2048]{3,2,1,0:T(8,128)(2,1)}, u32[]{:S(2)}, u32[]{:S(2)}) collective-permute-start(bf16[4,2,128,2048]{3,2,1,0:T(8,128)(2,1)} %bitcast.601), channel_id=1, source_target_pairs={{0,2},{1,3},{2,0},{3,1},{4,6},{5,7},{6,4},{7,5},{8,10},{9,11},{10,... | collective-permute-start | bytes 12582920 | tf_op jit(solution)/shard_map/ppermute | solution.py:78
  608.3 46.5 %collective-permute-start.70 = (bf16[2,2,128,512]{3,2,1,0:T(8,128)(2,1)}, bf16[2,2,128,512]{3,2,1,0:T(8,128)(2,1)}, u32[]{:S(2)}, u32[]{:S(2)}) collective-permute-start(bf16[2,2,128,512]{3,2,1,0:T(8,128)(2,1)} %bitcast.639), channel_id=1, source_target_pairs={{0,8},{1,9},{2,10},{3,11},{4,12},{5,13},{6,14},{7,15},{8,16},{9,17... | collective-permute-start | bytes 1572872 | tf_op jit(solution)/shard_map/ppermute | solution.py:78
  662.7 75.1 %collective-permute-start.80 = (bf16[4,128,2048]{2,1,0:T(8,128)(2,1)}, bf16[4,128,2048]{2,1,0:T(8,128)(2,1)}, u32[]{:S(2)}, u32[]{:S(2)}) collective-permute-start(bf16[4,128,2048]{2,1,0:T(8,128)(2,1)} %get-tuple-element.501), channel_id=1, source_target_pairs={{0,4},{1,5},{2,6},{3,7},{4,0},{5,1},{6,2},{7,3},{8,12},{9,13},{10,... | collective-permute-start | bytes 6291464 | tf_op jit(solution)/shard_map/ppermute | solution.py:78
  667.9 41.6 %collective-permute-start.72 = (bf16[128,768]{1,0:T(8,128)(2,1)}, bf16[128,768]{1,0:T(8,128)(2,1)}, u32[]{:S(2)}, u32[]{:S(2)}) collective-permute-start(bf16[128,768]{1,0:T(8,128)(2,1)} %get-tuple-element.540), channel_id=1, source_target_pairs={{0,8},{1,9},{2,10},{3,11},{4,12},{5,13},{6,14},{7,15},{8,16},{9,17... | collective-permute-start | bytes 589832 | tf_op jit(solution)/shard_map/ppermute | solution.py:78
  670.3 41.1 %collective-permute-start.82 = (bf16[2,128,768]{2,1,0:T(8,128)(2,1)}, bf16[2,128,768]{2,1,0:T(8,128)(2,1)}, u32[]{:S(2)}, u32[]{:S(2)}) collective-permute-start(bf16[2,128,768]{2,1,0:T(8,128)(2,1)} %fusion.53), channel_id=1, source_target_pairs={{0,24},{1,25},{2,26},{3,27},{4,28},{5,29},{6,30},{7,31},{8,0},{9,1... | collective-permute-start | bytes 1179656 | tf_op jit(solution)/shard_map/ppermute | solution.py:78
  726.7 49.5 %collective-permute-start.76 = (bf16[128,768]{1,0:T(8,128)(2,1)S(1)}, bf16[128,768]{1,0:T(8,128)(2,1)S(1)}, u32[]{:S(2)}, u32[]{:S(2)}) collective-permute-start(bf16[128,768]{1,0:T(8,128)(2,1)S(1)} %copy-done.105), channel_id=1, source_target_pairs={{0,24},{1,25},{2,26},{3,27},{4,28},{5,29},{6,30},{7,31},{8,0},{9,1... | collective-permute-start | bytes 589832 | tf_op jit(solution)/shard_map/ppermute | solution.py:78
  771.8 82.5 %collective-permute-start.103 = (bf16[128,2048]{1,0:T(8,128)(2,1)}, bf16[128,2048]{1,0:T(8,128)(2,1)}, u32[]{:S(2)}, u32[]{:S(2)}) collective-permute-start(bf16[128,2048]{1,0:T(8,128)(2,1)} %get-tuple-element.354), channel_id=1, source_target_pairs={{0,24},{1,25},{2,26},{3,27},{4,28},{5,29},{6,30},{7,31},{8,0},{9,1... | collective-permute-start | bytes 1572872 | tf_op jit(solution)/shard_map/ppermute | solution.py:78
  776.2 78.6 %collective-permute-start.104 = (bf16[128,2048]{1,0:T(8,128)(2,1)}, bf16[128,2048]{1,0:T(8,128)(2,1)}, u32[]{:S(2)}, u32[]{:S(2)}) collective-permute-start(bf16[128,2048]{1,0:T(8,128)(2,1)} %fusion.41), channel_id=1, source_target_pairs={{0,8},{1,9},{2,10},{3,11},{4,12},{5,13},{6,14},{7,15},{8,16},{9,17... | collective-permute-start | bytes 1572872 | tf_op jit(solution)/shard_map/ppermute | solution.py:78
  782.1 40.5 %collective-permute-start.92 = (bf16[2,128,1536]{2,1,0:T(8,128)(2,1)}, bf16[2,128,1536]{2,1,0:T(8,128)(2,1)}, u32[]{:S(2)}, u32[]{:S(2)}) collective-permute-start(bf16[2,128,1536]{2,1,0:T(8,128)(2,1)} %get-tuple-element.348), channel_id=1, source_target_pairs={{0,24},{1,25},{2,26},{3,27},{4,28},{5,29},{6,30},{7,31},{8,0},{9,1... | collective-permute-start | bytes 2359304 | tf_op jit(solution)/shard_map/ppermute | solution.py:78
  785.5 51.2 %collective-permute-start.93 = (bf16[2,128,1536]{2,1,0:T(8,128)(2,1)}, bf16[2,128,1536]{2,1,0:T(8,128)(2,1)}, u32[]{:S(2)}, u32[]{:S(2)}) collective-permute-start(bf16[2,128,1536]{2,1,0:T(8,128)(2,1)} %get-tuple-element.349), channel_id=1, source_target_pairs={{0,8},{1,9},{2,10},{3,11},{4,12},{5,13},{6,14},{7,15},{8,16},{9,17... | collective-permute-start | bytes 2359304 | tf_op jit(solution)/shard_map/ppermute | solution.py:78
  (233 other events, 4510.7 us)
Sparse Core Ops, SparseCore 0:
  10.8 147.1 all-gather.2
  160.2 74.7 all-gather.4

commit v5 on v4

--- a/solution.py
+++ b/solution.py
@@ -539,9 +539,10 @@
 
 
 TOKEN_ORDERS = (("x", "y", "z"), ("y", "z", "x"), ("z", "x", "y"))
+EARLY_ORDERS = (("z", "x", "y"), ("x", "z", "y"))
+LATE_ORDERS = (("y", "x", "z"), ("y", "z", "x"))
 GATHER_ORDERS = (("z", "y", "x"), ("x", "z", "y"), ("y", "x", "z"))
-PROJECTION_ORDERS = (("x", "z"), ("z", "x"))
-OUTPUT_ORDERS = (("x", "z"),)
+CHUNK_ORDERS = (("x", "z"), ("z", "x"))
 TURNS = (1, -1, 1)
 
 
@@ -552,19 +553,16 @@
     yield
 
 
-def tokens_home_jobs(lattice, partner, own, received=None):
+def tokens_home_jobs(lattice, partner, own, received, orders):
     jobs = []
-    for n, order in enumerate(TOKEN_ORDERS):
+    for n, order in enumerate(orders):
         if not lattice:
             jobs.append(scatter_job(partner[n], own[n]))
             continue
         shape = (4, 2, 2) + own[n].shape[1:]
         mine = own[n].reshape(shape)
-        if received is None:
-            jobs.append(home_job(partner[n].reshape(shape), mine, "zxy", order, TURNS[n]))
-        else:
-            both = Pending(mine, received[n].reshape(shape))
-            jobs.append(home_job(None, both, "zxy", order, TURNS[n]))
+        both = Pending(mine, received[n].reshape(shape))
+        jobs.append(home_job(None, both, "zxy", order, TURNS[n]))
     return jobs
 
 
@@ -580,11 +578,11 @@
     return tuple(chunk_products(order, left, right, widths) for order in chunk_orders())
 
 
-def weight_grads_jobs(lattice, first, second, orders):
+def weight_grads_jobs(lattice, first, second):
     if not lattice:
         return [product_job(first, second)]
     jobs = []
-    for n, order in enumerate(orders):
+    for n, order in enumerate(CHUNK_ORDERS):
         shape = (4, 2) + first[n].shape[1:]
         jobs.append(
             home_job(first[n].reshape(shape), second[n].reshape(shape), "zx", order, TURNS[n])
@@ -617,7 +615,7 @@
     experts_here = gate_weight.shape[0]
     capacity = 2 * row_count * routes.shape[1] // experts
 
-    links, slow = Links(), Links()
+    links, slow, outer = Links(), Links(), Links()
     projections = jnp.concatenate(
         [query_weight, key_projection_matrix, value_projection_matrix], axis=0
     )
@@ -643,7 +641,8 @@
     projections_full = lax.all_gather(projections.T, DP, axis=0, tiled=True)
     if lattice:
         cuts = (width // 8 * 3, width // 16 * 11)
-        grads_at = links.add(*spread_jobs(cotangent, cuts, "zxy", GATHER_ORDERS))
+        grads_at = slow.add(*spread_jobs(cotangent, cuts[:1], "zxy", EARLY_ORDERS))
+        links.marks = links.marks + slow.marks
 
     def join_up(gate, up):
         return jnp.concatenate([gate, up], axis=2)
@@ -654,8 +653,11 @@
     up_both = links.round(join_up, gate_weight, up_weight)
     output_held = after(output_weight, up_both[0, :8, :LANES])
     output_full = lax.all_gather(output_held, DP, axis=0, tiled=True)
+    slow.aside(links)
     up_both_t = links.round(turn_last, up_both)
+    slow.aside(links)
     down_t = links.round(turn_last, down_weight)
+    slow.aside(links)
     while gathered_at[0] is None:
         links.round()
     gathered, other_inputs = gathered_at[0], other_inputs_at[0]
@@ -729,6 +731,7 @@
         project, projections_full
     )
     mixed_low, attend, attend_low = links.round(attention, query_groups, key_low, value_low)
+    slow.aside(links)
     links.finish()
     ready = (positions, masks, router_t, up_both, up_both_t, down_t)
     mixed_low, (positions, masks, router_t, up_both, up_both_t, down_t) = (
@@ -743,6 +746,7 @@
     block_starts = (0, 0)
     if lattice:
         tokens_at = links.add(*spread_jobs(post_low, cuts, "zxy", GATHER_ORDERS))
+        slow.aside(links)
         links.finish()
         all_tokens, all_grads = gathered_groups(tokens_at), gathered_groups(grads_at)
     else:
@@ -778,7 +782,7 @@
     def slot_product(left, right):
         return jnp.einsum("esd,esf->edf", left, right, preferred_element_type=F32)
 
-    out_widths = (wide, wide, width - 2 * wide)
+    out_widths = (wide, width - wide)
 
     def outputs(gated):
         return [
@@ -786,7 +790,7 @@
             for n in range(2)
         ]
 
-    home = links.add(*tokens_home_jobs(lattice, partner, own, received))
+    home = links.add(*tokens_home_jobs(lattice, partner, own, received, TOKEN_ORDERS))
     out_partner, out_own = links.round(outputs, gated)
     out_received = [hop(group, "core") for group in out_partner] if lattice else None
     grad_gate_w = links.round(slot_product, rows, grad_gate_pre)
@@ -806,8 +810,9 @@
     grad_mid = grad_out + grad_mid_norm
     grad_mid_low = grad_mid.astype(BF16)
     (other_grads,) = links.add(swap_job(grad_mid_low))
-    out_jobs = tokens_home_jobs(lattice, out_partner, out_own, out_received)
-    out_home = links.add(*out_jobs)
+    out_jobs = tokens_home_jobs(lattice, out_partner, out_own, out_received, LATE_ORDERS)
+    out_home = outer.add(*out_jobs)
+    links.marks = links.marks + outer.marks
     grad_up_w = slot_product(*after((rows, grad_up_pre), links.marks))
     links.marks = [grad_up_w]
     while other_grads[0] is None:
@@ -826,8 +831,11 @@
         grad_scores = (attend * (grad_attend - row_inner)).astype(BF16)
         return grad_groups, grad_scores
 
-    chunks = weight_grads_chunks(lattice, grad_attention, mixed_low, (query_rows,))
-    grad_output_at = slow.add(*weight_grads_jobs(lattice, *chunks, OUTPUT_ORDERS))
+    out_split = query_rows // 8 * 3
+    chunks = weight_grads_chunks(
+        lattice, grad_attention, mixed_low, (out_split, query_rows - out_split)
+    )
+    grad_output_at = slow.add(*weight_grads_jobs(lattice, *chunks))
     links.marks = links.marks + slow.marks
     grad_groups, grad_scores = links.round(back_scores, grad_attention)
     slow.aside(links)
@@ -873,7 +881,7 @@
         lattice, sequence, grad_projected, (split, total_rows - split)
     )
     grad_projections_at = links.add(
-        *weight_grads_jobs(lattice, *chunks, PROJECTION_ORDERS), rank=-1
+        *weight_grads_jobs(lattice, *chunks), rank=-1
     )
     slow.aside(links)
     normed_parts = links.round(
@@ -882,6 +890,7 @@
     (grad_normed,) = links.add(sum_tokens_job(normed_parts), rank=-1)
     links.round()
     slow.aside(links)
+    outer.aside(links)
     grad_in_norm, input_terms = norm_back(grad_normed[0], input_scale, input_hat, input_inv)
     grad_input_gain = jnp.sum(input_terms, axis=0)
     grad_inputs = (grad_mid + grad_in_norm).astype(BF16)
@@ -889,9 +898,10 @@
     flat = jnp.concatenate([part.reshape(device_count, -1) for part in late_parts], axis=1)
     flat = jnp.pad(flat, ((0, 0), (0, -flat.shape[1] % LANES)))
     (late,) = links.add(reduce_small_job(flat.reshape(device_count, -1, LANES)))
-    while links.active or slow.active:
+    while links.active or slow.active or outer.active:
         links.round()
         slow.aside(links)
+        outer.aside(links)
     result = (residual_mid + jnp.concatenate([p[0] for p in out_home], axis=1)).astype(BF16)
     grad_output_w = jnp.concatenate([place[0] for place in grad_output_at], axis=1)
     grad_projections = jnp.concatenate([place[0] for place in grad_projections_at], axis=1).T

time: 887 us -> 876 us (0.988)
  starting transfers between devices: 129 us -> 118 us
  waiting for transfers between devices: 319 us -> 330 us
    all_gather x1, waiting for transfers between devices: 42.5 us -> 12 us  [on_device(): output_full = lax.all_gather(output_held, DP, axis=0, tiled=True)]
    all_gather x1, waiting for transfers between devices: 0.01 us -> 21.9 us  [on_device(): projections_full = lax.all_gather(projections.T, DP, axis=0, tiled=True)]
    ppermute x87 -> x80, waiting for transfers between devices: 248 us -> 265 us  [hop(): return lax.ppermute(values, BOTH, pairs)]
    ppermute x87 -> x80, starting transfers between devices: 113 us -> 98.4 us  [hop(): return lax.ppermute(values, BOTH, pairs)]
    convert_element_type x27 -> x25, other arithmetic: 57.6 us -> 51.7 us  [piece(): return Pending(*picked).total().astype(BF16)]
    unnamed x305 -> x253, local copies, waits for them, and re-layouts: 20.8 us -> 19.1 us
  transfers between devices with their start and end apart: 107 -> 100, of which waited for: 42 -> 39; matrix products, arithmetic and copies ran while one was open for 30% -> 29% of each run, Pallas kernels for 9% -> 9%
where the time goes in v5:
time: 876 us; the launch traced here: 869 us
  waiting for transfers between devices  330 us (38%)
  other arithmetic  132 us (15%)
  Pallas kernels  124 us (14%)
  starting transfers between devices  118 us (13%)
  matrix products  79.6 us (9%)
  local copies, waits for them, and re-layouts  69.7 us (8%)
  between operations  16.4 us (2%)
    ppermute x80, waiting for transfers between devices, hop(): return lax.ppermute(values, BOTH, pairs)  265 us
    ppermute x80, starting transfers between devices, hop(): return lax.ppermute(values, BOTH, pairs)  98.4 us
    pallas_call x2, Pallas kernels, expert_grads(): call(first, *tokens, *grads, position, mask, router_t, up_both, up_both_t...  82.1 us
    convert_element_type x25, other arithmetic, piece(): return Pending(*picked).total().astype(BF16)  51.7 us
    dot_general x3, matrix products, slot_product(): return jnp.einsum('esd,esf->edf', left, right, preferred_element_type=F32)  42.8 us
    dot_general x7, matrix products, dot(): lax.dot_general(left, right, (((left_dim,), (right_dim,)), ((), ())), pre...  28 us
    all_gather x1, waiting for transfers between devices, on_device(): projections_full = lax.all_gather(projections.T, DP, axis=0, tiled=True)  21.9 us
    pallas_call x2, Pallas kernels, expert_outputs(): return call(gated, position, down)  21.5 us
  transfers between devices with their start and end apart: 100, of which 39 were waited for; matrix products, arithmetic and copies ran while one was open for 29% of the time, Pallas kernels for 9%

profile of v5, /device:TPU:0, one launch (start us, length us, event | category | flops | bytes accessed | tf_op | source)
XLA Modules:
  0.0 869.1 jit_solution(6479300945725926362)
XLA Ops:
  60.0 12.8 %collective-permute-done.10 = bf16[1,2,1,128,1280]{4,3,2,1,0:T(8,128)(2,1)S(1)} collective-permute-done((bf16[1,2,1,128,1280]{4,3,2,1,0:T(8,128)(2,1)}, bf16[1,2,1,128,1280]{4,3,2,1,0:T(8,128)(2,1)S(1)}, u32[]{:S(2)}, u32[]{:S(2)}) %collective-permute-start.10) | collective-permute-done | bytes 655392 | tf_op jit(solution)/shard_map/ppermute | solution.py:78
  72.8 16.9 %collective-permute-done.11 = bf16[1,2,1,128,1280]{4,3,2,1,0:T(8,128)(2,1)} collective-permute-done((bf16[1,2,1,128,1280]{4,3,2,1,0:T(8,128)(2,1)}, bf16[1,2,1,128,1280]{4,3,2,1,0:T(8,128)(2,1)}, u32[]{:S(2)}, u32[]{:S(2)}) %collective-permute-start.11) | collective-permute-done | bytes 655392 | tf_op jit(solution)/shard_map/ppermute | solution.py:78
  96.0 9.3 %collective-permute-done.9 = bf16[16,50,128]{2,0,1:T(8,128)(2,1)} collective-permute-done((bf16[16,50,128]{2,0,1:T(8,128)(2,1)}, bf16[16,50,128]{2,0,1:T(8,128)(2,1)}, u32[]{:S(2)}, u32[]{:S(2)}) %collective-permute-start.9) | collective-permute-done | bytes 204832 | tf_op jit(solution)/shard_map/ppermute | solution.py:208
  132.8 21.9 %all-gather.3.cloned.1.call-done = bf16[2048,2560]{0,1:T(8,128)(2,1)} async-done(((bf16[128,2560]{0,1:T(8,128)(2,1)}), bf16[2048,2560]{0,1:T(8,128)(2,1)}) %all-gather.3.cloned.1.call-update) | async-done | bytes 10485776 | tf_op jit(solution)/shard_map/all_gather | solution.py:641
  187.6 24.6 %collective-permute-done.16 = bf16[4,2,1,128,1280]{4,3,2,1,0:T(8,128)(2,1)} collective-permute-done((bf16[4,2,1,128,1280]{4,3,2,1,0:T(8,128)(2,1)}, bf16[4,2,1,128,1280]{4,3,2,1,0:T(8,128)(2,1)}, u32[]{:S(2)}, u32[]{:S(2)}) %collective-permute-start.16) | collective-permute-done | bytes 2621472 | tf_op jit(solution)/shard_map/ppermute | solution.py:78
  217.4 12.0 %all-gather.5.cloned.1.call-done = bf16[2048,2048]{1,0:T(8,128)(2,1)} async-done(((bf16[128,2048]{1,0:T(8,128)(2,1)}), bf16[2048,2048]{1,0:T(8,128)(2,1)}) %all-gather.5.cloned.1.call-update) | async-done | bytes 8388624 | tf_op jit(solution)/shard_map/all_gather | solution.py:655
  237.8 12.6 %collective-permute-done.18 = bf16[128,2048]{1,0:T(8,128)(2,1)} collective-permute-done((bf16[128,2048]{1,0:T(8,128)(2,1)S(1)}, bf16[128,2048]{1,0:T(8,128)(2,1)}, u32[]{:S(2)}, u32[]{:S(2)}) %collective-permute-start.18) | collective-permute-done | bytes 524320 | tf_op jit(solution)/shard_map/ppermute | solution.py:248
  303.4 15.6 %collective-permute-done.29 = bf16[1,2,2,128,640]{4,3,2,1,0:T(8,128)(2,1)S(1)} collective-permute-done((bf16[1,2,2,128,640]{4,3,2,1,0:T(8,128)(2,1)S(1)}, bf16[1,2,2,128,640]{4,3,2,1,0:T(8,128)(2,1)S(1)}, u32[]{:S(2)}, u32[]{:S(2)}) %collective-permute-start.29) | collective-permute-done | bytes 655392 | tf_op jit(solution)/shard_map/ppermute | solution.py:78
  319.0 11.0 %collective-permute-done.30 = bf16[1,2,2,128,640]{4,3,2,1,0:T(8,128)(2,1)S(1)} collective-permute-done((bf16[1,2,2,128,640]{4,3,2,1,0:T(8,128)(2,1)S(1)}, bf16[1,2,2,128,640]{4,3,2,1,0:T(8,128)(2,1)S(1)}, u32[]{:S(2)}, u32[]{:S(2)}) %collective-permute-start.30) | collective-permute-done | bytes 655392 | tf_op jit(solution)/shard_map/ppermute | solution.py:78
  335.8 13.0 %collective-permute-done.33 = bf16[1,2,2,128,640]{4,3,2,1,0:T(8,128)(2,1)S(1)} collective-permute-done((bf16[1,2,2,128,640]{4,3,2,1,0:T(8,128)(2,1)S(1)}, bf16[1,2,2,128,640]{4,3,2,1,0:T(8,128)(2,1)S(1)}, u32[]{:S(2)}, u32[]{:S(2)}) %collective-permute-start.33) | collective-permute-done | bytes 655392 | tf_op jit(solution)/shard_map/ppermute | solution.py:78
  359.5 40.7 %expert_grads.2 = (bf16[2,2048,2048]{2,1,0:T(8,128)(2,1)}, bf16[2,2048,2048]{2,1,0:T(8,128)(2,1)}, bf16[2,2048,384]{2,1,0:T(8,128)(2,1)}, bf16[2,2048,384]{2,1,0...) custom-call(s32[1]{0:T(128)} %bitcast.26.first, ...), custom_call_target="tpu_custom_call" | custom-call | flops 25769803776 | bytes 50331648 | tf_op jit(solution)/shard_map/expert_grads/pallas_call | solution.py:431
  407.5 41.3 %expert_grads.3 = (bf16[2,2048,2048]{2,1,0:T(8,128)(2,1)}, bf16[2,2048,2048]{2,1,0:T(8,128)(2,1)}, bf16[2,2048,384]{2,1,0:T(8,128)(2,1)}, bf16[2,2048,384]{2,1,0...) custom-call(s32[1]{0:T(128)} %bitcast.26.first, ...), custom_call_target="tpu_custom_call", output_to_operand_aliasing={{0}: (12, {}), {1}: (13, {}), {2}: (14, {}), {3}: (15, {}),... | custom-call | flops 25769803776 | bytes 50331648 | tf_op jit(solution)/shard_map/expert_grads/pallas_call | solution.py:431
  462.7 10.7 %expert_outputs.3 = (bf16[16,128,768]{2,1,0:T(8,128)(2,1)}, bf16[16,128,1280]{2,1,0:T(8,128)(2,1)}) custom-call(bf16[2,2048,384]{2,1,0:T(8,128)(2,1)} %get-tuple-element.281.gated_ref, f32[16,2,128]{2,1,0:T(2,128)} %gather_fusion, bf16[2,384,2048]{2,1,0:T(8,128)(2,1)} %down_ref.3), custom_call_target="tpu_custom_call" | custom-call | flops 4294967296 | bytes 16777216 | tf_op jit(solution)/shard_map/expert_outputs/pallas_call | solution.py:480
  473.4 10.8 %expert_outputs.2 = (bf16[16,128,768]{2,1,0:T(8,128)(2,1)}, bf16[16,128,1280]{2,1,0:T(8,128)(2,1)}) custom-call(bf16[2,2048,384]{2,1,0:T(8,128)(2,1)} %get-tuple-element.281.gated_ref, f32[16,2,128]{2,1,0:T(2,128)} %gather_fusion.1, bf16[2,384,2048]{2,1,0:T(8,128)(2,1)} %down_ref.3), custom_call_target="tpu_custom_call" | custom-call | flops 4294967296 | bytes 16777216 | tf_op jit(solution)/shard_map/expert_outputs/pallas_call | solution.py:480
  502.2 15.0 %fusion.192 = f32[2,2048,384]{2,1,0:T(8,128)} fusion(bf16[2,2048,2048]{2,1,0:T(8,128)(2,1)} %get-tuple-element.294, bf16[2,2048,384]{2,1,0:T(8,128)(2,1)} %get-tuple-element.273), kind=kOutput, calls=%fused_computation.462 | convolution fusion | flops 6442450944 | bytes 26214400 | tf_op jit(solution)/shard_map/esd,esf->edf/dot_general | solution.py:783
  518.9 19.8 %collective-permute-done.49 = bf16[2,2,128,640]{3,2,1,0:T(8,128)(2,1)S(1)} collective-permute-done((bf16[2,2,128,640]{3,2,1,0:T(8,128)(2,1)S(1)}, bf16[2,2,128,640]{3,2,1,0:T(8,128)(2,1)S(1)}, u32[]{:S(2)}, u32[]{:S(2)}) %collective-permute-start.49) | collective-permute-done | bytes 655392 | tf_op jit(solution)/shard_map/ppermute | solution.py:78
  541.0 13.1 %fusion.193 = f32[2,384,2048]{2,1,0:T(8,128)} fusion(bf16[2,2048,384]{2,1,0:T(8,128)(2,1)} %get-tuple-element.281.gated_ref, bf16[2,2048,2048]{2,1,0:T(8,128)(2,1)} %get-tuple-element.282), kind=kOutput, calls=%fused_computation.463 | convolution fusion | flops 6442450944 | bytes 26214400 | tf_op jit(solution)/shard_map/esd,esf->edf/dot_general | solution.py:783
  578.8 14.6 %fusion.194 = f32[2,2048,384]{2,1,0:T(8,128)} fusion(bf16[2,2048,2048]{2,1,0:T(8,128)(2,1)} %get-tuple-element.294, bf16[2,2048,384]{2,1,0:T(8,128)(2,1)S(1)} %copy-done.120), kind=kOutput, calls=%fused_computation.464 | convolution fusion | flops 6442450944 | bytes 26214400 | tf_op jit(solution)/shard_map/esd,esf->edf/dot_general | solution.py:783
  683.0 11.3 %collective-permute-done.66 = bf16[2,128,1280]{2,1,0:T(8,128)(2,1)S(1)} collective-permute-done((bf16[2,128,1280]{2,1,0:T(8,128)(2,1)}, bf16[2,128,1280]{2,1,0:T(8,128)(2,1)S(1)}, u32[]{:S(2)}, u32[]{:S(2)}) %collective-permute-start.66) | collective-permute-done | bytes 655392 | tf_op jit(solution)/shard_map/ppermute | solution.py:78
  713.5 9.4 %collective-permute-done.68 = bf16[4,128,768]{2,1,0:T(8,128)(2,1)S(1)} collective-permute-done((bf16[4,128,768]{2,1,0:T(8,128)(2,1)S(1)}, bf16[4,128,768]{2,1,0:T(8,128)(2,1)S(1)}, u32[]{:S(2)}, u32[]{:S(2)}) %collective-permute-start.68) | collective-permute-done | bytes 786464 | tf_op jit(solution)/shard_map/ppermute | solution.py:78
  725.2 18.2 %collective-permute-done.74 = bf16[4,128,1024]{2,1,0:T(8,128)(2,1)S(1)} collective-permute-done((bf16[4,128,1024]{2,1,0:T(8,128)(2,1)S(1)}, bf16[4,128,1024]{2,1,0:T(8,128)(2,1)S(1)}, u32[]{:S(2)}, u32[]{:S(2)}) %collective-permute-start.74) | collective-permute-done | bytes 1048608 | tf_op jit(solution)/shard_map/ppermute | solution.py:78
  761.6 33.4 %collective-permute-done.92 = bf16[128,1024]{1,0:T(8,128)(2,1)S(1)} collective-permute-done((bf16[128,1024]{1,0:T(8,128)(2,1)}, bf16[128,1024]{1,0:T(8,128)(2,1)S(1)}, u32[]{:S(2)}, u32[]{:S(2)}) %collective-permute-start.92) | collective-permute-done | bytes 262176 | tf_op jit(solution)/shard_map/ppermute | solution.py:78
  813.9 10.3 %collective-permute-start.69 = (bf16[128,768]{1,0:T(8,128)(2,1)S(1)}, bf16[128,768]{1,0:T(8,128)(2,1)S(1)}, u32[]{:S(2)}, u32[]{:S(2)}) collective-permute-start(bf16[128,768]{1,0:T(8,128)(2,1)S(1)} %copy-done.81), channel_id=1, source_target_pairs={{0,8},{1,9},{2,10},{3,11},{4,12},{5,13},{6,14},{7,15},{8,16},{9,17... | collective-permute-start | bytes 589832 | tf_op jit(solution)/shard_map/ppermute | solution.py:78
  826.6 12.7 %collective-permute-done.69 = bf16[128,768]{1,0:T(8,128)(2,1)S(1)} collective-permute-done((bf16[128,768]{1,0:T(8,128)(2,1)S(1)}, bf16[128,768]{1,0:T(8,128)(2,1)S(1)}, u32[]{:S(2)}, u32[]{:S(2)}) %collective-permute-start.69) | collective-permute-done | bytes 196640 | tf_op jit(solution)/shard_map/ppermute | solution.py:78
  (647 shorter events, 441.5 us)
Async XLA Ops:
  7.3 147.4 %all-gather.3.cloned.1.call-start = ((), (), s32[]{:S(2)}) async-start(), calls=%async_computation | async-start | bytes 11141120 | tf_op jit(solution)/shard_map/all_gather | solution.py:641
  9.4 220.0 %all-gather.5.cloned.1.call-start = ((), (), s32[]{:S(2)}) async-start(), calls=%async_computation.1 | async-start | bytes 8912896 | tf_op jit(solution)/shard_map/all_gather | solution.py:655
  42.2 47.5 %collective-permute-start.11 = (bf16[1,2,1,128,1280]{4,3,2,1,0:T(8,128)(2,1)}, bf16[1,2,1,128,1280]{4,3,2,1,0:T(8,128)(2,1)}, u32[]{:S(2)}, u32[]{:S(2)}) collective-permute-start(bf16[1,2,1,128,1280]{4,3,2,1,0:T(8,128)(2,1)} %pad_maximum_fusion.13), channel_id=1, source_target_pairs={{0,24},{1,25},{2,26},{3,27},{4,28},{5,29},{6,30},{7,31},{8,0},{9,1... | collective-permute-start | bytes 1966088 | tf_op jit(solution)/shard_map/ppermute | solution.py:78
  54.4 50.9 %collective-permute-start.9 = (bf16[16,50,128]{2,0,1:T(8,128)(2,1)}, bf16[16,50,128]{2,0,1:T(8,128)(2,1)}, u32[]{:S(2)}, u32[]{:S(2)}) collective-permute-start(bf16[16,50,128]{2,0,1:T(8,128)(2,1)} %constant_dynamic-slice_fusion.5), channel_id=1, source_target_pairs={{0,16},{1,17},{2,18},{3,19},{4,20},{5,21},{6,22},{7,23},{8,24},{9,... | collective-permute-start | bytes 614408 | tf_op jit(solution)/shard_map/ppermute | solution.py:208
  56.0 61.1 %collective-permute-start.15 = (bf16[4,1,1,128,768]{4,3,2,1,0:T(8,128)(2,1)}, bf16[4,1,1,128,768]{4,3,2,1,0:T(8,128)(2,1)S(1)}, u32[]{:S(2)}, u32[]{:S(2)}) collective-permute-start(bf16[4,1,1,128,768]{4,3,2,1,0:T(8,128)(2,1)} %pad_maximum_fusion.11), channel_id=1, source_target_pairs={{0,4},{1,5},{2,6},{3,7},{4,0},{5,1},{6,2},{7,3},{8,12},{9,13},{10,... | collective-permute-start | bytes 2359304 | tf_op jit(solution)/shard_map/ppermute | solution.py:78
  89.7 38.8 %collective-permute-start.14 = (bf16[1,2,1,128,1280]{4,3,2,1,0:T(8,128)(2,1)}, bf16[1,2,1,128,1280]{4,3,2,1,0:T(8,128)(2,1)}, u32[]{:S(2)}, u32[]{:S(2)}) collective-permute-start(bf16[1,2,1,128,1280]{4,3,2,1,0:T(8,128)(2,1)} %collective-permute-done.11), channel_id=1, source_target_pairs={{0,24},{1,25},{2,26},{3,27},{4,28},{5,29},{6,30},{7,31},{8,0},{9,1... | collective-permute-start | bytes 1966088 | tf_op jit(solution)/shard_map/ppermute | solution.py:78
  120.3 63.7 %collective-permute-start.17 = (bf16[4,2,1,128,768]{4,3,2,1,0:T(8,128)(2,1)}, bf16[4,2,1,128,768]{4,3,2,1,0:T(8,128)(2,1)}, u32[]{:S(2)}, u32[]{:S(2)}) collective-permute-start(bf16[4,2,1,128,768]{4,3,2,1,0:T(8,128)(2,1)} %pad_maximum_fusion.6), channel_id=1, source_target_pairs={{0,1},{1,0},{2,3},{3,2},{4,5},{5,4},{6,7},{7,6},{8,9},{9,8},{10,11... | collective-permute-start | bytes 4718600 | tf_op jit(solution)/shard_map/ppermute | solution.py:78
  131.3 80.9 %collective-permute-start.16 = (bf16[4,2,1,128,1280]{4,3,2,1,0:T(8,128)(2,1)}, bf16[4,2,1,128,1280]{4,3,2,1,0:T(8,128)(2,1)}, u32[]{:S(2)}, u32[]{:S(2)}) collective-permute-start(bf16[4,2,1,128,1280]{4,3,2,1,0:T(8,128)(2,1)} %pad_maximum_fusion.3), channel_id=1, source_target_pairs={{0,1},{1,0},{2,3},{3,2},{4,5},{5,4},{6,7},{7,6},{8,9},{9,8},{10,11... | collective-permute-start | bytes 7864328 | tf_op jit(solution)/shard_map/ppermute | solution.py:78
  286.4 45.8 %collective-permute-start.28 = (bf16[4,1,2,128,768]{4,3,2,1,0:T(8,128)(2,1)S(1)}, bf16[4,1,2,128,768]{4,3,2,1,0:T(8,128)(2,1)S(1)}, u32[]{:S(2)}, u32[]{:S(2)}) collective-permute-start(bf16[4,1,2,128,768]{4,3,2,1,0:T(8,128)(2,1)S(1)} %pad_maximum_fusion.7), channel_id=1, source_target_pairs={{0,4},{1,5},{2,6},{3,7},{4,0},{5,1},{6,2},{7,3},{8,12},{9,13},{10,... | collective-permute-start | bytes 4718600 | tf_op jit(solution)/shard_map/ppermute | solution.py:78
  287.0 64.7 %collective-permute-start.38 = (bf16[16,128,1280]{2,1,0:T(8,128)(2,1)}, bf16[16,128,1280]{2,1,0:T(8,128)(2,1)}, u32[]{:S(2)}, u32[]{:S(2)}) collective-permute-start(bf16[16,128,1280]{2,1,0:T(8,128)(2,1)} %bitcast.22.refs_4_), channel_id=1, source_target_pairs={{0,2},{1,3},{2,0},{3,1},{4,6},{5,7},{6,4},{7,5},{8,10},{9,11},{10,... | collective-permute-start | bytes 15728648 | tf_op jit(solution)/shard_map/ppermute | solution.py:78
  400.2 48.6 %collective-permute-start.39 = (bf16[16,128,768]{2,1,0:T(8,128)(2,1)}, bf16[16,128,768]{2,1,0:T(8,128)(2,1)}, u32[]{:S(2)}, u32[]{:S(2)}) collective-permute-start(bf16[16,128,768]{2,1,0:T(8,128)(2,1)} %get-tuple-element.257), channel_id=1, source_target_pairs={{0,2},{1,3},{2,0},{3,1},{4,6},{5,7},{6,4},{7,5},{8,10},{9,11},{10,... | collective-permute-start | bytes 9437192 | tf_op jit(solution)/shard_map/ppermute | solution.py:78
  404.1 50.7 %collective-permute-start.40 = (bf16[16,128,768]{2,1,0:T(8,128)(2,1)}, bf16[16,128,768]{2,1,0:T(8,128)(2,1)}, u32[]{:S(2)}, u32[]{:S(2)}) collective-permute-start(bf16[16,128,768]{2,1,0:T(8,128)(2,1)} %get-tuple-element.259), channel_id=1, source_target_pairs={{0,2},{1,3},{2,0},{3,1},{4,6},{5,7},{6,4},{7,5},{8,10},{9,11},{10,... | collective-permute-start | bytes 9437192 | tf_op jit(solution)/shard_map/ppermute | solution.py:78
  407.3 51.8 %collective-permute-start.41 = (bf16[16,128,640]{2,1,0:T(8,128)(2,1)}, bf16[16,128,640]{2,1,0:T(8,128)(2,1)}, u32[]{:S(2)}, u32[]{:S(2)}) collective-permute-start(bf16[16,128,640]{2,1,0:T(8,128)(2,1)} %get-tuple-element.261), channel_id=1, source_target_pairs={{0,2},{1,3},{2,0},{3,1},{4,6},{5,7},{6,4},{7,5},{8,10},{9,11},{10,... | collective-permute-start | bytes 7864328 | tf_op jit(solution)/shard_map/ppermute | solution.py:78
  486.4 84.3 %collective-permute-start.42 = (bf16[16,128,768]{2,1,0:T(8,128)(2,1)}, bf16[16,128,768]{2,1,0:T(8,128)(2,1)S(1)}, u32[]{:S(2)}, u32[]{:S(2)}) collective-permute-start(bf16[16,128,768]{2,1,0:T(8,128)(2,1)} %get-tuple-element.264), channel_id=1, source_target_pairs={{0,2},{1,3},{2,0},{3,1},{4,6},{5,7},{6,4},{7,5},{8,10},{9,11},{10,... | collective-permute-start | bytes 9437192 | tf_op jit(solution)/shard_map/ppermute | solution.py:78
  500.1 38.6 %collective-permute-start.49 = (bf16[2,2,128,640]{3,2,1,0:T(8,128)(2,1)S(1)}, bf16[2,2,128,640]{3,2,1,0:T(8,128)(2,1)S(1)}, u32[]{:S(2)}, u32[]{:S(2)}) collective-permute-start(bf16[2,2,128,640]{3,2,1,0:T(8,128)(2,1)S(1)} %bitcast.611), channel_id=1, source_target_pairs={{0,24},{1,25},{2,26},{3,27},{4,28},{5,29},{6,30},{7,31},{8,0},{9,1... | collective-permute-start | bytes 1966088 | tf_op jit(solution)/shard_map/ppermute | solution.py:78
  500.2 38.5 %collective-permute-start.50 = (bf16[2,2,128,640]{3,2,1,0:T(8,128)(2,1)S(1)}, bf16[2,2,128,640]{3,2,1,0:T(8,128)(2,1)S(1)}, u32[]{:S(2)}, u32[]{:S(2)}) collective-permute-start(bf16[2,2,128,640]{3,2,1,0:T(8,128)(2,1)S(1)} %fusion.37), channel_id=1, source_target_pairs={{0,8},{1,9},{2,10},{3,11},{4,12},{5,13},{6,14},{7,15},{8,16},{9,17... | collective-permute-start | bytes 1966088 | tf_op jit(solution)/shard_map/ppermute | solution.py:78
  517.2 57.4 %collective-permute-start.60 = (bf16[16,128,1280]{2,1,0:T(8,128)(2,1)}, bf16[16,128,1280]{2,1,0:T(8,128)(2,1)S(1)}, u32[]{:S(2)}, u32[]{:S(2)}) collective-permute-start(bf16[16,128,1280]{2,1,0:T(8,128)(2,1)} %get-tuple-element.293), channel_id=1, source_target_pairs={{0,2},{1,3},{2,0},{3,1},{4,6},{5,7},{6,4},{7,5},{8,10},{9,11},{10,... | collective-permute-start | bytes 15728648 | tf_op jit(solution)/shard_map/ppermute | solution.py:78
  604.7 90.7 %collective-permute-start.43 = (bf16[4,2,128,768]{3,2,1,0:T(8,128)(2,1)}, bf16[4,2,128,768]{3,2,1,0:T(8,128)(2,1)}, u32[]{:S(2)}, u32[]{:S(2)}) collective-permute-start(bf16[4,2,128,768]{3,2,1,0:T(8,128)(2,1)} %get-tuple-element.491), channel_id=1, source_target_pairs={{0,1},{1,0},{2,3},{3,2},{4,5},{5,4},{6,7},{7,6},{8,9},{9,8},{10,11... | collective-permute-start | bytes 4718600 | tf_op jit(solution)/shard_map/ppermute | solution.py:78
  605.5 93.6 %collective-permute-start.81 = (bf16[4,2,128,1280]{3,2,1,0:T(8,128)(2,1)}, bf16[4,2,128,1280]{3,2,1,0:T(8,128)(2,1)}, u32[]{:S(2)}, u32[]{:S(2)}) collective-permute-start(bf16[4,2,128,1280]{3,2,1,0:T(8,128)(2,1)} %fusion.5), channel_id=1, source_target_pairs={{0,1},{1,0},{2,3},{3,2},{4,5},{5,4},{6,7},{7,6},{8,9},{9,8},{10,11... | collective-permute-start | bytes 7864328 | tf_op jit(solution)/shard_map/ppermute | solution.py:78
  663.9 42.4 %collective-permute-start.71 = (bf16[4,2,128,1536]{3,2,1,0:T(8,128)(2,1)}, bf16[4,2,128,1536]{3,2,1,0:T(8,128)(2,1)}, u32[]{:S(2)}, u32[]{:S(2)}) collective-permute-start(bf16[4,2,128,1536]{3,2,1,0:T(8,128)(2,1)} %bitcast.102), channel_id=1, source_target_pairs={{0,2},{1,3},{2,0},{3,1},{4,6},{5,7},{6,4},{7,5},{8,10},{9,11},{10,... | collective-permute-start | bytes 9437192 | tf_op jit(solution)/shard_map/ppermute | solution.py:78
  694.3 115.5 %collective-permute-start.95 = (bf16[128,768]{1,0:T(8,128)(2,1)}, bf16[128,768]{1,0:T(8,128)(2,1)}, u32[]{:S(2)}, u32[]{:S(2)}) collective-permute-start(bf16[128,768]{1,0:T(8,128)(2,1)} %get-tuple-element.313), channel_id=1, source_target_pairs={{0,24},{1,25},{2,26},{3,27},{4,28},{5,29},{6,30},{7,31},{8,0},{9,1... | collective-permute-start | bytes 589832 | tf_op jit(solution)/shard_map/ppermute | solution.py:78
  748.6 52.6 %collective-permute-start.78 = (bf16[2,128,1536]{2,1,0:T(8,128)(2,1)}, bf16[2,128,1536]{2,1,0:T(8,128)(2,1)}, u32[]{:S(2)}, u32[]{:S(2)}) collective-permute-start(bf16[2,128,1536]{2,1,0:T(8,128)(2,1)} %add_convert_fusion.10), channel_id=1, source_target_pairs={{0,24},{1,25},{2,26},{3,27},{4,28},{5,29},{6,30},{7,31},{8,0},{9,1... | collective-permute-start | bytes 2359304 | tf_op jit(solution)/shard_map/ppermute | solution.py:78
  750.7 50.7 %collective-permute-start.79 = (bf16[2,128,1536]{2,1,0:T(8,128)(2,1)}, bf16[2,128,1536]{2,1,0:T(8,128)(2,1)}, u32[]{:S(2)}, u32[]{:S(2)}) collective-permute-start(bf16[2,128,1536]{2,1,0:T(8,128)(2,1)} %get-tuple-element.326), channel_id=1, source_target_pairs={{0,8},{1,9},{2,10},{3,11},{4,12},{5,13},{6,14},{7,15},{8,16},{9,17... | collective-permute-start | bytes 2359304 | tf_op jit(solution)/shard_map/ppermute | solution.py:78
  759.6 38.9 %collective-permute-start.93 = (bf16[128,1024]{1,0:T(8,128)(2,1)S(1)}, bf16[128,1024]{1,0:T(8,128)(2,1)S(1)}, u32[]{:S(2)}, u32[]{:S(2)}) collective-permute-start(bf16[128,1024]{1,0:T(8,128)(2,1)S(1)} %fusion.71), channel_id=1, source_target_pairs={{0,8},{1,9},{2,10},{3,11},{4,12},{5,13},{6,14},{7,15},{8,16},{9,17... | collective-permute-start | bytes 786440 | tf_op jit(solution)/shard_map/ppermute | solution.py:78
  (199 other events, 2997.9 us)
Sparse Core Ops, SparseCore 0:
  10.8 143.8 all-gather.2
  156.8 72.5 all-gather.4

commit v6 on v5

--- a/solution.py
+++ b/solution.py
@@ -562,7 +562,8 @@
         shape = (4, 2, 2) + own[n].shape[1:]
         mine = own[n].reshape(shape)
         both = Pending(mine, received[n].reshape(shape))
-        jobs.append(home_job(None, both, "zxy", order, TURNS[n]))
+        turn = 1 if orders is LATE_ORDERS else TURNS[n]
+        jobs.append(home_job(None, both, "zxy", order, turn))
     return jobs
 
 

time: 876 us -> 876 us (level)
  no operation moved by 1% of the time
where the time goes in v6:
time: 876 us; the launch traced here: 869 us
  waiting for transfers between devices  329 us (38%)
  other arithmetic  132 us (15%)
  Pallas kernels  124 us (14%)
  starting transfers between devices  119 us (14%)
  matrix products  79.6 us (9%)
  local copies, waits for them, and re-layouts  69.7 us (8%)
  between operations  16.4 us (2%)
    ppermute x80, waiting for transfers between devices, hop(): return lax.ppermute(values, BOTH, pairs)  264 us
    ppermute x80, starting transfers between devices, hop(): return lax.ppermute(values, BOTH, pairs)  99.7 us
    pallas_call x2, Pallas kernels, expert_grads(): call(first, *tokens, *grads, position, mask, router_t, up_both, up_both_t...  82.1 us
    convert_element_type x25, other arithmetic, piece(): return Pending(*picked).total().astype(BF16)  51.7 us
    dot_general x3, matrix products, slot_product(): return jnp.einsum('esd,esf->edf', left, right, preferred_element_type=F32)  42.8 us
    dot_general x7, matrix products, dot(): lax.dot_general(left, right, (((left_dim,), (right_dim,)), ((), ())), pre...  28 us
    all_gather x1, waiting for transfers between devices, on_device(): projections_full = lax.all_gather(projections.T, DP, axis=0, tiled=True)  21.9 us
    pallas_call x2, Pallas kernels, expert_outputs(): return call(gated, position, down)  21.5 us
  transfers between devices with their start and end apart: 100, of which 39 were waited for; matrix products, arithmetic and copies ran while one was open for 29% of the time, Pallas kernels for 9%

profile of v6, /device:TPU:0, one launch (start us, length us, event | category | flops | bytes accessed | tf_op | source)
XLA Modules:
  0.0 869.0 jit_solution(15305631750715547601)
XLA Ops:
  44.1 8.6 copy.467.refs_9_
  60.0 12.8 %collective-permute-done.10 = bf16[1,2,1,128,1280]{4,3,2,1,0:T(8,128)(2,1)S(1)} collective-permute-done((bf16[1,2,1,128,1280]{4,3,2,1,0:T(8,128)(2,1)}, bf16[1,2,1,128,1280]{4,3,2,1,0:T(8,128)(2,1)S(1)}, u32[]{:S(2)}, u32[]{:S(2)}) %collective-permute-start.10) | collective-permute-done | bytes 655392 | tf_op jit(solution)/shard_map/ppermute | solution.py:78
  72.8 16.9 %collective-permute-done.11 = bf16[1,2,1,128,1280]{4,3,2,1,0:T(8,128)(2,1)} collective-permute-done((bf16[1,2,1,128,1280]{4,3,2,1,0:T(8,128)(2,1)}, bf16[1,2,1,128,1280]{4,3,2,1,0:T(8,128)(2,1)}, u32[]{:S(2)}, u32[]{:S(2)}) %collective-permute-start.11) | collective-permute-done | bytes 655392 | tf_op jit(solution)/shard_map/ppermute | solution.py:78
  96.0 9.3 %collective-permute-done.9 = bf16[16,50,128]{2,0,1:T(8,128)(2,1)} collective-permute-done((bf16[16,50,128]{2,0,1:T(8,128)(2,1)}, bf16[16,50,128]{2,0,1:T(8,128)(2,1)}, u32[]{:S(2)}, u32[]{:S(2)}) %collective-permute-start.9) | collective-permute-done | bytes 204832 | tf_op jit(solution)/shard_map/ppermute | solution.py:208
  132.8 21.9 %all-gather.3.cloned.1.call-done = bf16[2048,2560]{0,1:T(8,128)(2,1)} async-done(((bf16[128,2560]{0,1:T(8,128)(2,1)}), bf16[2048,2560]{0,1:T(8,128)(2,1)}) %all-gather.3.cloned.1.call-update) | async-done | bytes 10485776 | tf_op jit(solution)/shard_map/all_gather | solution.py:642
  187.6 24.6 %collective-permute-done.16 = bf16[4,2,1,128,1280]{4,3,2,1,0:T(8,128)(2,1)} collective-permute-done((bf16[4,2,1,128,1280]{4,3,2,1,0:T(8,128)(2,1)}, bf16[4,2,1,128,1280]{4,3,2,1,0:T(8,128)(2,1)}, u32[]{:S(2)}, u32[]{:S(2)}) %collective-permute-start.16) | collective-permute-done | bytes 2621472 | tf_op jit(solution)/shard_map/ppermute | solution.py:78
  217.4 12.0 %all-gather.5.cloned.1.call-done = bf16[2048,2048]{1,0:T(8,128)(2,1)} async-done(((bf16[128,2048]{1,0:T(8,128)(2,1)}), bf16[2048,2048]{1,0:T(8,128)(2,1)}) %all-gather.5.cloned.1.call-update) | async-done | bytes 8388624 | tf_op jit(solution)/shard_map/all_gather | solution.py:656
  237.8 12.6 %collective-permute-done.18 = bf16[128,2048]{1,0:T(8,128)(2,1)} collective-permute-done((bf16[128,2048]{1,0:T(8,128)(2,1)S(1)}, bf16[128,2048]{1,0:T(8,128)(2,1)}, u32[]{:S(2)}, u32[]{:S(2)}) %collective-permute-start.18) | collective-permute-done | bytes 524320 | tf_op jit(solution)/shard_map/ppermute | solution.py:248
  303.4 15.6 %collective-permute-done.29 = bf16[1,2,2,128,640]{4,3,2,1,0:T(8,128)(2,1)S(1)} collective-permute-done((bf16[1,2,2,128,640]{4,3,2,1,0:T(8,128)(2,1)S(1)}, bf16[1,2,2,128,640]{4,3,2,1,0:T(8,128)(2,1)S(1)}, u32[]{:S(2)}, u32[]{:S(2)}) %collective-permute-start.29) | collective-permute-done | bytes 655392 | tf_op jit(solution)/shard_map/ppermute | solution.py:78
  319.0 11.0 %collective-permute-done.30 = bf16[1,2,2,128,640]{4,3,2,1,0:T(8,128)(2,1)S(1)} collective-permute-done((bf16[1,2,2,128,640]{4,3,2,1,0:T(8,128)(2,1)S(1)}, bf16[1,2,2,128,640]{4,3,2,1,0:T(8,128)(2,1)S(1)}, u32[]{:S(2)}, u32[]{:S(2)}) %collective-permute-start.30) | collective-permute-done | bytes 655392 | tf_op jit(solution)/shard_map/ppermute | solution.py:78
  335.8 13.0 %collective-permute-done.33 = bf16[1,2,2,128,640]{4,3,2,1,0:T(8,128)(2,1)S(1)} collective-permute-done((bf16[1,2,2,128,640]{4,3,2,1,0:T(8,128)(2,1)S(1)}, bf16[1,2,2,128,640]{4,3,2,1,0:T(8,128)(2,1)S(1)}, u32[]{:S(2)}, u32[]{:S(2)}) %collective-permute-start.33) | collective-permute-done | bytes 655392 | tf_op jit(solution)/shard_map/ppermute | solution.py:78
  359.5 40.7 %expert_grads.2 = (bf16[2,2048,2048]{2,1,0:T(8,128)(2,1)}, bf16[2,2048,2048]{2,1,0:T(8,128)(2,1)}, bf16[2,2048,384]{2,1,0:T(8,128)(2,1)}, bf16[2,2048,384]{2,1,0...) custom-call(s32[1]{0:T(128)} %bitcast.26.first, ...), custom_call_target="tpu_custom_call" | custom-call | flops 25769803776 | bytes 50331648 | tf_op jit(solution)/shard_map/expert_grads/pallas_call | solution.py:431
  407.5 41.3 %expert_grads.3 = (bf16[2,2048,2048]{2,1,0:T(8,128)(2,1)}, bf16[2,2048,2048]{2,1,0:T(8,128)(2,1)}, bf16[2,2048,384]{2,1,0:T(8,128)(2,1)}, bf16[2,2048,384]{2,1,0...) custom-call(s32[1]{0:T(128)} %bitcast.26.first, ...), custom_call_target="tpu_custom_call", output_to_operand_aliasing={{0}: (12, {}), {1}: (13, {}), {2}: (14, {}), {3}: (15, {}),... | custom-call | flops 25769803776 | bytes 50331648 | tf_op jit(solution)/shard_map/expert_grads/pallas_call | solution.py:431
  462.7 10.7 %expert_outputs.3 = (bf16[16,128,768]{2,1,0:T(8,128)(2,1)}, bf16[16,128,1280]{2,1,0:T(8,128)(2,1)}) custom-call(bf16[2,2048,384]{2,1,0:T(8,128)(2,1)} %get-tuple-element.281.gated_ref, f32[16,2,128]{2,1,0:T(2,128)} %gather_fusion, bf16[2,384,2048]{2,1,0:T(8,128)(2,1)} %down_ref.3), custom_call_target="tpu_custom_call" | custom-call | flops 4294967296 | bytes 16777216 | tf_op jit(solution)/shard_map/expert_outputs/pallas_call | solution.py:480
  473.4 10.8 %expert_outputs.2 = (bf16[16,128,768]{2,1,0:T(8,128)(2,1)}, bf16[16,128,1280]{2,1,0:T(8,128)(2,1)}) custom-call(bf16[2,2048,384]{2,1,0:T(8,128)(2,1)} %get-tuple-element.281.gated_ref, f32[16,2,128]{2,1,0:T(2,128)} %gather_fusion.1, bf16[2,384,2048]{2,1,0:T(8,128)(2,1)} %down_ref.3), custom_call_target="tpu_custom_call" | custom-call | flops 4294967296 | bytes 16777216 | tf_op jit(solution)/shard_map/expert_outputs/pallas_call | solution.py:480
  502.2 15.0 %fusion.192 = f32[2,2048,384]{2,1,0:T(8,128)} fusion(bf16[2,2048,2048]{2,1,0:T(8,128)(2,1)} %get-tuple-element.294, bf16[2,2048,384]{2,1,0:T(8,128)(2,1)} %get-tuple-element.273), kind=kOutput, calls=%fused_computation.462 | convolution fusion | flops 6442450944 | bytes 26214400 | tf_op jit(solution)/shard_map/esd,esf->edf/dot_general | solution.py:784
  518.9 19.8 %collective-permute-done.49 = bf16[2,2,128,640]{3,2,1,0:T(8,128)(2,1)S(1)} collective-permute-done((bf16[2,2,128,640]{3,2,1,0:T(8,128)(2,1)S(1)}, bf16[2,2,128,640]{3,2,1,0:T(8,128)(2,1)S(1)}, u32[]{:S(2)}, u32[]{:S(2)}) %collective-permute-start.49) | collective-permute-done | bytes 655392 | tf_op jit(solution)/shard_map/ppermute | solution.py:78
  541.0 13.1 %fusion.193 = f32[2,384,2048]{2,1,0:T(8,128)} fusion(bf16[2,2048,384]{2,1,0:T(8,128)(2,1)} %get-tuple-element.281.gated_ref, bf16[2,2048,2048]{2,1,0:T(8,128)(2,1)} %get-tuple-element.282), kind=kOutput, calls=%fused_computation.463 | convolution fusion | flops 6442450944 | bytes 26214400 | tf_op jit(solution)/shard_map/esd,esf->edf/dot_general | solution.py:784
  578.8 14.6 %fusion.194 = f32[2,2048,384]{2,1,0:T(8,128)} fusion(bf16[2,2048,2048]{2,1,0:T(8,128)(2,1)} %get-tuple-element.294, bf16[2,2048,384]{2,1,0:T(8,128)(2,1)S(1)} %copy-done.120), kind=kOutput, calls=%fused_computation.464 | convolution fusion | flops 6442450944 | bytes 26214400 | tf_op jit(solution)/shard_map/esd,esf->edf/dot_general | solution.py:784
  683.0 11.3 %collective-permute-done.66 = bf16[2,128,1280]{2,1,0:T(8,128)(2,1)S(1)} collective-permute-done((bf16[2,128,1280]{2,1,0:T(8,128)(2,1)}, bf16[2,128,1280]{2,1,0:T(8,128)(2,1)S(1)}, u32[]{:S(2)}, u32[]{:S(2)}) %collective-permute-start.66) | collective-permute-done | bytes 655392 | tf_op jit(solution)/shard_map/ppermute | solution.py:78
  725.2 18.2 %collective-permute-done.74 = bf16[4,128,1024]{2,1,0:T(8,128)(2,1)S(1)} collective-permute-done((bf16[4,128,1024]{2,1,0:T(8,128)(2,1)S(1)}, bf16[4,128,1024]{2,1,0:T(8,128)(2,1)S(1)}, u32[]{:S(2)}, u32[]{:S(2)}) %collective-permute-start.74) | collective-permute-done | bytes 1048608 | tf_op jit(solution)/shard_map/ppermute | solution.py:78
  761.6 33.4 %collective-permute-done.92 = bf16[128,1024]{1,0:T(8,128)(2,1)S(1)} collective-permute-done((bf16[128,1024]{1,0:T(8,128)(2,1)}, bf16[128,1024]{1,0:T(8,128)(2,1)S(1)}, u32[]{:S(2)}, u32[]{:S(2)}) %collective-permute-start.92) | collective-permute-done | bytes 262176 | tf_op jit(solution)/shard_map/ppermute | solution.py:78
  813.9 10.3 %collective-permute-start.69 = (bf16[128,768]{1,0:T(8,128)(2,1)S(1)}, bf16[128,768]{1,0:T(8,128)(2,1)S(1)}, u32[]{:S(2)}, u32[]{:S(2)}) collective-permute-start(bf16[128,768]{1,0:T(8,128)(2,1)S(1)} %copy-done.81), channel_id=1, source_target_pairs={{0,8},{1,9},{2,10},{3,11},{4,12},{5,13},{6,14},{7,15},{8,16},{9,17... | collective-permute-start | bytes 589832 | tf_op jit(solution)/shard_map/ppermute | solution.py:78
  826.6 12.6 %collective-permute-done.69 = bf16[128,768]{1,0:T(8,128)(2,1)S(1)} collective-permute-done((bf16[128,768]{1,0:T(8,128)(2,1)S(1)}, bf16[128,768]{1,0:T(8,128)(2,1)S(1)}, u32[]{:S(2)}, u32[]{:S(2)}) %collective-permute-start.69) | collective-permute-done | bytes 196640 | tf_op jit(solution)/shard_map/ppermute | solution.py:78
  (647 shorter events, 442.2 us)
Async XLA Ops:
  7.3 147.4 %all-gather.3.cloned.1.call-start = ((), (), s32[]{:S(2)}) async-start(), calls=%async_computation | async-start | bytes 11141120 | tf_op jit(solution)/shard_map/all_gather | solution.py:642
  9.4 220.0 %all-gather.5.cloned.1.call-start = ((), (), s32[]{:S(2)}) async-start(), calls=%async_computation.1 | async-start | bytes 8912896 | tf_op jit(solution)/shard_map/all_gather | solution.py:656
  42.2 47.5 %collective-permute-start.11 = (bf16[1,2,1,128,1280]{4,3,2,1,0:T(8,128)(2,1)}, bf16[1,2,1,128,1280]{4,3,2,1,0:T(8,128)(2,1)}, u32[]{:S(2)}, u32[]{:S(2)}) collective-permute-start(bf16[1,2,1,128,1280]{4,3,2,1,0:T(8,128)(2,1)} %pad_maximum_fusion.13), channel_id=1, source_target_pairs={{0,24},{1,25},{2,26},{3,27},{4,28},{5,29},{6,30},{7,31},{8,0},{9,1... | collective-permute-start | bytes 1966088 | tf_op jit(solution)/shard_map/ppermute | solution.py:78
  54.4 50.9 %collective-permute-start.9 = (bf16[16,50,128]{2,0,1:T(8,128)(2,1)}, bf16[16,50,128]{2,0,1:T(8,128)(2,1)}, u32[]{:S(2)}, u32[]{:S(2)}) collective-permute-start(bf16[16,50,128]{2,0,1:T(8,128)(2,1)} %constant_dynamic-slice_fusion.5), channel_id=1, source_target_pairs={{0,16},{1,17},{2,18},{3,19},{4,20},{5,21},{6,22},{7,23},{8,24},{9,... | collective-permute-start | bytes 614408 | tf_op jit(solution)/shard_map/ppermute | solution.py:208
  56.0 61.1 %collective-permute-start.15 = (bf16[4,1,1,128,768]{4,3,2,1,0:T(8,128)(2,1)}, bf16[4,1,1,128,768]{4,3,2,1,0:T(8,128)(2,1)S(1)}, u32[]{:S(2)}, u32[]{:S(2)}) collective-permute-start(bf16[4,1,1,128,768]{4,3,2,1,0:T(8,128)(2,1)} %pad_maximum_fusion.11), channel_id=1, source_target_pairs={{0,4},{1,5},{2,6},{3,7},{4,0},{5,1},{6,2},{7,3},{8,12},{9,13},{10,... | collective-permute-start | bytes 2359304 | tf_op jit(solution)/shard_map/ppermute | solution.py:78
  89.7 38.8 %collective-permute-start.14 = (bf16[1,2,1,128,1280]{4,3,2,1,0:T(8,128)(2,1)}, bf16[1,2,1,128,1280]{4,3,2,1,0:T(8,128)(2,1)}, u32[]{:S(2)}, u32[]{:S(2)}) collective-permute-start(bf16[1,2,1,128,1280]{4,3,2,1,0:T(8,128)(2,1)} %collective-permute-done.11), channel_id=1, source_target_pairs={{0,24},{1,25},{2,26},{3,27},{4,28},{5,29},{6,30},{7,31},{8,0},{9,1... | collective-permute-start | bytes 1966088 | tf_op jit(solution)/shard_map/ppermute | solution.py:78
  120.3 63.7 %collective-permute-start.17 = (bf16[4,2,1,128,768]{4,3,2,1,0:T(8,128)(2,1)}, bf16[4,2,1,128,768]{4,3,2,1,0:T(8,128)(2,1)}, u32[]{:S(2)}, u32[]{:S(2)}) collective-permute-start(bf16[4,2,1,128,768]{4,3,2,1,0:T(8,128)(2,1)} %pad_maximum_fusion.6), channel_id=1, source_target_pairs={{0,1},{1,0},{2,3},{3,2},{4,5},{5,4},{6,7},{7,6},{8,9},{9,8},{10,11... | collective-permute-start | bytes 4718600 | tf_op jit(solution)/shard_map/ppermute | solution.py:78
  131.3 80.9 %collective-permute-start.16 = (bf16[4,2,1,128,1280]{4,3,2,1,0:T(8,128)(2,1)}, bf16[4,2,1,128,1280]{4,3,2,1,0:T(8,128)(2,1)}, u32[]{:S(2)}, u32[]{:S(2)}) collective-permute-start(bf16[4,2,1,128,1280]{4,3,2,1,0:T(8,128)(2,1)} %pad_maximum_fusion.3), channel_id=1, source_target_pairs={{0,1},{1,0},{2,3},{3,2},{4,5},{5,4},{6,7},{7,6},{8,9},{9,8},{10,11... | collective-permute-start | bytes 7864328 | tf_op jit(solution)/shard_map/ppermute | solution.py:78
  286.4 45.8 %collective-permute-start.28 = (bf16[4,1,2,128,768]{4,3,2,1,0:T(8,128)(2,1)S(1)}, bf16[4,1,2,128,768]{4,3,2,1,0:T(8,128)(2,1)S(1)}, u32[]{:S(2)}, u32[]{:S(2)}) collective-permute-start(bf16[4,1,2,128,768]{4,3,2,1,0:T(8,128)(2,1)S(1)} %pad_maximum_fusion.7), channel_id=1, source_target_pairs={{0,4},{1,5},{2,6},{3,7},{4,0},{5,1},{6,2},{7,3},{8,12},{9,13},{10,... | collective-permute-start | bytes 4718600 | tf_op jit(solution)/shard_map/ppermute | solution.py:78
  287.0 64.7 %collective-permute-start.38 = (bf16[16,128,1280]{2,1,0:T(8,128)(2,1)}, bf16[16,128,1280]{2,1,0:T(8,128)(2,1)}, u32[]{:S(2)}, u32[]{:S(2)}) collective-permute-start(bf16[16,128,1280]{2,1,0:T(8,128)(2,1)} %bitcast.22.refs_4_), channel_id=1, source_target_pairs={{0,2},{1,3},{2,0},{3,1},{4,6},{5,7},{6,4},{7,5},{8,10},{9,11},{10,... | collective-permute-start | bytes 15728648 | tf_op jit(solution)/shard_map/ppermute | solution.py:78
  400.2 48.6 %collective-permute-start.39 = (bf16[16,128,768]{2,1,0:T(8,128)(2,1)}, bf16[16,128,768]{2,1,0:T(8,128)(2,1)}, u32[]{:S(2)}, u32[]{:S(2)}) collective-permute-start(bf16[16,128,768]{2,1,0:T(8,128)(2,1)} %get-tuple-element.257), channel_id=1, source_target_pairs={{0,2},{1,3},{2,0},{3,1},{4,6},{5,7},{6,4},{7,5},{8,10},{9,11},{10,... | collective-permute-start | bytes 9437192 | tf_op jit(solution)/shard_map/ppermute | solution.py:78
  404.1 50.7 %collective-permute-start.40 = (bf16[16,128,768]{2,1,0:T(8,128)(2,1)}, bf16[16,128,768]{2,1,0:T(8,128)(2,1)}, u32[]{:S(2)}, u32[]{:S(2)}) collective-permute-start(bf16[16,128,768]{2,1,0:T(8,128)(2,1)} %get-tuple-element.259), channel_id=1, source_target_pairs={{0,2},{1,3},{2,0},{3,1},{4,6},{5,7},{6,4},{7,5},{8,10},{9,11},{10,... | collective-permute-start | bytes 9437192 | tf_op jit(solution)/shard_map/ppermute | solution.py:78
  407.3 51.8 %collective-permute-start.41 = (bf16[16,128,640]{2,1,0:T(8,128)(2,1)}, bf16[16,128,640]{2,1,0:T(8,128)(2,1)}, u32[]{:S(2)}, u32[]{:S(2)}) collective-permute-start(bf16[16,128,640]{2,1,0:T(8,128)(2,1)} %get-tuple-element.261), channel_id=1, source_target_pairs={{0,2},{1,3},{2,0},{3,1},{4,6},{5,7},{6,4},{7,5},{8,10},{9,11},{10,... | collective-permute-start | bytes 7864328 | tf_op jit(solution)/shard_map/ppermute | solution.py:78
  486.4 84.3 %collective-permute-start.42 = (bf16[16,128,768]{2,1,0:T(8,128)(2,1)}, bf16[16,128,768]{2,1,0:T(8,128)(2,1)S(1)}, u32[]{:S(2)}, u32[]{:S(2)}) collective-permute-start(bf16[16,128,768]{2,1,0:T(8,128)(2,1)} %get-tuple-element.264), channel_id=1, source_target_pairs={{0,2},{1,3},{2,0},{3,1},{4,6},{5,7},{6,4},{7,5},{8,10},{9,11},{10,... | collective-permute-start | bytes 9437192 | tf_op jit(solution)/shard_map/ppermute | solution.py:78
  500.1 38.6 %collective-permute-start.49 = (bf16[2,2,128,640]{3,2,1,0:T(8,128)(2,1)S(1)}, bf16[2,2,128,640]{3,2,1,0:T(8,128)(2,1)S(1)}, u32[]{:S(2)}, u32[]{:S(2)}) collective-permute-start(bf16[2,2,128,640]{3,2,1,0:T(8,128)(2,1)S(1)} %bitcast.611), channel_id=1, source_target_pairs={{0,24},{1,25},{2,26},{3,27},{4,28},{5,29},{6,30},{7,31},{8,0},{9,1... | collective-permute-start | bytes 1966088 | tf_op jit(solution)/shard_map/ppermute | solution.py:78
  500.2 38.5 %collective-permute-start.50 = (bf16[2,2,128,640]{3,2,1,0:T(8,128)(2,1)S(1)}, bf16[2,2,128,640]{3,2,1,0:T(8,128)(2,1)S(1)}, u32[]{:S(2)}, u32[]{:S(2)}) collective-permute-start(bf16[2,2,128,640]{3,2,1,0:T(8,128)(2,1)S(1)} %fusion.37), channel_id=1, source_target_pairs={{0,8},{1,9},{2,10},{3,11},{4,12},{5,13},{6,14},{7,15},{8,16},{9,17... | collective-permute-start | bytes 1966088 | tf_op jit(solution)/shard_map/ppermute | solution.py:78
  517.2 57.4 %collective-permute-start.60 = (bf16[16,128,1280]{2,1,0:T(8,128)(2,1)}, bf16[16,128,1280]{2,1,0:T(8,128)(2,1)S(1)}, u32[]{:S(2)}, u32[]{:S(2)}) collective-permute-start(bf16[16,128,1280]{2,1,0:T(8,128)(2,1)} %get-tuple-element.293), channel_id=1, source_target_pairs={{0,2},{1,3},{2,0},{3,1},{4,6},{5,7},{6,4},{7,5},{8,10},{9,11},{10,... | collective-permute-start | bytes 15728648 | tf_op jit(solution)/shard_map/ppermute | solution.py:78
  604.7 90.7 %collective-permute-start.43 = (bf16[4,2,128,768]{3,2,1,0:T(8,128)(2,1)}, bf16[4,2,128,768]{3,2,1,0:T(8,128)(2,1)}, u32[]{:S(2)}, u32[]{:S(2)}) collective-permute-start(bf16[4,2,128,768]{3,2,1,0:T(8,128)(2,1)} %get-tuple-element.491), channel_id=1, source_target_pairs={{0,1},{1,0},{2,3},{3,2},{4,5},{5,4},{6,7},{7,6},{8,9},{9,8},{10,11... | collective-permute-start | bytes 4718600 | tf_op jit(solution)/shard_map/ppermute | solution.py:78
  605.5 93.6 %collective-permute-start.81 = (bf16[4,2,128,1280]{3,2,1,0:T(8,128)(2,1)}, bf16[4,2,128,1280]{3,2,1,0:T(8,128)(2,1)}, u32[]{:S(2)}, u32[]{:S(2)}) collective-permute-start(bf16[4,2,128,1280]{3,2,1,0:T(8,128)(2,1)} %fusion.5), channel_id=1, source_target_pairs={{0,1},{1,0},{2,3},{3,2},{4,5},{5,4},{6,7},{7,6},{8,9},{9,8},{10,11... | collective-permute-start | bytes 7864328 | tf_op jit(solution)/shard_map/ppermute | solution.py:78
  663.9 42.3 %collective-permute-start.71 = (bf16[4,2,128,1536]{3,2,1,0:T(8,128)(2,1)}, bf16[4,2,128,1536]{3,2,1,0:T(8,128)(2,1)}, u32[]{:S(2)}, u32[]{:S(2)}) collective-permute-start(bf16[4,2,128,1536]{3,2,1,0:T(8,128)(2,1)} %bitcast.102), channel_id=1, source_target_pairs={{0,2},{1,3},{2,0},{3,1},{4,6},{5,7},{6,4},{7,5},{8,10},{9,11},{10,... | collective-permute-start | bytes 9437192 | tf_op jit(solution)/shard_map/ppermute | solution.py:78
  694.3 115.5 %collective-permute-start.95 = (bf16[128,768]{1,0:T(8,128)(2,1)}, bf16[128,768]{1,0:T(8,128)(2,1)}, u32[]{:S(2)}, u32[]{:S(2)}) collective-permute-start(bf16[128,768]{1,0:T(8,128)(2,1)} %get-tuple-element.313), channel_id=1, source_target_pairs={{0,24},{1,25},{2,26},{3,27},{4,28},{5,29},{6,30},{7,31},{8,0},{9,1... | collective-permute-start | bytes 589832 | tf_op jit(solution)/shard_map/ppermute | solution.py:78
  748.6 52.6 %collective-permute-start.78 = (bf16[2,128,1536]{2,1,0:T(8,128)(2,1)}, bf16[2,128,1536]{2,1,0:T(8,128)(2,1)}, u32[]{:S(2)}, u32[]{:S(2)}) collective-permute-start(bf16[2,128,1536]{2,1,0:T(8,128)(2,1)} %add_convert_fusion.10), channel_id=1, source_target_pairs={{0,24},{1,25},{2,26},{3,27},{4,28},{5,29},{6,30},{7,31},{8,0},{9,1... | collective-permute-start | bytes 2359304 | tf_op jit(solution)/shard_map/ppermute | solution.py:78
  750.7 50.7 %collective-permute-start.79 = (bf16[2,128,1536]{2,1,0:T(8,128)(2,1)}, bf16[2,128,1536]{2,1,0:T(8,128)(2,1)}, u32[]{:S(2)}, u32[]{:S(2)}) collective-permute-start(bf16[2,128,1536]{2,1,0:T(8,128)(2,1)} %get-tuple-element.326), channel_id=1, source_target_pairs={{0,8},{1,9},{2,10},{3,11},{4,12},{5,13},{6,14},{7,15},{8,16},{9,17... | collective-permute-start | bytes 2359304 | tf_op jit(solution)/shard_map/ppermute | solution.py:78
  759.6 38.9 %collective-permute-start.93 = (bf16[128,1024]{1,0:T(8,128)(2,1)S(1)}, bf16[128,1024]{1,0:T(8,128)(2,1)S(1)}, u32[]{:S(2)}, u32[]{:S(2)}) collective-permute-start(bf16[128,1024]{1,0:T(8,128)(2,1)S(1)} %fusion.71), channel_id=1, source_target_pairs={{0,8},{1,9},{2,10},{3,11},{4,12},{5,13},{6,14},{7,15},{8,16},{9,17... | collective-permute-start | bytes 786440 | tf_op jit(solution)/shard_map/ppermute | solution.py:78
  (199 other events, 2996.6 us)
Sparse Core Ops, SparseCore 0:
  10.8 143.8 all-gather.2
  156.8 72.5 all-gather.4
